TPU v7x, 32 devices: a whole 2x2x4 slice. The times are simulated.
32 devices in a mesh: gx: 4 (over y, x), gy: 2 (over core), gz: 4 (over z).
Axes of the slice: x: 2, y: 2, z: 4, core: 2. Of those that a mesh axis runs over, the one named last changes fastest.
Arguments:
- phi_start: float32 [64, 96, 512], P('gx', 'gy', 'gz'), may hold values from -30 to 30
Outputs:
- phi_final: float32 [64, 96, 512], P('gx', 'gy', 'gz')
- residuals: float32 [3], replicated
All inputs are finite; a program needn't handle non-finite values.
Results may differ from a plain program's by a relative error of at most 0.0003.
Values sent between devices are 32-bit elements; how exact they have to be, the bound alone decides.
No kernel may reach another device: no remote copies, remote signals or barrier semaphores. Data moves between devices by JAX's collectives and lax.ppermute only.
A program may use at most 64 MiB of HBM per device.

v0:
```python
import jax
import jax.numpy as jnp
from jax import lax
from jax.sharding import PartitionSpec as P

ITERS = 3


pseudo_step = 0.45


def extended_2(cells, sides, width):
    for axis, dim in sides:
        count = lax.axis_size(axis)
        ends = count - 1
        head = lax.slice_in_dim(cells, 0, width, axis=dim)
        tail = lax.slice_in_dim(cells, cells.shape[dim] - width, cells.shape[dim], axis=dim)
        cells = jnp.concatenate(
            [
                lax.ppermute(tail, axis, [(i, (i + 1) % count) for i in range(ends)]),
                cells,
                lax.ppermute(head, axis, [((i + 1) % count, i) for i in range(ends)]),
            ],
            axis=dim,
        )
    return cells


def smooth_sign(field):
    return field / jnp.sqrt(field * field + 1.0)


def upwind_term(back, fwd, positive):
    plus = jnp.maximum(jnp.maximum(back, 0.0) ** 2, jnp.minimum(fwd, 0.0) ** 2)
    minus = jnp.maximum(jnp.minimum(back, 0.0) ** 2, jnp.maximum(fwd, 0.0) ** 2)
    return jnp.where(positive, plus, minus)


def update(ext, sgn):
    center = ext[1:-1, 1:-1, 1:-1]
    positive = sgn > 0.0
    total = upwind_term(center - ext[:-2, 1:-1, 1:-1], ext[2:, 1:-1, 1:-1] - center, positive)
    total = total + upwind_term(
        center - ext[1:-1, :-2, 1:-1], ext[1:-1, 2:, 1:-1] - center, positive
    )
    total = total + upwind_term(
        center - ext[1:-1, 1:-1, :-2], ext[1:-1, 1:-1, 2:] - center, positive
    )
    return center - pseudo_step * sgn * (jnp.sqrt(total) - 1.0)


def clamp_axis(field, margin, dim, count, place):
    length = field.shape[dim]
    position = lax.broadcasted_iota(jnp.int32, field.shape, dim)
    low_value = lax.slice_in_dim(field, margin, margin + 1, axis=dim)
    high_value = lax.slice_in_dim(field, length - margin - 1, length - margin, axis=dim)
    field = jnp.where((place == 0) & (position < margin), low_value, field)
    return jnp.where((place == count - 1) & (position >= length - margin), high_value, field)


def clamp_edges(field, margin):
    field = clamp_axis(field, margin, 0, lax.axis_size("gx"), lax.axis_index("gx"))
    field = clamp_axis(field, margin, 1, lax.axis_size("gy"), lax.axis_index("gy"))
    return clamp_axis(field, margin, 2, lax.axis_size("gz"), lax.axis_index("gz"))


def crop(field, margin):
    if margin == 0:
        return field
    return field[margin:-margin, margin:-margin, margin:-margin]


def reduce_now(partial_value):
    return lax.psum(partial_value, ("gx", "gy", "gz"))


def local(phi_start):
    partials = []
    extended = extended_2(phi_start, (("gx", 0), ("gy", 1), ("gz", 2)), ITERS)
    extended = clamp_edges(extended, ITERS)
    sign_wide = smooth_sign(extended)
    current = extended
    for step in range(ITERS):
        margin = ITERS - step
        newer = update(current, crop(sign_wide, step + 1))
        difference = crop(newer, margin - 1) - crop(current, margin)
        partials.append(reduce_now(jnp.sum(difference * difference)))
        if margin - 1 > 0:
            newer = clamp_edges(newer, margin - 1)
        current = newer
    stacked = jnp.stack(partials)
    cells = phi_start.shape[0] * phi_start.shape[1] * phi_start.shape[2]
    cells = cells * lax.axis_size("gx") * lax.axis_size("gy") * lax.axis_size("gz")
    residuals = jnp.sqrt(stacked / jnp.float32(cells)) / pseudo_step
    return (current, residuals)


def solution(mesh):
    return jax.shard_map(
        local,
        mesh=mesh,
        in_specs=(P("gx", "gy", "gz"),),
        out_specs=(P("gx", "gy", "gz"), P()),
        check_vma=False,
    )
```

profile of v0, /device:TPU:0, one launch (start us, length us, event | category | flops | bytes accessed | tf_op | source)
XLA Modules:
  0.0 102.0 jit_solution(16079190205514697008)
XLA Ops:
  0.6 1.1 %copy.19 = f32[16,48,128]{2,0,1:T(8,128)S(1)} copy(f32[16,48,128]{2,1,0:T(8,128)} %param.1) | data formatting | bytes 786432 | tf_op args[0]
  1.8 4.9 %collective-permute-start = (f32[3,48,128]{2,0,1:T(4,128)S(1)}, f32[3,48,128]{2,0,1:T(4,128)S(1)}, u32[]{:S(2)}, u32[]{:S(2)}) collective-permute-start(f32[3,48,128]{2,0,1:T(4,128)S(1)} %get-tuple-element.35), channel_id=1, source_target_pairs={{0,8},{8,16},{16,24},{1,9},{9,17},{17,25},{2,10},{10,18},{18,26},{... | collective-permute-start | bytes 221192 | tf_op jit(solution)/shard_map/ppermute | solution.py:20
  6.7 1.3 %collective-permute-start.1 = (f32[3,48,128]{2,0,1:T(4,128)S(1)}, f32[3,48,128]{2,0,1:T(4,128)S(1)}, u32[]{:S(2)}, u32[]{:S(2)}) collective-permute-start(f32[3,48,128]{2,0,1:T(4,128)S(1)} %get-tuple-element.36), channel_id=1, source_target_pairs={{8,0},{16,8},{24,16},{9,1},{17,9},{25,17},{10,2},{18,10},{26,18},{... | collective-permute-start | bytes 221192 | tf_op jit(solution)/shard_map/ppermute | solution.py:22
  8.1 0.6 compare_and_fusion.4
  9.7 0.6 compare_and_fusion.2
  10.3 2.9 %collective-permute-done.1 = f32[3,48,128]{2,0,1:T(4,128)S(1)} collective-permute-done((f32[3,48,128]{2,0,1:T(4,128)S(1)}, f32[3,48,128]{2,0,1:T(4,128)S(1)}, u32[]{:S(2)}, u32[]{:S(2)}) %collective-permute-start.1) | collective-permute-done | bytes 73760 | tf_op jit(solution)/shard_map/ppermute | solution.py:22
  13.2 1.3 %collective-permute-start.2 = (f32[22,3,128]{2,0,1:T(8,128)S(1)}, f32[22,3,128]{2,0,1:T(8,128)S(1)}, u32[]{:S(2)}, u32[]{:S(2)}) collective-permute-start(f32[22,3,128]{2,0,1:T(8,128)S(1)} %get-tuple-element.33), channel_id=1, source_target_pairs={{0,4},{1,5},{2,6},{3,7},{8,12},{9,13},{10,14},{11,15},{16,20},{17,... | collective-permute-start | bytes 101384 | tf_op jit(solution)/shard_map/ppermute | solution.py:20
  14.5 1.3 %collective-permute-start.3 = (f32[22,3,128]{2,0,1:T(8,128)S(1)}, f32[22,3,128]{2,0,1:T(8,128)S(1)}, u32[]{:S(2)}, u32[]{:S(2)}) collective-permute-start(f32[22,3,128]{2,0,1:T(8,128)S(1)} %get-tuple-element.34), channel_id=1, source_target_pairs={{4,0},{5,1},{6,2},{7,3},{12,8},{13,9},{14,10},{15,11},{20,16},{21,... | collective-permute-start | bytes 101384 | tf_op jit(solution)/shard_map/ppermute | solution.py:22
  16.4 1.2 %collective-permute-done.3 = f32[22,3,128]{2,0,1:T(8,128)S(1)} collective-permute-done((f32[22,3,128]{2,0,1:T(8,128)S(1)}, f32[22,3,128]{2,0,1:T(8,128)S(1)}, u32[]{:S(2)}, u32[]{:S(2)}) %collective-permute-start.3) | collective-permute-done | bytes 33824 | tf_op jit(solution)/shard_map/ppermute | solution.py:22
  18.3 3.5 %collective-permute-start.4 = (f32[22,54,3]{1,0,2:T(8,128)S(1)}, f32[22,54,3]{1,0,2:T(8,128)S(1)}, u32[]{:S(2)}, u32[]{:S(2)}) collective-permute-start(f32[22,54,3]{1,0,2:T(8,128)S(1)} %copy.22), channel_id=1, source_target_pairs={{0,1},{1,2},{2,3},{4,5},{5,6},{6,7},{8,9},{9,10},{10,11},{12,13},{... | collective-permute-start | bytes 42776 | tf_op jit(solution)/shard_map/ppermute | solution.py:20
  22.1 1.3 %collective-permute-start.5 = (f32[22,54,3]{1,0,2:T(8,128)S(1)}, f32[22,54,3]{1,0,2:T(8,128)S(1)}, u32[]{:S(2)}, u32[]{:S(2)}) collective-permute-start(f32[22,54,3]{1,0,2:T(8,128)S(1)} %copy.23), channel_id=1, source_target_pairs={{1,0},{2,1},{3,2},{5,4},{6,5},{7,6},{9,8},{10,9},{11,10},{13,12},{... | collective-permute-start | bytes 42776 | tf_op jit(solution)/shard_map/ppermute | solution.py:22
  24.3 3.7 %collective-permute-done.5 = f32[22,54,3]{1,0,2:T(8,128)S(1)} collective-permute-done((f32[22,54,3]{1,0,2:T(8,128)S(1)}, f32[22,54,3]{1,0,2:T(8,128)S(1)}, u32[]{:S(2)}, u32[]{:S(2)}) %collective-permute-start.5) | collective-permute-done | bytes 14288 | tf_op jit(solution)/shard_map/ppermute | solution.py:22
  28.3 0.8 pad_maximum_fusion
  29.2 0.8 select_select_fusion.2
  30.1 1.0 %select_select_fusion.1 = f32[22,54,134]{2,0,1:T(8,128)S(1)} fusion(f32[22,134]{1,0:T(8,128)S(1)} %get-tuple-element.16, f32[22,134]{1,0:T(8,128)S(1)} %get-tuple-element.15, pred[54]{0:T(512)(128)(4,1)S(1)} %get-tuple-element.41, pred[54]{0:T(512)(128)(4,1)S(1)} %get-tuple-element.42, f32[54,134]{1,0:T(8,128)S(1)} %get-tuple-element.37, ...), kind=kLoop, calls=%fused_computation.3 | loop fusion | flops 1591920 | bytes 1355160 | tf_op jit(solution)/shard_map/jit(_where)/select_n | solution.py:58
  32.4 3.3 %rsqrt_multiply_fusion = (f32[22,54,134]{2,0,1:T(8,128)S(1)}, f32[22,54,134]{2,0,1:T(8,128)S(1)}) fusion(f32[22,54]{0,1:T(8,128)S(1)} %bitcast.56, pred[134]{0:T(512)(128)(4,1)} %get-tuple-element.43, f32[22,54]{0,1:T(8,128)S(1)} %bitcast.55, pred[134]{0:T(512)(128)(4,1)} %get-tuple-element.44, f32[22,134]{1,0:T(8,128)S(1)} %get-tuple-element.16, ...), kind=kLoop, calls=%fused_computation.1 | loop fusion | flops 2387880 | bytes 2001700 | tf_op jit(solution)/shard_map/div | solution.py:30
  35.7 3.2 %multiply_subtract_fusion = f32[20,52,132]{2,0,1:T(8,128)S(1)} fusion(f32[22,54,134]{2,0,1:T(8,128)S(1)} %get-tuple-element.12, f32[22,54,134]{2,0,1:T(8,128)S(1)} %get-tuple-element.11), kind=kLoop, calls=%fused_computation.14 | loop fusion | flops 6314880 | bytes 4942080 | tf_op jit(solution)/shard_map/sub | solution.py:49
  38.9 1.0 %fusion.3 = f32[]{:T(128)} fusion(f32[22,54,134]{2,0,1:T(8,128)S(1)} %get-tuple-element.12, f32[20,52,132]{2,0,1:T(8,128)S(1)} %multiply_subtract_fusion), kind=kLoop, calls=%fused_computation.31 | loop fusion | flops 294911 | bytes 786436 | tf_op jit(solution)/shard_map/reduce_sum | solution.py:87
  41.3 1.5 %fusion.8 = (f32[20,52,1]{2,0,1:T(8,128)}, f32[20,52,1]{2,0,1:T(8,128)}) fusion(f32[20,52,132]{2,0,1:T(8,128)S(1)} %select_select_fusion.4), kind=kLoop, calls=%fused_computation.78 | loop fusion | bytes 16640 | tf_op jit(solution)/shard_map/slice | solution.py:56
  42.8 1.5 %copy.42 = f32[20,52,1]{0,1,2:T(8,128)S(1)} copy(f32[20,52,1]{2,0,1:T(8,128)} %get-tuple-element.20) | data formatting | bytes 8320 | tf_op jit(solution)/shard_map/jit(_where)/broadcast_in_dim | solution.py:57
  44.3 1.5 %copy.41 = f32[20,52,1]{0,1,2:T(8,128)S(1)} copy(f32[20,52,1]{2,0,1:T(8,128)} %get-tuple-element.19) | data formatting | bytes 8320 | tf_op jit(solution)/shard_map/jit(_where)/broadcast_in_dim | solution.py:58
  45.8 0.6 select_select_fusion.3
  46.5 3.1 %multiply_subtract_fusion.1 = f32[18,50,130]{2,0,1:T(8,128)S(1)} fusion(f32[20,52,132]{2,0,1:T(8,128)S(1)} %select_select_fusion.3, f32[22,54,134]{2,0,1:T(8,128)S(1)} %get-tuple-element.11), kind=kLoop, calls=%fused_computation.24 | loop fusion | flops 5382000 | bytes 4212000 | tf_op jit(solution)/shard_map/sub | solution.py:49
  49.6 1.0 fusion.1
  51.9 1.2 %fusion.10 = (f32[18,50,1]{2,0,1:T(8,128)}, f32[18,50,1]{2,0,1:T(8,128)}) fusion(f32[18,50,130]{2,0,1:T(8,128)S(1)} %select_select_fusion.7), kind=kLoop, calls=%fused_computation.80 | loop fusion | bytes 14400 | tf_op jit(solution)/shard_map/slice | solution.py:56
  53.2 1.5 %copy.43 = f32[18,50,1]{0,1,2:T(8,128)S(1)} copy(f32[18,50,1]{2,0,1:T(8,128)} %get-tuple-element.25) | data formatting | bytes 7200 | tf_op jit(solution)/shard_map/jit(_where)/broadcast_in_dim | solution.py:58
  54.7 1.5 %copy.44 = f32[18,50,1]{0,1,2:T(8,128)S(1)} copy(f32[18,50,1]{2,0,1:T(8,128)} %get-tuple-element.26) | data formatting | bytes 7200 | tf_op jit(solution)/shard_map/jit(_where)/broadcast_in_dim | solution.py:57
  56.2 0.6 select_select_fusion.6
  56.8 1.6 %multiply_reduce_fusion = (f32[]{:T(128)}, f32[16,48,128]{2,0,1:T(8,128)S(1)}) fusion(f32[18,50,130]{2,0,1:T(8,128)S(1)} %select_select_fusion.6, f32[22,54,134]{2,0,1:T(8,128)S(1)} %get-tuple-element.11), kind=kLoop, calls=%fused_computation.38 | loop fusion | flops 4816895 | bytes 3538948 | tf_op jit(solution)/shard_map/reduce_sum | solution.py:87
  58.4 0.9 copy.38
  59.3 40.2 %all-reduce = (f32[1]{0:T(128)}, f32[1]{0:T(128)}, f32[1]{0:T(128)}) all-reduce(f32[1]{0:T(128)} %bitcast.20, f32[1]{0:T(128)} %bitcast.19, f32[1]{0:T(128)} %bitcast.18), channel_id=1, replica_groups=mesh['gx'=4,'gy'=2,'gz'=4] {'gx','gy','gz'}, use_global_device_ids=true, to_apply=%region_5.6 | all-reduce | flops 3 | bytes 24 | tf_op jit(solution)/shard_map/psum | solution.py:74
  99.5 2.5 %fusion.5 = f32[3]{0:T(128)} fusion(f32[1]{0:T(128)} %get-tuple-element.6, f32[1]{0:T(128)} %get-tuple-element.7, f32[1]{0:T(128)} %get-tuple-element.8), kind=kLoop, calls=%fused_computation.75 | loop fusion | flops 12 | bytes 24 | tf_op jit(solution)/shard_map/div | solution.py:94
  (60 shorter events, 7.9 us)
Async XLA Ops:
  1.8 8.5 %collective-permute-start = (f32[3,48,128]{2,0,1:T(4,128)S(1)}, f32[3,48,128]{2,0,1:T(4,128)S(1)}, u32[]{:S(2)}, u32[]{:S(2)}) collective-permute-start(f32[3,48,128]{2,0,1:T(4,128)S(1)} %get-tuple-element.35), channel_id=1, source_target_pairs={{0,8},{8,16},{16,24},{1,9},{9,17},{17,25},{2,10},{10,18},{18,26},{... | collective-permute-start | bytes 221192 | tf_op jit(solution)/shard_map/ppermute | solution.py:20
  6.7 6.5 %collective-permute-start.1 = (f32[3,48,128]{2,0,1:T(4,128)S(1)}, f32[3,48,128]{2,0,1:T(4,128)S(1)}, u32[]{:S(2)}, u32[]{:S(2)}) collective-permute-start(f32[3,48,128]{2,0,1:T(4,128)S(1)} %get-tuple-element.36), channel_id=1, source_target_pairs={{8,0},{16,8},{24,16},{9,1},{17,9},{25,17},{10,2},{18,10},{26,18},{... | collective-permute-start | bytes 221192 | tf_op jit(solution)/shard_map/ppermute | solution.py:22
  8.0 22.0 %copy-start.4 = (pred[54]{0:T(512)(128)(4,1)}, pred[54]{0:T(512)(128)(4,1)S(1)}, u32[]{:S(2)}) copy-start(pred[54]{0:T(512)(128)(4,1)S(1)} %get-tuple-element.41) | copy-start | bytes 166
  8.1 22.0 %copy-start.5 = (pred[54]{0:T(512)(128)(4,1)}, pred[54]{0:T(512)(128)(4,1)S(1)}, u32[]{:S(2)}) copy-start(pred[54]{0:T(512)(128)(4,1)S(1)} %get-tuple-element.42) | copy-start | bytes 166
  13.2 3.2 %collective-permute-start.2 = (f32[22,3,128]{2,0,1:T(8,128)S(1)}, f32[22,3,128]{2,0,1:T(8,128)S(1)}, u32[]{:S(2)}, u32[]{:S(2)}) collective-permute-start(f32[22,3,128]{2,0,1:T(8,128)S(1)} %get-tuple-element.33), channel_id=1, source_target_pairs={{0,4},{1,5},{2,6},{3,7},{8,12},{9,13},{10,14},{11,15},{16,20},{17,... | collective-permute-start | bytes 101384 | tf_op jit(solution)/shard_map/ppermute | solution.py:20
  14.5 3.1 %collective-permute-start.3 = (f32[22,3,128]{2,0,1:T(8,128)S(1)}, f32[22,3,128]{2,0,1:T(8,128)S(1)}, u32[]{:S(2)}, u32[]{:S(2)}) collective-permute-start(f32[22,3,128]{2,0,1:T(8,128)S(1)} %get-tuple-element.34), channel_id=1, source_target_pairs={{4,0},{5,1},{6,2},{7,3},{12,8},{13,9},{14,10},{15,11},{20,16},{21,... | collective-permute-start | bytes 101384 | tf_op jit(solution)/shard_map/ppermute | solution.py:22
  18.3 5.6 %collective-permute-start.4 = (f32[22,54,3]{1,0,2:T(8,128)S(1)}, f32[22,54,3]{1,0,2:T(8,128)S(1)}, u32[]{:S(2)}, u32[]{:S(2)}) collective-permute-start(f32[22,54,3]{1,0,2:T(8,128)S(1)} %copy.22), channel_id=1, source_target_pairs={{0,1},{1,2},{2,3},{4,5},{5,6},{6,7},{8,9},{9,10},{10,11},{12,13},{... | collective-permute-start | bytes 42776 | tf_op jit(solution)/shard_map/ppermute | solution.py:20
  22.1 5.9 %collective-permute-start.5 = (f32[22,54,3]{1,0,2:T(8,128)S(1)}, f32[22,54,3]{1,0,2:T(8,128)S(1)}, u32[]{:S(2)}, u32[]{:S(2)}) collective-permute-start(f32[22,54,3]{1,0,2:T(8,128)S(1)} %copy.23), channel_id=1, source_target_pairs={{1,0},{2,1},{3,2},{5,4},{6,5},{7,6},{9,8},{10,9},{11,10},{13,12},{... | collective-permute-start | bytes 42776 | tf_op jit(solution)/shard_map/ppermute | solution.py:22
  40.1 0.7 copy-start.2
  40.1 0.7 copy-start.3
  42.8 3.0 %copy-start.8 = (pred[132]{0:T(512)(128)(4,1)S(1)}, pred[132]{0:T(512)(128)(4,1)}, u32[]{:S(2)}) copy-start(pred[132]{0:T(512)(128)(4,1)} %get-tuple-element.49) | copy-start | bytes 400
  42.8 3.0 %copy-start.9 = (pred[132]{0:T(512)(128)(4,1)S(1)}, pred[132]{0:T(512)(128)(4,1)}, u32[]{:S(2)}) copy-start(pred[132]{0:T(512)(128)(4,1)} %get-tuple-element.50) | copy-start | bytes 400
  46.5 4.2 %copy-start = (pred[18]{0:T(512)(128)(4,1)S(1)}, pred[18]{0:T(512)(128)(4,1)}, u32[]{:S(2)}) copy-start(pred[18]{0:T(512)(128)(4,1)} %get-tuple-element.51) | copy-start | bytes 58
  46.5 4.2 %copy-start.1 = (pred[18]{0:T(512)(128)(4,1)S(1)}, pred[18]{0:T(512)(128)(4,1)}, u32[]{:S(2)}) copy-start(pred[18]{0:T(512)(128)(4,1)} %get-tuple-element.52) | copy-start | bytes 58
  50.7 0.7 copy-start.6
  50.7 0.7 copy-start.7
  51.9 4.2 %copy-start.10 = (pred[130]{0:T(512)(128)(4,1)S(1)}, pred[130]{0:T(512)(128)(4,1)}, u32[]{:S(2)}) copy-start(pred[130]{0:T(512)(128)(4,1)} %get-tuple-element.55) | copy-start | bytes 394
  51.9 4.2 %copy-start.11 = (pred[130]{0:T(512)(128)(4,1)S(1)}, pred[130]{0:T(512)(128)(4,1)}, u32[]{:S(2)}) copy-start(pred[130]{0:T(512)(128)(4,1)} %get-tuple-element.56) | copy-start | bytes 394
where the time goes:
time: 102 us
  blocking collectives  40.2 us (39%)
  other arithmetic  24.7 us (24%)
  local copies, waits for them, and re-layouts  14.7 us (14%)
  starting transfers between devices  13.5 us (13%)
  waiting for transfers between devices  7.76 us (8%)
  between operations  1.03 us (1%)
    psum x1, blocking collectives, reduce_now(): return lax.psum(partial_value, ('gx', 'gy', 'gz'))  40.2 us
    ppermute x3, starting transfers between devices, extended_2(): lax.ppermute(tail, axis, [(i, (i + 1) % count) for i in range(ends)])  9.66 us
    ppermute x3, waiting for transfers between devices, extended_2(): lax.ppermute(head, axis, [((i + 1) % count, i) for i in range(ends)])  7.75 us
    sub x2, other arithmetic, update(): return center - pseudo_step * sgn * (jnp.sqrt(total) - 1.0)  6.34 us
    select_n x8, other arithmetic, clamp_axis(): jnp.where((place == count - 1) & (position >= length - margin), high_valu...  4.72 us
    ppermute x3, starting transfers between devices, extended_2(): lax.ppermute(head, axis, [((i + 1) % count, i) for i in range(ends)])  3.88 us
    reduce_sum x3, other arithmetic, local(): partials.append(reduce_now(jnp.sum(difference * difference)))  3.58 us
    broadcast_in_dim x6, local copies, waits for them, and re-layouts, clamp_axis(): jnp.where((place == count - 1) & (position >= length - margin), high_valu...  3.46 us
  transfers between devices with their start and end apart: 6, of which 3 were waited for; matrix products, arithmetic and copies ran while one was open for 4% of the time, Pallas kernels for 0%

commit v1 on v0

v1 whole, which is shorter than its diff:
```python
import functools

import jax
import jax.numpy as jnp
from jax import lax
from jax.experimental import pallas as pl
from jax.experimental.pallas import tpu as pltpu
from jax.sharding import PartitionSpec as P

ITERS = 3
HALO = ITERS
AXES = ("gx", "gy", "gz")
TILE = 8
HALF = 64

pseudo_step = 0.45


def pair_swap(value, partner):
    sizes = [lax.axis_size(a) for a in AXES]

    def flat(place):
        return (place[0] * sizes[1] + place[1]) * sizes[2] + place[2]

    pairs = []
    for i in range(sizes[0]):
        for j in range(sizes[1]):
            for k in range(sizes[2]):
                pairs.append((flat((i, j, k)), flat(partner((i, j, k)))))
    return lax.ppermute(value, AXES, pairs)


def neighbour(dim, colour):
    sizes = [lax.axis_size(a) for a in AXES]

    def partner(place):
        place = list(place)
        here = place[dim]
        there = here ^ 1 if colour == 0 else ((here - 1) ^ 1) + 1
        if 0 <= there < sizes[dim]:
            place[dim] = there
        elif dim != 1 and sizes[1] % 2 == 0:
            place[1] ^= 1
        elif colour == 1 and sizes[dim] % 2 == 0:
            place[dim] = sizes[dim] - 1 - here
        return tuple(place)

    return partner


def exchange(value_even, value_odd, dim):
    first = pair_swap(value_even, neighbour(dim, 0))
    if lax.axis_size(AXES[dim]) == 2:
        return first, first
    return first, pair_swap(value_odd, neighbour(dim, 1))


def sum_over_devices(value):
    sizes = [lax.axis_size(a) for a in AXES]
    if any(n & (n - 1) for n in sizes):
        return lax.psum(value, AXES)
    rounds = []
    for dim in (1, 0, 2):
        bit = 1
        while bit < sizes[dim]:
            rounds.append((dim, bit))
            bit *= 2
    crossed = False
    for dim, bit in rounds:

        def partner(place, dim=dim, bit=bit, flip=crossed):
            place = list(place)
            place[dim] ^= bit
            if flip:
                place[1] ^= 1
            return tuple(place)

        value = value + pair_swap(value, partner)
        crossed = crossed or (dim, bit) == (1, 1)
    return value


def at_ends(axis):
    place = lax.axis_index(axis)
    return place == 0, place == lax.axis_size(axis) - 1


def odd(axis):
    return lax.rem(lax.axis_index(axis), 2) == 1


def low_high(first, second, axis):
    is_odd = odd(axis)
    return jnp.where(is_odd, first, second), jnp.where(is_odd, second, first)


def sign_factors(field):
    sgn = field * lax.rsqrt(field * field + 1.0)
    return jnp.where(field > 0.0, 1.0, -1.0), pseudo_step * sgn


def upwind(sc, s, prev, nxt):
    term = jnp.maximum(sc - jnp.minimum(s * prev, s * nxt), 0.0)
    return term * term


def stepped(c, k, total):
    root = total * lax.rsqrt(jnp.maximum(total, 1e-30))
    return c - k * (root - 1.0)


def plane_pieces(x, sizes, b_ref, xa_ref, xb_ref, ya_ref, yb_ref):
    planes = sizes[0]
    if x < HALO:
        own = low_high(xa_ref[x], xb_ref[x], "gx")[0]
    elif x >= HALO + planes:
        own = low_high(xa_ref[x - HALO - planes], xb_ref[x - HALO - planes], "gx")[1]
    else:
        own = b_ref[x - HALO]
    low, high = low_high(ya_ref[x], yb_ref[x], "gy")
    return own, low, high


def strip_kernel(
    sizes, b_ref, xa_ref, xb_ref, ya_ref, yb_ref, strip_ref, send_ref, lines_ref
):
    planes, rows, lanes = sizes
    wide = planes + 2 * HALO
    pitch = strip_ref.shape[0] // (3 * HALO)
    for x in range(wide):
        own, low, high = plane_pieces(x, sizes, b_ref, xa_ref, xb_ref, ya_ref, yb_ref)
        turned = jnp.concatenate([low, own, high], axis=0).T
        both = jnp.concatenate([turned[0:TILE], turned[lanes - TILE : lanes]], axis=1)
        lines_ref[pl.ds(x, TILE, stride=pitch)] = both
    near = lax.broadcasted_iota(jnp.int32, (pitch, 2 * HALF), 1) < HALF
    shift = TILE - 2 * HALO
    for j in range(3 * HALO):
        low = lines_ref[(j - HALO) * pitch : (j - HALO + 1) * pitch] if j >= HALO else None
        high = lines_ref[(j + shift) * pitch : (j + shift + 1) * pitch] if j < 2 * HALO else None
        if low is None:
            value = high
        elif high is None:
            value = low
        else:
            value = jnp.where(near, low, high)
            send_ref[(j - HALO) * pitch : (j - HALO + 1) * pitch] = value
        strip_ref[j * pitch : (j + 1) * pitch] = value


def main_kernel(
    sizes, b_ref, xa_ref, xb_ref, ya_ref, yb_ref, out_ref, acc_ref, e0, e1, s_ref, k_ref
):
    planes, rows, lanes = sizes
    wide = planes + 2 * HALO
    tall = rows + TILE
    x_first, x_last = at_ends("gx")
    y_first, y_last = at_ends("gy")
    sub = lax.broadcasted_iota(jnp.int32, (TILE, lanes), 0)
    lane = lax.broadcasted_iota(jnp.int32, (TILE, lanes), 1)

    for x in range(wide):
        own, low, high = plane_pieces(x, sizes, b_ref, xa_ref, xb_ref, ya_ref, yb_ref)
        full = jnp.concatenate([own, jnp.where(sub < TILE // 2, high, low)], axis=0)
        e0[x] = full
        s, k = sign_factors(full)
        s_ref[x] = s
        k_ref[x] = k

    def clamp_planes(ref):
        @pl.when(x_first)
        def _():
            ref[HALO - 1] = ref[HALO]

        @pl.when(x_last)
        def _():
            ref[HALO + planes] = ref[HALO + planes - 1]

    def plane_step(src, x):
        c = src[x]
        edge = c[rows:tall]
        edge = jnp.where((sub == TILE - 1) & y_first, c[0:1], edge)
        edge = jnp.where((sub == 0) & y_last, c[rows - 1 : rows], edge)
        around = jnp.concatenate([c[0:rows], edge], axis=0)
        s = s_ref[x]
        sc = s * c
        total = upwind(sc, s, src[x - 1], src[x + 1])
        total = total + upwind(
            sc, s, pltpu.roll(around, 1, 0), pltpu.roll(around, tall - 1, 0)
        )
        total = total + upwind(sc, s, pltpu.roll(c, 1, 1), pltpu.roll(c, lanes - 1, 1))
        new = stepped(c, k_ref[x], total)
        change = new[0:rows] - c[0:rows]
        change = change * change
        part = change[0:TILE]
        for t in range(TILE, rows, TILE):
            part = part + change[t : t + TILE]
        return new, part

    inner = (lane >= HALO) & (lane < lanes - HALO)
    bufs = (e0, e1, e0)
    for it in range(ITERS):
        src = bufs[it]
        clamp_planes(src)
        last = it == ITERS - 1

        def body(x, acc, src=src, it=it, last=last, counted=True):
            new, part = plane_step(src, x)
            if last:
                out_ref[x - HALO] = new[0:rows]
            else:
                bufs[it + 1][x] = new
            return acc + part if counted else acc

        acc = jnp.zeros((TILE, lanes), jnp.float32)
        for x in range(it + 1, HALO):
            body(x, acc, counted=False)
            body(wide - 1 - x, acc, counted=False)
        acc = lax.fori_loop(HALO, HALO + planes, body, acc, unroll=4)
        acc_ref[it] = jnp.where(inner, acc, 0.0)


def edge_kernel(sizes, strip_ref, za_ref, zb_ref, acc_ref, out_ref, sum_ref):
    planes, rows, lanes = sizes
    pitch = strip_ref.shape[0] // (3 * HALO)
    x_first, x_last = at_ends("gx")
    y_first, y_last = at_ends("gy")
    z_first, z_last = at_ends("gz")
    shape = (pitch, 2 * HALF)
    line = lax.broadcasted_iota(jnp.int32, shape, 0)
    lane = lax.broadcasted_iota(jnp.int32, shape, 1)
    near = lane < HALF
    y = jnp.where(near, lane, lane - HALF) - TILE
    x = line - HALO
    low_x = (x == 0) & x_first
    high_x = (x == planes - 1) & x_last
    low_y = (y == 0) & y_first
    high_y = (y == rows - 1) & y_last
    low_z = near & z_first
    high_z = (lane >= HALF) & z_last
    mine = (x >= 0) & (x < planes) & (y >= 0) & (y < rows)

    state = []
    for j in range(3 * HALO):
        own = strip_ref[j * pitch : (j + 1) * pitch]
        if j < HALO:
            got = low_high(
                za_ref[j * pitch : (j + 1) * pitch], zb_ref[j * pitch : (j + 1) * pitch], "gz"
            )[0]
            own = jnp.where(near, pltpu.roll(got, HALF, 1), own)
        elif j >= 2 * HALO:
            i = j - 2 * HALO
            got = low_high(
                za_ref[i * pitch : (i + 1) * pitch], zb_ref[i * pitch : (i + 1) * pitch], "gz"
            )[1]
            own = jnp.where(near, own, pltpu.roll(got, HALF, 1))
        state.append(own)
    factors = [sign_factors(v) for v in state]

    sums = []
    for it in range(ITERS):
        new = list(state)
        change = jnp.zeros(shape, jnp.float32)
        for j in range(it + 1, 3 * HALO - 1 - it):
            c = state[j]
            s, k = factors[j]
            sc = s * c
            total = upwind(
                sc,
                s,
                jnp.where(low_x, c, pltpu.roll(c, 1, 0)),
                jnp.where(high_x, c, pltpu.roll(c, pitch - 1, 0)),
            )
            total = total + upwind(
                sc,
                s,
                jnp.where(low_y, c, pltpu.roll(c, 1, 1)),
                jnp.where(high_y, c, pltpu.roll(c, 2 * HALF - 1, 1)),
            )
            before, after = state[j - 1], state[j + 1]
            if j == HALO:
                before = jnp.where(low_z, c, before)
            if j == 2 * HALO - 1:
                after = jnp.where(high_z, c, after)
            total = total + upwind(sc, s, before, after)
            new[j] = stepped(c, k, total)
            if HALO <= j < 2 * HALO:
                change = change + (new[j] - c) * (new[j] - c)
        state = new
        change = jnp.where(mine, change, 0.0)
        part = acc_ref[it]
        for t in range(0, pitch, TILE):
            part = part + change[t : t + TILE]
        sums.append(jnp.sum(part, axis=0, keepdims=True))
    for i in range(HALO):
        out_ref[i * pitch : (i + 1) * pitch] = state[HALO + i]
    sums.append(jnp.zeros((TILE - ITERS, 2 * HALF), jnp.float32))
    sum_ref[...] = jnp.concatenate(sums, axis=0)


def merge_kernel(sizes, main_ref, edge_ref, out_ref):
    planes, rows, lanes = sizes
    pitch = edge_ref.shape[0] // HALO
    lane = lax.broadcasted_iota(jnp.int32, (rows, lanes), 1)
    for x in range(planes):
        lines = edge_ref[pl.ds(x + HALO, HALO, stride=pitch)]
        lines = jnp.concatenate(
            [lines, jnp.zeros((lanes - HALO, 2 * HALF), jnp.float32)], axis=0
        )
        turned = lines.T
        near = turned[TILE : TILE + rows]
        far = pltpu.roll(turned[HALF + TILE : HALF + TILE + rows], lanes - HALO, 1)
        value = jnp.where(lane < HALO, near, main_ref[x])
        out_ref[x] = jnp.where(lane >= lanes - HALO, far, value)


def vmem(n):
    return [pl.BlockSpec(memory_space=pltpu.VMEM)] * n


def cost(us, nbytes):
    return pl.CostEstimate(flops=int(us * 3.5e6), bytes_accessed=nbytes, transcendentals=0)


def local(phi_start):
    sizes = phi_start.shape
    planes, rows, lanes = sizes
    wide = planes + 2 * HALO
    tall = rows + TILE
    pitch = -(-wide // TILE) * TILE
    f32 = jnp.float32

    low, high = phi_start[:HALO], phi_start[planes - HALO :]
    x_odd, y_odd = odd("gx"), odd("gy")
    xa, xb = exchange(jnp.where(x_odd, low, high), jnp.where(x_odd, high, low), 0)

    tops = jnp.concatenate([t[:, :TILE] for t in (*low_high(xa, xb, "gx"),)], axis=0)
    tails = jnp.concatenate([t[:, rows - TILE :] for t in (*low_high(xa, xb, "gx"),)], axis=0)
    tops = jnp.concatenate([tops[:HALO], phi_start[:, :TILE], tops[HALO:]], axis=0)
    tails = jnp.concatenate([tails[:HALO], phi_start[:, rows - TILE :], tails[HALO:]], axis=0)
    ya, yb = exchange(jnp.where(y_odd, tops, tails), jnp.where(y_odd, tails, tops), 1)

    strip, send = pl.pallas_call(
        functools.partial(strip_kernel, sizes),
        out_shape=(
            jax.ShapeDtypeStruct((3 * HALO * pitch, 2 * HALF), f32),
            jax.ShapeDtypeStruct((HALO * pitch, 2 * HALF), f32),
        ),
        in_specs=vmem(5),
        out_specs=tuple(vmem(2)),
        scratch_shapes=[pltpu.VMEM((TILE * pitch, 2 * HALF), f32)],
        cost_estimate=cost(1, 10**6),
        name="strips",
    )(phi_start, xa, xb, ya, yb)
    za, zb = exchange(send, send, 2)

    inner, acc = pl.pallas_call(
        functools.partial(main_kernel, sizes),
        out_shape=(
            jax.ShapeDtypeStruct(sizes, f32),
            jax.ShapeDtypeStruct((ITERS, TILE, lanes), f32),
        ),
        in_specs=vmem(5),
        out_specs=tuple(vmem(2)),
        scratch_shapes=[pltpu.VMEM((wide, tall, lanes), f32)] * 4,
        cost_estimate=cost(3, 10**6),
        name="inner",
    )(phi_start, xa, xb, ya, yb)

    edge, sums = pl.pallas_call(
        functools.partial(edge_kernel, sizes),
        out_shape=(
            jax.ShapeDtypeStruct((HALO * pitch, 2 * HALF), f32),
            jax.ShapeDtypeStruct((TILE, 2 * HALF), f32),
        ),
        in_specs=vmem(4),
        out_specs=tuple(vmem(2)),
        cost_estimate=cost(1, 10**5),
        name="edges",
    )(strip, za, zb, acc)

    phi_final = pl.pallas_call(
        functools.partial(merge_kernel, sizes),
        out_shape=jax.ShapeDtypeStruct(sizes, f32),
        in_specs=vmem(2),
        out_specs=vmem(1)[0],
        cost_estimate=cost(1, 10**6),
        name="merge",
    )(inner, edge)

    totals = jnp.sum(sum_over_devices(sums)[:ITERS], axis=1)
    cells = planes * rows * lanes
    for axis in AXES:
        cells = cells * lax.axis_size(axis)
    residuals = jnp.sqrt(totals / jnp.float32(cells)) / pseudo_step
    return (phi_final, residuals)


def solution(mesh):
    return jax.shard_map(
        local,
        mesh=mesh,
        in_specs=(P("gx", "gy", "gz"),),
        out_specs=(P("gx", "gy", "gz"), P()),
        check_vma=False,
    )
```

time: 102 us -> 40.4 us (0.40)
  blocking collectives: 40.2 us -> 0 us
  other arithmetic: 24.7 us -> 2.31 us
  local copies, waits for them, and re-layouts: 14.7 us -> 2.73 us
  Pallas kernels: 0 us -> 10.5 us
  waiting for transfers between devices: 7.76 us -> 14 us
  starting transfers between devices: 13.5 us -> 9.77 us
    psum x1 -> x0, blocking collectives: 40.2 us -> none  [reduce_now(): return lax.psum(partial_value, ('gx', 'gy', 'gz'))]
    pallas_call x0 -> x4, Pallas kernels: none -> 10.5 us  [the longest x1 4.07 us: local(): pl.pallas_call(functools.partial(main_kernel, sizes), out_shape=(jax.Shap...]
    broadcast_in_dim x9 -> x0, local copies, waits for them, and re-layouts: 6.9 us -> none  [the longest x6 3.46 us: clamp_axis(): jnp.where((place == count - 1) & (position >= length - margin), high_valu...]
    sub x2 -> x0, other arithmetic: 6.34 us -> none  [update(): return center - pseudo_step * sgn * (jnp.sqrt(total) - 1.0)]
    ppermute x6 -> x10, waiting for transfers between devices: 7.76 us -> 14 us  [pair_swap(): return lax.ppermute(value, AXES, pairs)]
    div x2 -> x1, other arithmetic: 5.75 us -> 0.53 us  [local(): residuals = jnp.sqrt(totals / jnp.float32(cells)) / pseudo_step]
    ppermute x6 -> x10, starting transfers between devices: 13.5 us -> 9.77 us  [pair_swap(): return lax.ppermute(value, AXES, pairs)]
    select_n x8 -> x3, other arithmetic: 4.72 us -> 0.97 us  [the longest x1 0.94 us: local(): jnp.where(x_odd, high, low)]
  transfers between devices with their start and end apart: 6 -> 10, of which waited for: 3 -> 7; matrix products, arithmetic and copies ran while one was open for 4% -> 2% of each run, Pallas kernels for 0% -> 16%
where the time goes in v1:
time: 40.4 us; the launch traced here: 40.1 us
  waiting for transfers between devices  14 us (35%)
  Pallas kernels  10.5 us (26%)
  starting transfers between devices  9.77 us (24%)
  local copies, waits for them, and re-layouts  2.73 us (7%)
  other arithmetic  2.31 us (6%)
  between operations  0.71 us (2%)
    ppermute x10, waiting for transfers between devices, pair_swap(): return lax.ppermute(value, AXES, pairs)  14 us
    ppermute x10, starting transfers between devices, pair_swap(): return lax.ppermute(value, AXES, pairs)  9.77 us
    pallas_call x1, Pallas kernels, local(): pl.pallas_call(functools.partial(main_kernel, sizes), out_shape=(jax.Shap...  4.07 us
    pallas_call x1, Pallas kernels, local(): pl.pallas_call(functools.partial(strip_kernel, sizes), out_shape=(jax.Sha...  2.29 us
    pallas_call x1, Pallas kernels, local(): pl.pallas_call(functools.partial(merge_kernel, sizes), out_shape=jax.Shap...  2.28 us
    pallas_call x1, Pallas kernels, local(): pl.pallas_call(functools.partial(edge_kernel, sizes), out_shape=(jax.Shap...  1.86 us
    unnamed x10, local copies, waits for them, and re-layouts  1.84 us
    select_n x1, other arithmetic, local(): jnp.where(x_odd, high, low)  0.94 us
  transfers between devices with their start and end apart: 10, of which 7 were waited for; matrix products, arithmetic and copies ran while one was open for 2% of the time, Pallas kernels for 16%

profile of v1, /device:TPU:0, one launch (start us, length us, event | category | flops | bytes accessed | tf_op | source)
XLA Modules:
  0.0 40.1 jit_solution(4667824100552431926)
XLA Ops:
  0.6 0.9 %slice_select_fusion = (f32[3,48,128]{2,1,0:T(8,128)S(1)}, f32[3,48,128]{2,1,0:T(8,128)S(1)}) fusion(f32[16,48,128]{2,1,0:T(8,128)} %b_ref.3, pred[]{:T(512)S(6)} %eq.8), kind=kLoop, calls=%fused_computation.1 | loop fusion | flops 36864 | bytes 294913 | tf_op jit(solution)/shard_map/jit(_where)/select_n | solution.py:334
  1.6 0.6 %collective-permute-start.1 = (f32[3,48,128]{2,1,0:T(8,128)S(1)}, f32[3,48,128]{2,1,0:T(8,128)S(1)}, u32[]{:S(2)}, u32[]{:S(2)}) collective-permute-start(f32[3,48,128]{2,1,0:T(8,128)S(1)} %get-tuple-element.16), channel_id=1, source_target_pairs={{0,4},{1,5},{2,6},{3,7},{4,0},{5,1},{6,2},{7,3},{8,16},{9,17},{10,... | collective-permute-start | bytes 221192 | tf_op jit(solution)/shard_map/ppermute | solution.py:30
  2.1 4.0 %collective-permute-start = (f32[3,48,128]{2,1,0:T(8,128)S(1)}, f32[3,48,128]{2,1,0:T(8,128)S(1)}, u32[]{:S(2)}, u32[]{:S(2)}) collective-permute-start(f32[3,48,128]{2,1,0:T(8,128)S(1)} %get-tuple-element.17), channel_id=1, source_target_pairs={{0,8},{1,9},{2,10},{3,11},{4,12},{5,13},{6,14},{7,15},{8,0},{9,1},... | collective-permute-start | bytes 221192 | tf_op jit(solution)/shard_map/ppermute | solution.py:30
  6.1 0.9 %fusion = (f32[16,8,128]{2,1,0:T(8,128)S(1)}, f32[16,8,128]{2,1,0:T(8,128)S(1)}) fusion(f32[16,48,128]{2,1,0:T(8,128)} %b_ref.3), kind=kLoop, calls=%fused_computation.7 | loop fusion | bytes 262144 | tf_op jit(solution)/shard_map/slice | solution.py:339
  7.0 0.0 collective-permute-done.1.xb_ref
  7.0 2.7 %collective-permute-done.xa_ref = f32[3,48,128]{2,1,0:T(8,128)S(1)} collective-permute-done((f32[3,48,128]{2,1,0:T(8,128)S(1)}, f32[3,48,128]{2,1,0:T(8,128)S(1)}, u32[]{:S(2)}, u32[]{:S(2)}) %collective-permute-start) | collective-permute-done | bytes 73760 | tf_op jit(solution)/shard_map/ppermute | solution.py:30
  9.7 0.6 %copy-done.2 = f32[3,48,128]{2,1,0:T(8,128)} copy-done((f32[3,48,128]{2,1,0:T(8,128)}, f32[3,48,128]{2,1,0:T(8,128)S(1)}, u32[]{:S(2)}) %copy-start.2) | copy-done | bytes 73752
  10.3 0.1 collective-permute-start.2
  10.4 1.3 %collective-permute-done.2.ya_ref.yb_ref = f32[22,8,128]{2,1,0:T(8,128)S(1)} collective-permute-done((f32[22,8,128]{2,1,0:T(8,128)S(1)}, f32[22,8,128]{2,1,0:T(8,128)S(1)}, u32[]{:S(2)}, u32[]{:S(2)}) %collective-permute-start.2) | collective-permute-done | bytes 90144 | tf_op jit(solution)/shard_map/ppermute | solution.py:30
  11.7 0.6 %copy-done = f32[22,8,128]{2,1,0:T(8,128)} copy-done((f32[22,8,128]{2,1,0:T(8,128)}, f32[22,8,128]{2,1,0:T(8,128)S(1)}, u32[]{:S(2)}) %copy-start) | copy-done | bytes 90136
  12.3 2.3 %strips.1 = (f32[216,128]{1,0:T(8,128)}, f32[72,128]{1,0:T(8,128)}) custom-call(f32[16,48,128]{2,1,0:T(8,128)} %b_ref.3, f32[3,48,128]{2,1,0:T(8,128)} %copy-done.2, f32[3,48,128]{2,1,0:T(8,128)} %copy-done.1, f32[22,8,128]{2,1,0:T(8,128)} %copy-done, f32[22,8,128]{2,1,0:T(8,128)} %copy-done), custom_call_target="tpu_custom_call" | custom-call | flops 3500000 | bytes 1000000 | tf_op jit(solution)/shard_map/strips/pallas_call | solution.py:342
  14.6 0.2 collective-permute-start.4
  14.7 3.0 %collective-permute-start.3 = (f32[72,128]{1,0:T(8,128)}, f32[72,128]{1,0:T(8,128)S(1)}, u32[]{:S(2)}, u32[]{:S(2)}) collective-permute-start(f32[72,128]{1,0:T(8,128)} %get-tuple-element.10), channel_id=1, source_target_pairs={{0,1},{1,0},{2,3},{3,2},{4,5},{5,4},{6,7},{7,6},{8,9},{9,8},{10,11... | collective-permute-start | bytes 110600 | tf_op jit(solution)/shard_map/ppermute | solution.py:30
  17.7 4.1 %inner.1 = (f32[16,48,128]{2,1,0:T(8,128)}, f32[3,8,128]{2,1,0:T(8,128)}) custom-call(f32[16,48,128]{2,1,0:T(8,128)} %b_ref.3, f32[3,48,128]{2,1,0:T(8,128)} %copy-done.2, f32[3,48,128]{2,1,0:T(8,128)} %copy-done.1, f32[22,8,128]{2,1,0:T(8,128)} %copy-done, f32[22,8,128]{2,1,0:T(8,128)} %copy-done), custom_call_target="tpu_custom_call" | custom-call | flops 10500000 | bytes 1000000 | tf_op jit(solution)/shard_map/inner/pallas_call | solution.py:356
  21.8 0.0 collective-permute-done.4.zb_ref
  21.8 0.0 collective-permute-done.3.za_ref
  21.8 0.6 %copy-done.3 = f32[72,128]{1,0:T(8,128)} copy-done((f32[72,128]{1,0:T(8,128)}, f32[72,128]{1,0:T(8,128)S(1)}, u32[]{:S(2)}) %copy-start.3) | copy-done | bytes 36888
  22.4 0.0 copy-done.4
  22.4 1.9 %edges.1 = (f32[72,128]{1,0:T(8,128)}, f32[8,128]{1,0:T(8,128)}) custom-call(f32[216,128]{1,0:T(8,128)} %get-tuple-element.9.strip_ref, f32[72,128]{1,0:T(8,128)} %copy-done.4, f32[72,128]{1,0:T(8,128)} %copy-done.3, f32[3,8,128]{2,1,0:T(8,128)} %get-tuple-element.11.acc_ref), custom_call_target="tpu_custom_call" | custom-call | flops 3500000 | bytes 100000 | tf_op jit(solution)/shard_map/edges/pallas_call | solution.py:369
  24.3 0.0 collective-permute-start.5
  24.3 1.4 %collective-permute-done.5 = f32[8,128]{1,0:T(8,128)S(1)} collective-permute-done((f32[8,128]{1,0:T(8,128)}, f32[8,128]{1,0:T(8,128)S(1)}, u32[]{:S(2)}, u32[]{:S(2)}) %collective-permute-start.5) | collective-permute-done | bytes 4128 | tf_op jit(solution)/shard_map/ppermute | solution.py:30
  25.7 0.7 %add.15 = f32[8,128]{1,0:T(8,128)S(1)} add(f32[8,128]{1,0:T(8,128)} %get-tuple-element.13, f32[8,128]{1,0:T(8,128)S(1)} %collective-permute-done.5) | non-fusion elementwise | flops 1024 | bytes 12288 | tf_op jit(solution)/shard_map/add | solution.py:78
  26.4 0.6 %collective-permute-start.6 = (f32[8,128]{1,0:T(8,128)S(1)}, f32[8,128]{1,0:T(8,128)S(1)}, u32[]{:S(2)}, u32[]{:S(2)}) collective-permute-start(f32[8,128]{1,0:T(8,128)S(1)} %add.15), channel_id=1, source_target_pairs={{0,12},{1,13},{2,14},{3,15},{4,8},{5,9},{6,10},{7,11},{8,4},{9,5},... | collective-permute-start | bytes 12296 | tf_op jit(solution)/shard_map/ppermute | solution.py:30
  26.9 2.5 %collective-permute-done.6 = f32[8,128]{1,0:T(8,128)S(1)} collective-permute-done((f32[8,128]{1,0:T(8,128)S(1)}, f32[8,128]{1,0:T(8,128)S(1)}, u32[]{:S(2)}, u32[]{:S(2)}) %collective-permute-start.6) | collective-permute-done | bytes 4128 | tf_op jit(solution)/shard_map/ppermute | solution.py:30
  29.4 0.5 %collective-permute-start.7 = (f32[8,128]{1,0:T(8,128)S(1)}, f32[8,128]{1,0:T(8,128)S(1)}, u32[]{:S(2)}, u32[]{:S(2)}) collective-permute-start(f32[8,128]{1,0:T(8,128)S(1)} %add.16), channel_id=1, source_target_pairs={{0,20},{1,21},{2,22},{3,23},{4,16},{5,17},{6,18},{7,19},{8,28},{9,... | collective-permute-start | bytes 12296 | tf_op jit(solution)/shard_map/ppermute | solution.py:30
  29.9 2.5 %collective-permute-done.7 = f32[8,128]{1,0:T(8,128)S(1)} collective-permute-done((f32[8,128]{1,0:T(8,128)S(1)}, f32[8,128]{1,0:T(8,128)S(1)}, u32[]{:S(2)}, u32[]{:S(2)}) %collective-permute-start.7) | collective-permute-done | bytes 4128 | tf_op jit(solution)/shard_map/ppermute | solution.py:30
  32.4 3.0 %collective-permute-done.8 = f32[8,128]{1,0:T(8,128)S(1)} collective-permute-done((f32[8,128]{1,0:T(8,128)S(1)}, f32[8,128]{1,0:T(8,128)S(1)}, u32[]{:S(2)}, u32[]{:S(2)}) %collective-permute-start.8) | collective-permute-done | bytes 4128 | tf_op jit(solution)/shard_map/ppermute | solution.py:30
  35.5 0.9 %collective-permute-start.9 = (f32[8,128]{1,0:T(8,128)S(1)}, f32[8,128]{1,0:T(8,128)S(1)}, u32[]{:S(2)}, u32[]{:S(2)}) collective-permute-start(f32[8,128]{1,0:T(8,128)S(1)} %add.18), channel_id=1, source_target_pairs={{0,6},{1,7},{2,4},{3,5},{4,2},{5,3},{6,0},{7,1},{8,14},{9,15},{10,... | collective-permute-start | bytes 12296 | tf_op jit(solution)/shard_map/ppermute | solution.py:30
  36.4 2.3 %merge.1 = f32[16,48,128]{2,1,0:T(8,128)} custom-call(f32[16,48,128]{2,1,0:T(8,128)} %get-tuple-element.8.main_ref, f32[72,128]{1,0:T(8,128)} %get-tuple-element.12.edge_ref), custom_call_target="tpu_custom_call" | custom-call | flops 3500000 | bytes 1000000 | tf_op jit(solution)/shard_map/merge/pallas_call | solution.py:381
  38.7 0.7 %collective-permute-done.9 = f32[8,128]{1,0:T(8,128)S(1)} collective-permute-done((f32[8,128]{1,0:T(8,128)S(1)}, f32[8,128]{1,0:T(8,128)S(1)}, u32[]{:S(2)}, u32[]{:S(2)}) %collective-permute-start.9) | collective-permute-done | bytes 4128 | tf_op jit(solution)/shard_map/ppermute | solution.py:30
  39.4 0.1 slice_reduce_fusion
  39.5 0.5 %sqrt_multiply_fusion = f32[3]{0:T(128)} fusion(f32[3]{0:T(128)S(1)} %slice_reduce_fusion), kind=kLoop, calls=%fused_computation.6 | loop fusion | flops 6 | bytes 24 | tf_op jit(solution)/shard_map/div | solution.py:394
  (14 shorter events, 0.1 us)
Async XLA Ops:
  1.6 5.4 %collective-permute-start.1 = (f32[3,48,128]{2,1,0:T(8,128)S(1)}, f32[3,48,128]{2,1,0:T(8,128)S(1)}, u32[]{:S(2)}, u32[]{:S(2)}) collective-permute-start(f32[3,48,128]{2,1,0:T(8,128)S(1)} %get-tuple-element.16), channel_id=1, source_target_pairs={{0,4},{1,5},{2,6},{3,7},{4,0},{5,1},{6,2},{7,3},{8,16},{9,17},{10,... | collective-permute-start | bytes 221192 | tf_op jit(solution)/shard_map/ppermute | solution.py:30
  2.1 7.5 %collective-permute-start = (f32[3,48,128]{2,1,0:T(8,128)S(1)}, f32[3,48,128]{2,1,0:T(8,128)S(1)}, u32[]{:S(2)}, u32[]{:S(2)}) collective-permute-start(f32[3,48,128]{2,1,0:T(8,128)S(1)} %get-tuple-element.17), channel_id=1, source_target_pairs={{0,8},{1,9},{2,10},{3,11},{4,12},{5,13},{6,14},{7,15},{8,0},{9,1},... | collective-permute-start | bytes 221192 | tf_op jit(solution)/shard_map/ppermute | solution.py:30
  7.0 2.7 %copy-start.1 = (f32[3,48,128]{2,1,0:T(8,128)}, f32[3,48,128]{2,1,0:T(8,128)S(1)}, u32[]{:S(2)}) copy-start(f32[3,48,128]{2,1,0:T(8,128)S(1)} %collective-permute-done.1.xb_ref) | copy-start | bytes 221188
  9.7 0.6 %copy-start.2 = (f32[3,48,128]{2,1,0:T(8,128)}, f32[3,48,128]{2,1,0:T(8,128)S(1)}, u32[]{:S(2)}) copy-start(f32[3,48,128]{2,1,0:T(8,128)S(1)} %collective-permute-done.xa_ref) | copy-start | bytes 221188
  10.3 1.4 %collective-permute-start.2 = (f32[22,8,128]{2,1,0:T(8,128)S(1)}, f32[22,8,128]{2,1,0:T(8,128)S(1)}, u32[]{:S(2)}, u32[]{:S(2)}) collective-permute-start(f32[22,8,128]{2,1,0:T(8,128)S(1)} %maximum_select_fusion), channel_id=1, source_target_pairs={{0,4},{1,5},{2,6},{3,7},{4,0},{5,1},{6,2},{7,3},{8,12},{9,13},{10,... | collective-permute-start | bytes 270344 | tf_op jit(solution)/shard_map/ppermute | solution.py:30
  11.7 0.6 %copy-start = (f32[22,8,128]{2,1,0:T(8,128)}, f32[22,8,128]{2,1,0:T(8,128)S(1)}, u32[]{:S(2)}) copy-start(f32[22,8,128]{2,1,0:T(8,128)S(1)} %collective-permute-done.2.ya_ref.yb_ref) | copy-start | bytes 270340
  14.6 7.2 %collective-permute-start.4 = (f32[72,128]{1,0:T(8,128)}, f32[72,128]{1,0:T(8,128)S(1)}, u32[]{:S(2)}, u32[]{:S(2)}) collective-permute-start(f32[72,128]{1,0:T(8,128)} %get-tuple-element.10), channel_id=1, source_target_pairs={{0,4},{1,2},{2,1},{3,7},{4,0},{5,6},{6,5},{7,3},{8,12},{9,10},{10,... | collective-permute-start | bytes 110600 | tf_op jit(solution)/shard_map/ppermute | solution.py:30
  14.7 7.1 %collective-permute-start.3 = (f32[72,128]{1,0:T(8,128)}, f32[72,128]{1,0:T(8,128)S(1)}, u32[]{:S(2)}, u32[]{:S(2)}) collective-permute-start(f32[72,128]{1,0:T(8,128)} %get-tuple-element.10), channel_id=1, source_target_pairs={{0,1},{1,0},{2,3},{3,2},{4,5},{5,4},{6,7},{7,6},{8,9},{9,8},{10,11... | collective-permute-start | bytes 110600 | tf_op jit(solution)/shard_map/ppermute | solution.py:30
  21.8 0.6 %copy-start.3 = (f32[72,128]{1,0:T(8,128)}, f32[72,128]{1,0:T(8,128)S(1)}, u32[]{:S(2)}) copy-start(f32[72,128]{1,0:T(8,128)S(1)} %collective-permute-done.4.zb_ref) | copy-start | bytes 110596
  21.8 0.6 %copy-start.4 = (f32[72,128]{1,0:T(8,128)}, f32[72,128]{1,0:T(8,128)S(1)}, u32[]{:S(2)}) copy-start(f32[72,128]{1,0:T(8,128)S(1)} %collective-permute-done.3.za_ref) | copy-start | bytes 110596
  24.3 1.4 %collective-permute-start.5 = (f32[8,128]{1,0:T(8,128)}, f32[8,128]{1,0:T(8,128)S(1)}, u32[]{:S(2)}, u32[]{:S(2)}) collective-permute-start(f32[8,128]{1,0:T(8,128)} %get-tuple-element.13), channel_id=1, source_target_pairs={{0,4},{1,5},{2,6},{3,7},{4,0},{5,1},{6,2},{7,3},{8,12},{9,13},{10,... | collective-permute-start | bytes 12296 | tf_op jit(solution)/shard_map/ppermute | solution.py:30
  26.4 3.0 %collective-permute-start.6 = (f32[8,128]{1,0:T(8,128)S(1)}, f32[8,128]{1,0:T(8,128)S(1)}, u32[]{:S(2)}, u32[]{:S(2)}) collective-permute-start(f32[8,128]{1,0:T(8,128)S(1)} %add.15), channel_id=1, source_target_pairs={{0,12},{1,13},{2,14},{3,15},{4,8},{5,9},{6,10},{7,11},{8,4},{9,5},... | collective-permute-start | bytes 12296 | tf_op jit(solution)/shard_map/ppermute | solution.py:30
  29.4 3.0 %collective-permute-start.7 = (f32[8,128]{1,0:T(8,128)S(1)}, f32[8,128]{1,0:T(8,128)S(1)}, u32[]{:S(2)}, u32[]{:S(2)}) collective-permute-start(f32[8,128]{1,0:T(8,128)S(1)} %add.16), channel_id=1, source_target_pairs={{0,20},{1,21},{2,22},{3,23},{4,16},{5,17},{6,18},{7,19},{8,28},{9,... | collective-permute-start | bytes 12296 | tf_op jit(solution)/shard_map/ppermute | solution.py:30
  32.4 3.0 %collective-permute-start.8 = (f32[8,128]{1,0:T(8,128)S(1)}, f32[8,128]{1,0:T(8,128)S(1)}, u32[]{:S(2)}, u32[]{:S(2)}) collective-permute-start(f32[8,128]{1,0:T(8,128)S(1)} %add.17), channel_id=1, source_target_pairs={{0,5},{1,4},{2,7},{3,6},{4,1},{5,0},{6,3},{7,2},{8,13},{9,12},{10,... | collective-permute-start | bytes 12296 | tf_op jit(solution)/shard_map/ppermute | solution.py:30
  35.5 3.9 %collective-permute-start.9 = (f32[8,128]{1,0:T(8,128)S(1)}, f32[8,128]{1,0:T(8,128)S(1)}, u32[]{:S(2)}, u32[]{:S(2)}) collective-permute-start(f32[8,128]{1,0:T(8,128)S(1)} %add.18), channel_id=1, source_target_pairs={{0,6},{1,7},{2,4},{3,5},{4,2},{5,3},{6,0},{7,1},{8,14},{9,15},{10,... | collective-permute-start | bytes 12296 | tf_op jit(solution)/shard_map/ppermute | solution.py:30

commit v2 on v1

--- a/solution.py
+++ b/solution.py
@@ -317,6 +317,10 @@
     return [pl.BlockSpec(memory_space=pltpu.VMEM)] * n
 
 
+def grant(mib):
+    return pltpu.CompilerParams(vmem_limit_bytes=mib * 2**20)
+
+
 def cost(us, nbytes):
     return pl.CostEstimate(flops=int(us * 3.5e6), bytes_accessed=nbytes, transcendentals=0)
 
@@ -349,6 +353,7 @@
         out_specs=tuple(vmem(2)),
         scratch_shapes=[pltpu.VMEM((TILE * pitch, 2 * HALF), f32)],
         cost_estimate=cost(1, 10**6),
+        compiler_params=grant(4),
         name="strips",
     )(phi_start, xa, xb, ya, yb)
     za, zb = exchange(send, send, 2)
@@ -363,6 +368,7 @@
         out_specs=tuple(vmem(2)),
         scratch_shapes=[pltpu.VMEM((wide, tall, lanes), f32)] * 4,
         cost_estimate=cost(3, 10**6),
+        compiler_params=grant(8),
         name="inner",
     )(phi_start, xa, xb, ya, yb)
 
@@ -375,6 +381,7 @@
         in_specs=vmem(4),
         out_specs=tuple(vmem(2)),
         cost_estimate=cost(1, 10**5),
+        compiler_params=grant(4),
         name="edges",
     )(strip, za, zb, acc)
 
@@ -384,6 +391,7 @@
         in_specs=vmem(2),
         out_specs=vmem(1)[0],
         cost_estimate=cost(1, 10**6),
+        compiler_params=grant(4),
         name="merge",
     )(inner, edge)
 

time: 40.4 us -> 32.5 us (0.80)
  Pallas kernels: 10.5 us -> 4.35 us
  starting transfers between devices: 9.77 us -> 11.8 us
  local copies, waits for them, and re-layouts: 2.73 us -> 0.89 us
  waiting for transfers between devices: 14 us -> 12.9 us
  other arithmetic: 2.31 us -> 1.62 us
    ppermute x10, starting transfers between devices: 9.77 us -> 11.8 us  [pair_swap(): return lax.ppermute(value, AXES, pairs)]
    pallas_call x1, Pallas kernels: 4.07 us -> 2.21 us  [local(): pl.pallas_call(functools.partial(main_kernel, sizes), out_shape=(jax.Shap...]
    unnamed x10 -> x2, local copies, waits for them, and re-layouts: 1.84 us -> 0.01 us
    pallas_call x1, Pallas kernels: 2.29 us -> 0.53 us  [local(): pl.pallas_call(functools.partial(strip_kernel, sizes), out_shape=(jax.Sha...]
    pallas_call x1, Pallas kernels: 1.86 us -> 0.32 us  [local(): pl.pallas_call(functools.partial(edge_kernel, sizes), out_shape=(jax.Shap...]
    ppermute x10, waiting for transfers between devices: 14 us -> 12.9 us  [pair_swap(): return lax.ppermute(value, AXES, pairs)]
    pallas_call x1, Pallas kernels: 2.28 us -> 1.29 us  [local(): pl.pallas_call(functools.partial(merge_kernel, sizes), out_shape=jax.Shap...]
    add x5, other arithmetic: 0.7 us -> 0.02 us  [sum_over_devices(): value = value + pair_swap(value, partner)]
  transfers between devices with their start and end apart: 10 -> 10, of which waited for: 7 -> 7; matrix products, arithmetic and copies ran while one was open for 2% -> 3% of each run, Pallas kernels for 16% -> 11%
where the time goes in v2:
time: 32.5 us; the launch traced here: 32.3 us
  waiting for transfers between devices  12.9 us (40%)
  starting transfers between devices  11.8 us (36%)
  Pallas kernels  4.35 us (13%)
  other arithmetic  1.62 us (5%)
  local copies, waits for them, and re-layouts  0.89 us (3%)
  between operations  0.73 us (2%)
    ppermute x10, waiting for transfers between devices, pair_swap(): return lax.ppermute(value, AXES, pairs)  12.9 us
    ppermute x10, starting transfers between devices, pair_swap(): return lax.ppermute(value, AXES, pairs)  11.8 us
    pallas_call x1, Pallas kernels, local(): pl.pallas_call(functools.partial(main_kernel, sizes), out_shape=(jax.Shap...  2.21 us
    pallas_call x1, Pallas kernels, local(): pl.pallas_call(functools.partial(merge_kernel, sizes), out_shape=jax.Shap...  1.29 us
    select_n x1, other arithmetic, local(): jnp.where(x_odd, high, low)  0.94 us
    slice x1, local copies, waits for them, and re-layouts, local(): phi_start[:, rows - TILE:]  0.88 us
  transfers between devices with their start and end apart: 10, of which 7 were waited for; matrix products, arithmetic and copies ran while one was open for 3% of the time, Pallas kernels for 11%

profile of v2, /device:TPU:0, one launch (start us, length us, event | category | flops | bytes accessed | tf_op | source)
XLA Modules:
  0.0 32.3 jit_solution(5244290862485654801)
XLA Ops:
  0.6 0.9 %slice_select_fusion = (f32[3,48,128]{2,1,0:T(8,128)S(1)}, f32[3,48,128]{2,1,0:T(8,128)S(1)}) fusion(f32[16,48,128]{2,1,0:T(8,128)} %b_ref.3, pred[]{:T(512)S(6)} %eq.8), kind=kLoop, calls=%fused_computation.1 | loop fusion | flops 36864 | bytes 294913 | tf_op jit(solution)/shard_map/jit(_where)/select_n | solution.py:338
  1.6 0.6 %collective-permute-start.1 = (f32[3,48,128]{2,1,0:T(8,128)S(1)}, f32[3,48,128]{2,1,0:T(8,128)S(1)}, u32[]{:S(2)}, u32[]{:S(2)}) collective-permute-start(f32[3,48,128]{2,1,0:T(8,128)S(1)} %get-tuple-element.16), channel_id=1, source_target_pairs={{0,4},{1,5},{2,6},{3,7},{4,0},{5,1},{6,2},{7,3},{8,16},{9,17},{10,... | collective-permute-start | bytes 221192 | tf_op jit(solution)/shard_map/ppermute | solution.py:30
  2.1 4.0 %collective-permute-start = (f32[3,48,128]{2,1,0:T(8,128)S(1)}, f32[3,48,128]{2,1,0:T(8,128)S(1)}, u32[]{:S(2)}, u32[]{:S(2)}) collective-permute-start(f32[3,48,128]{2,1,0:T(8,128)S(1)} %get-tuple-element.17), channel_id=1, source_target_pairs={{0,8},{1,9},{2,10},{3,11},{4,12},{5,13},{6,14},{7,15},{8,0},{9,1},... | collective-permute-start | bytes 221192 | tf_op jit(solution)/shard_map/ppermute | solution.py:30
  6.1 0.9 %fusion = (f32[16,8,128]{2,1,0:T(8,128)S(1)}, f32[16,8,128]{2,1,0:T(8,128)S(1)}) fusion(f32[16,48,128]{2,1,0:T(8,128)} %b_ref.3), kind=kLoop, calls=%fused_computation.7 | loop fusion | bytes 262144 | tf_op jit(solution)/shard_map/slice | solution.py:343
  7.0 0.0 copy-start
  7.0 0.0 collective-permute-done.1.xb_ref
  7.0 2.6 %collective-permute-done.xa_ref = f32[3,48,128]{2,1,0:T(8,128)S(1)} collective-permute-done((f32[3,48,128]{2,1,0:T(8,128)S(1)}, f32[3,48,128]{2,1,0:T(8,128)S(1)}, u32[]{:S(2)}, u32[]{:S(2)}) %collective-permute-start) | collective-permute-done | bytes 73760 | tf_op jit(solution)/shard_map/ppermute | solution.py:30
  9.7 0.1 collective-permute-start.2
  9.8 1.3 %collective-permute-done.2.ya_ref.yb_ref = f32[22,8,128]{2,1,0:T(8,128)S(1)} collective-permute-done((f32[22,8,128]{2,1,0:T(8,128)S(1)}, f32[22,8,128]{2,1,0:T(8,128)S(1)}, u32[]{:S(2)}, u32[]{:S(2)}) %collective-permute-start.2) | collective-permute-done | bytes 90144 | tf_op jit(solution)/shard_map/ppermute | solution.py:30
  11.1 0.0 copy-done
  11.1 0.5 %strips.1 = (f32[216,128]{1,0:T(8,128)S(1)}, f32[72,128]{1,0:T(8,128)S(1)}) custom-call(f32[16,48,128]{2,1,0:T(8,128)S(1)} %copy-done, f32[3,48,128]{2,1,0:T(8,128)S(1)} %collective-permute-done.xa_ref, f32[3,48,128]{2,1,0:T(8,128)S(1)} %collective-permute-done.1.xb_ref, f32[22,8,128]{2,1,0:T(8,128)S(1)} %collective-permute-done.2.ya_ref.yb_ref, ...), custom_call_target="tpu_custom_call" | custom-call | flops 3500000 | bytes 1000000 | tf_op jit(solution)/shard_map/strips/pallas_call | solution.py:346
  11.6 0.2 collective-permute-start.4
  11.8 3.0 %collective-permute-start.3 = (f32[72,128]{1,0:T(8,128)S(1)}, f32[72,128]{1,0:T(8,128)S(1)}, u32[]{:S(2)}, u32[]{:S(2)}) collective-permute-start(f32[72,128]{1,0:T(8,128)S(1)} %get-tuple-element.10), channel_id=1, source_target_pairs={{0,1},{1,0},{2,3},{3,2},{4,5},{5,4},{6,7},{7,6},{8,9},{9,8},{10,11... | collective-permute-start | bytes 110600 | tf_op jit(solution)/shard_map/ppermute | solution.py:30
  14.8 2.2 %inner.1 = (f32[16,48,128]{2,1,0:T(8,128)S(1)}, f32[3,8,128]{2,1,0:T(8,128)S(1)}) custom-call(f32[16,48,128]{2,1,0:T(8,128)S(1)} %copy-done, f32[3,48,128]{2,1,0:T(8,128)S(1)} %collective-permute-done.xa_ref, f32[3,48,128]{2,1,0:T(8,128)S(1)} %collective-permute-done.1.xb_ref, f32[22,8,128]{2,1,0:T(8,128)S(1)} %collective-permute-done.2.ya_ref.yb_ref, ...), custom_call_target="tpu_custom_call" | custom-call | flops 10500000 | bytes 1000000 | tf_op jit(solution)/shard_map/inner/pallas_call | solution.py:361
  17.0 0.0 collective-permute-done.4.zb_ref
  17.0 0.0 collective-permute-done.3.za_ref
  17.0 0.3 edges.1
  17.4 0.1 collective-permute-start.5
  17.4 1.2 %collective-permute-done.5 = f32[8,128]{1,0:T(8,128)S(1)} collective-permute-done((f32[8,128]{1,0:T(8,128)S(1)}, f32[8,128]{1,0:T(8,128)S(1)}, u32[]{:S(2)}, u32[]{:S(2)}) %collective-permute-start.5) | collective-permute-done | bytes 4128 | tf_op jit(solution)/shard_map/ppermute | solution.py:30
  18.6 0.6 %collective-permute-start.6 = (f32[8,128]{1,0:T(8,128)S(1)}, f32[8,128]{1,0:T(8,128)S(1)}, u32[]{:S(2)}, u32[]{:S(2)}) collective-permute-start(f32[8,128]{1,0:T(8,128)S(1)} %add.15), channel_id=1, source_target_pairs={{0,12},{1,13},{2,14},{3,15},{4,8},{5,9},{6,10},{7,11},{8,4},{9,5},... | collective-permute-start | bytes 12296 | tf_op jit(solution)/shard_map/ppermute | solution.py:30
  19.2 2.5 %collective-permute-done.6 = f32[8,128]{1,0:T(8,128)S(1)} collective-permute-done((f32[8,128]{1,0:T(8,128)S(1)}, f32[8,128]{1,0:T(8,128)S(1)}, u32[]{:S(2)}, u32[]{:S(2)}) %collective-permute-start.6) | collective-permute-done | bytes 4128 | tf_op jit(solution)/shard_map/ppermute | solution.py:30
  21.6 0.5 %collective-permute-start.7 = (f32[8,128]{1,0:T(8,128)S(1)}, f32[8,128]{1,0:T(8,128)S(1)}, u32[]{:S(2)}, u32[]{:S(2)}) collective-permute-start(f32[8,128]{1,0:T(8,128)S(1)} %add.16), channel_id=1, source_target_pairs={{0,20},{1,21},{2,22},{3,23},{4,16},{5,17},{6,18},{7,19},{8,28},{9,... | collective-permute-start | bytes 12296 | tf_op jit(solution)/shard_map/ppermute | solution.py:30
  22.2 2.5 %collective-permute-done.7 = f32[8,128]{1,0:T(8,128)S(1)} collective-permute-done((f32[8,128]{1,0:T(8,128)S(1)}, f32[8,128]{1,0:T(8,128)S(1)}, u32[]{:S(2)}, u32[]{:S(2)}) %collective-permute-start.7) | collective-permute-done | bytes 4128 | tf_op jit(solution)/shard_map/ppermute | solution.py:30
  24.7 1.5 %collective-permute-start.8 = (f32[8,128]{1,0:T(8,128)S(1)}, f32[8,128]{1,0:T(8,128)S(1)}, u32[]{:S(2)}, u32[]{:S(2)}) collective-permute-start(f32[8,128]{1,0:T(8,128)S(1)} %add.17), channel_id=1, source_target_pairs={{0,5},{1,4},{2,7},{3,6},{4,1},{5,0},{6,3},{7,2},{8,13},{9,12},{10,... | collective-permute-start | bytes 12296 | tf_op jit(solution)/shard_map/ppermute | solution.py:30
  26.2 1.5 %collective-permute-done.8 = f32[8,128]{1,0:T(8,128)S(1)} collective-permute-done((f32[8,128]{1,0:T(8,128)S(1)}, f32[8,128]{1,0:T(8,128)S(1)}, u32[]{:S(2)}, u32[]{:S(2)}) %collective-permute-start.8) | collective-permute-done | bytes 4128 | tf_op jit(solution)/shard_map/ppermute | solution.py:30
  27.7 1.4 %collective-permute-start.9 = (f32[8,128]{1,0:T(8,128)S(1)}, f32[8,128]{1,0:T(8,128)S(1)}, u32[]{:S(2)}, u32[]{:S(2)}) collective-permute-start(f32[8,128]{1,0:T(8,128)S(1)} %add.18), channel_id=1, source_target_pairs={{0,6},{1,7},{2,4},{3,5},{4,2},{5,3},{6,0},{7,1},{8,14},{9,15},{10,... | collective-permute-start | bytes 12296 | tf_op jit(solution)/shard_map/ppermute | solution.py:30
  29.1 1.3 %merge.1 = f32[16,48,128]{2,1,0:T(8,128)} custom-call(f32[16,48,128]{2,1,0:T(8,128)S(1)} %get-tuple-element.8.main_ref, f32[72,128]{1,0:T(8,128)S(1)} %get-tuple-element.12.edge_ref), custom_call_target="tpu_custom_call" | custom-call | flops 3500000 | bytes 1000000 | tf_op jit(solution)/shard_map/merge/pallas_call | solution.py:388
  30.4 1.3 %collective-permute-done.9 = f32[8,128]{1,0:T(8,128)S(1)} collective-permute-done((f32[8,128]{1,0:T(8,128)S(1)}, f32[8,128]{1,0:T(8,128)S(1)}, u32[]{:S(2)}, u32[]{:S(2)}) %collective-permute-start.9) | collective-permute-done | bytes 4128 | tf_op jit(solution)/shard_map/ppermute | solution.py:30
  31.6 0.1 slice_reduce_fusion
  31.8 0.5 %sqrt_multiply_fusion = f32[3]{0:T(128)} fusion(f32[3]{0:T(128)S(1)} %slice_reduce_fusion), kind=kLoop, calls=%fused_computation.6 | loop fusion | flops 6 | bytes 24 | tf_op jit(solution)/shard_map/div | solution.py:402
  (8 shorter events, 0.1 us)
Async XLA Ops:
  1.6 5.4 %collective-permute-start.1 = (f32[3,48,128]{2,1,0:T(8,128)S(1)}, f32[3,48,128]{2,1,0:T(8,128)S(1)}, u32[]{:S(2)}, u32[]{:S(2)}) collective-permute-start(f32[3,48,128]{2,1,0:T(8,128)S(1)} %get-tuple-element.16), channel_id=1, source_target_pairs={{0,4},{1,5},{2,6},{3,7},{4,0},{5,1},{6,2},{7,3},{8,16},{9,17},{10,... | collective-permute-start | bytes 221192 | tf_op jit(solution)/shard_map/ppermute | solution.py:30
  2.1 7.5 %collective-permute-start = (f32[3,48,128]{2,1,0:T(8,128)S(1)}, f32[3,48,128]{2,1,0:T(8,128)S(1)}, u32[]{:S(2)}, u32[]{:S(2)}) collective-permute-start(f32[3,48,128]{2,1,0:T(8,128)S(1)} %get-tuple-element.17), channel_id=1, source_target_pairs={{0,8},{1,9},{2,10},{3,11},{4,12},{5,13},{6,14},{7,15},{8,0},{9,1},... | collective-permute-start | bytes 221192 | tf_op jit(solution)/shard_map/ppermute | solution.py:30
  7.0 4.1 %copy-start = (f32[16,48,128]{2,1,0:T(8,128)S(1)}, f32[16,48,128]{2,1,0:T(8,128)}, u32[]{:S(2)}) copy-start(f32[16,48,128]{2,1,0:T(8,128)} %b_ref.3) | copy-start | bytes 1179652
  9.7 1.4 %collective-permute-start.2 = (f32[22,8,128]{2,1,0:T(8,128)S(1)}, f32[22,8,128]{2,1,0:T(8,128)S(1)}, u32[]{:S(2)}, u32[]{:S(2)}) collective-permute-start(f32[22,8,128]{2,1,0:T(8,128)S(1)} %maximum_select_fusion), channel_id=1, source_target_pairs={{0,4},{1,5},{2,6},{3,7},{4,0},{5,1},{6,2},{7,3},{8,12},{9,13},{10,... | collective-permute-start | bytes 270344 | tf_op jit(solution)/shard_map/ppermute | solution.py:30
  11.6 5.4 %collective-permute-start.4 = (f32[72,128]{1,0:T(8,128)S(1)}, f32[72,128]{1,0:T(8,128)S(1)}, u32[]{:S(2)}, u32[]{:S(2)}) collective-permute-start(f32[72,128]{1,0:T(8,128)S(1)} %get-tuple-element.10), channel_id=1, source_target_pairs={{0,4},{1,2},{2,1},{3,7},{4,0},{5,6},{6,5},{7,3},{8,12},{9,10},{10,... | collective-permute-start | bytes 110600 | tf_op jit(solution)/shard_map/ppermute | solution.py:30
  11.8 5.2 %collective-permute-start.3 = (f32[72,128]{1,0:T(8,128)S(1)}, f32[72,128]{1,0:T(8,128)S(1)}, u32[]{:S(2)}, u32[]{:S(2)}) collective-permute-start(f32[72,128]{1,0:T(8,128)S(1)} %get-tuple-element.10), channel_id=1, source_target_pairs={{0,1},{1,0},{2,3},{3,2},{4,5},{5,4},{6,7},{7,6},{8,9},{9,8},{10,11... | collective-permute-start | bytes 110600 | tf_op jit(solution)/shard_map/ppermute | solution.py:30
  17.4 1.2 %collective-permute-start.5 = (f32[8,128]{1,0:T(8,128)S(1)}, f32[8,128]{1,0:T(8,128)S(1)}, u32[]{:S(2)}, u32[]{:S(2)}) collective-permute-start(f32[8,128]{1,0:T(8,128)S(1)} %get-tuple-element.13), channel_id=1, source_target_pairs={{0,4},{1,5},{2,6},{3,7},{4,0},{5,1},{6,2},{7,3},{8,12},{9,13},{10,... | collective-permute-start | bytes 12296 | tf_op jit(solution)/shard_map/ppermute | solution.py:30
  18.6 3.0 %collective-permute-start.6 = (f32[8,128]{1,0:T(8,128)S(1)}, f32[8,128]{1,0:T(8,128)S(1)}, u32[]{:S(2)}, u32[]{:S(2)}) collective-permute-start(f32[8,128]{1,0:T(8,128)S(1)} %add.15), channel_id=1, source_target_pairs={{0,12},{1,13},{2,14},{3,15},{4,8},{5,9},{6,10},{7,11},{8,4},{9,5},... | collective-permute-start | bytes 12296 | tf_op jit(solution)/shard_map/ppermute | solution.py:30
  21.6 3.0 %collective-permute-start.7 = (f32[8,128]{1,0:T(8,128)S(1)}, f32[8,128]{1,0:T(8,128)S(1)}, u32[]{:S(2)}, u32[]{:S(2)}) collective-permute-start(f32[8,128]{1,0:T(8,128)S(1)} %add.16), channel_id=1, source_target_pairs={{0,20},{1,21},{2,22},{3,23},{4,16},{5,17},{6,18},{7,19},{8,28},{9,... | collective-permute-start | bytes 12296 | tf_op jit(solution)/shard_map/ppermute | solution.py:30
  24.7 3.0 %collective-permute-start.8 = (f32[8,128]{1,0:T(8,128)S(1)}, f32[8,128]{1,0:T(8,128)S(1)}, u32[]{:S(2)}, u32[]{:S(2)}) collective-permute-start(f32[8,128]{1,0:T(8,128)S(1)} %add.17), channel_id=1, source_target_pairs={{0,5},{1,4},{2,7},{3,6},{4,1},{5,0},{6,3},{7,2},{8,13},{9,12},{10,... | collective-permute-start | bytes 12296 | tf_op jit(solution)/shard_map/ppermute | solution.py:30
  27.7 3.9 %collective-permute-start.9 = (f32[8,128]{1,0:T(8,128)S(1)}, f32[8,128]{1,0:T(8,128)S(1)}, u32[]{:S(2)}, u32[]{:S(2)}) collective-permute-start(f32[8,128]{1,0:T(8,128)S(1)} %add.18), channel_id=1, source_target_pairs={{0,6},{1,7},{2,4},{3,5},{4,2},{5,3},{6,0},{7,1},{8,14},{9,15},{10,... | collective-permute-start | bytes 12296 | tf_op jit(solution)/shard_map/ppermute | solution.py:30

commit v3 on v1

v3 whole, which is shorter than its diff:
```python
import functools

import jax
import jax.numpy as jnp
from jax import lax
from jax.experimental import pallas as pl
from jax.experimental.pallas import tpu as pltpu
from jax.sharding import PartitionSpec as P

ITERS = 3
HALO = ITERS
AXES = ("gx", "gy", "gz")
TILE = 8
HALF = 64

pseudo_step = 0.45


def pair_swap(value, partner):
    sizes = [lax.axis_size(a) for a in AXES]

    def flat(place):
        return (place[0] * sizes[1] + place[1]) * sizes[2] + place[2]

    pairs = []
    for i in range(sizes[0]):
        for j in range(sizes[1]):
            for k in range(sizes[2]):
                pairs.append((flat((i, j, k)), flat(partner((i, j, k)))))
    return lax.ppermute(value, AXES, pairs)


def neighbour(dim, colour, cross):
    sizes = [lax.axis_size(a) for a in AXES]

    def partner(place):
        place = list(place)
        here = place[dim]
        there = here ^ 1 if colour == 0 else ((here - 1) ^ 1) + 1
        if 0 <= there < sizes[dim]:
            place[dim] = there
            if cross:
                place[1] ^= 1
        elif dim != 1 and sizes[1] % 2 == 0:
            place[1] ^= 1
        elif colour == 1 and sizes[dim] % 2 == 0:
            place[dim] = sizes[dim] - 1 - here
        return tuple(place)

    return partner


def exchange(value_even, value_odd, dim, cross=False):
    first = pair_swap(value_even, neighbour(dim, 0, cross))
    if lax.axis_size(AXES[dim]) == 2:
        return first, first
    return first, pair_swap(value_odd, neighbour(dim, 1, cross))


def other_row(place):
    return (place[0], place[1] ^ 1, place[2])


def sum_over_devices(value):
    sizes = [lax.axis_size(a) for a in AXES]
    if any(n & (n - 1) for n in sizes):
        return lax.psum(value, AXES)
    rounds = []
    for dim in (1, 0, 2):
        bit = 1
        while bit < sizes[dim]:
            rounds.append((dim, bit))
            bit *= 2
    crossed = False
    for dim, bit in rounds:

        def partner(place, dim=dim, bit=bit, flip=crossed):
            place = list(place)
            place[dim] ^= bit
            if flip:
                place[1] ^= 1
            return tuple(place)

        value = value + pair_swap(value, partner)
        crossed = crossed or (dim, bit) == (1, 1)
    return value


def at_ends(axis):
    place = lax.axis_index(axis)
    return place == 0, place == lax.axis_size(axis) - 1


def odd(axis):
    return lax.rem(lax.axis_index(axis), 2) == 1


def low_high(first, second, axis):
    is_odd = odd(axis)
    return jnp.where(is_odd, first, second), jnp.where(is_odd, second, first)


def sign_factors(field):
    sgn = field * lax.rsqrt(field * field + 1.0)
    return jnp.where(field > 0.0, 1.0, -1.0), pseudo_step * sgn


def upwind(sc, s, prev, nxt):
    term = jnp.maximum(sc - jnp.minimum(s * prev, s * nxt), 0.0)
    return term * term


def stepped(c, k, total):
    root = total * lax.rsqrt(jnp.maximum(total, 1e-30))
    return c - k * (root - 1.0)


def faces_kernel(sizes, b_ref, *outs):
    planes, rows, _ = sizes
    x_odd, y_odd = odd("gx"), odd("gy")
    for n, ref in enumerate(outs[:2]):
        low = x_odd if n == 0 else ~x_odd
        ref[...] = b_ref[pl.ds(jnp.where(low, 0, planes - HALO), HALO)]
    for n, ref in enumerate(outs[2:]):
        low = y_odd if n == 0 else ~y_odd
        start = pl.multiple_of(jnp.where(low, 0, rows - TILE), TILE)
        ref[...] = b_ref[:, pl.ds(start, TILE)]


def plane_step(c, s, k, before, after, marks):
    sub, y_first, y_last, rows = marks
    tall, lanes = c.shape
    edge = c[rows:tall]
    edge = jnp.where((sub == TILE - 1) & y_first, c[0:1], edge)
    edge = jnp.where((sub == 0) & y_last, c[rows - 1 : rows], edge)
    around = jnp.concatenate([c[0:rows], edge], axis=0)
    sc = s * c
    total = upwind(sc, s, before, after)
    total = total + upwind(sc, s, pltpu.roll(around, 1, 0), pltpu.roll(around, tall - 1, 0))
    total = total + upwind(sc, s, pltpu.roll(c, 1, 1), pltpu.roll(c, lanes - 1, 1))
    new = stepped(c, k, total)
    change = new[0:rows] - c[0:rows]
    change = change * change
    part = change[0:TILE]
    for t in range(TILE, rows, TILE):
        part = part + change[t : t + TILE]
    return new, part


def plane_marks(sizes):
    _, rows, lanes = sizes
    y_first, y_last = at_ends("gy")
    return lax.broadcasted_iota(jnp.int32, (TILE, lanes), 0), y_first, y_last, rows


def turned_lines(own, mix, lanes):
    turned = jnp.concatenate([mix, own, mix], axis=0).T
    return jnp.concatenate([turned[0:TILE], turned[lanes - TILE : lanes]], axis=1)


def middle(lines_ref, i, pitch, near):
    low = lines_ref[i * pitch : (i + 1) * pitch]
    shift = TILE - HALO
    return jnp.where(near, low, lines_ref[(i + shift) * pitch : (i + shift + 1) * pitch])


def pre_kernel(
    sizes, b_ref, mix_ref, e1_ref, e2_ref, out_ref, s_ref, k_ref, acc_ref, lines_ref, mid_ref, e0
):
    planes, rows, lanes = sizes
    pitch = lines_ref.shape[0] // TILE
    marks = plane_marks(sizes)
    lane = lax.broadcasted_iota(jnp.int32, (TILE, lanes), 1)
    near = lax.broadcasted_iota(jnp.int32, (pitch, 2 * HALF), 1) < HALF

    for p in range(planes):
        own, mix = b_ref[p], mix_ref[p]
        lines_ref[pl.ds(p + HALO, TILE, stride=pitch)] = turned_lines(own, mix, lanes)
        full = jnp.concatenate([own, mix], axis=0)
        e0[p] = full
        s_ref[p], k_ref[p] = sign_factors(full)
    for i in range(HALO):
        mid_ref[i * pitch : (i + 1) * pitch] = middle(lines_ref, i, pitch, near)

    inner = (lane >= HALO) & (lane < lanes - HALO)
    bufs = (e0, e1_ref, e2_ref)
    for it in range(ITERS):

        def body(p, acc, it=it):
            src = bufs[it]
            new, part = plane_step(src[p], s_ref[p], k_ref[p], src[p - 1], src[p + 1], marks)
            if it == ITERS - 1:
                out_ref[p] = new[0:rows]
            else:
                bufs[it + 1][p] = new
            return acc + part

        acc = jnp.zeros((TILE, lanes), jnp.float32)
        acc = lax.fori_loop(it + 1, planes - 1 - it, body, acc, unroll=(7, 6, 5)[it])
        acc_ref[it] = jnp.where(inner, acc, 0.0)


def ends_kernel(sizes, cross, *refs):
    planes, rows, lanes = sizes
    lines_ref, halo_ref, mix_ref = refs[:3]
    if cross:
        mid_ref, held_ref, held_mix_ref = refs[3:6]
    strip_ref, send_ref, lines, given = refs[-4:]
    pitch = lines_ref.shape[0] // TILE
    near = lax.broadcasted_iota(jnp.int32, (pitch, 2 * HALF), 1) < HALF
    lines[...] = lines_ref[...]
    for i in range(2 * HALO):
        x = i if i < HALO else i + planes
        lines[pl.ds(x, TILE, stride=pitch)] = turned_lines(halo_ref[i], mix_ref[i], lanes)
        if cross:
            given[pl.ds(x, TILE, stride=pitch)] = turned_lines(
                held_ref[i], held_mix_ref[i], lanes
            )
    shift = TILE - 2 * HALO
    for j in range(3 * HALO):
        if j < HALO:
            value = lines[(j + shift) * pitch : (j + shift + 1) * pitch]
        elif j >= 2 * HALO:
            value = lines[(j - HALO) * pitch : (j - HALO + 1) * pitch]
        else:
            value = middle(lines, j - HALO, pitch, near)
        strip_ref[j * pitch : (j + 1) * pitch] = value
        i = j - HALO
        if 0 <= i < HALO:
            if cross:
                line = lax.broadcasted_iota(jnp.int32, (pitch, 2 * HALF), 0)
                theirs = (line >= HALO) & (line < HALO + planes)
                value = jnp.where(
                    theirs, mid_ref[i * pitch : (i + 1) * pitch], middle(given, i, pitch, near)
                )
            send_ref[i * pitch : (i + 1) * pitch] = value


def post_kernel(
    sizes,
    b_ref,
    mix_ref,
    halo_ref,
    halo_mix_ref,
    e1_ref,
    e2_ref,
    s_ref,
    k_ref,
    pre_acc_ref,
    out_ref,
    acc_ref,
    f1,
    f2,
):
    planes, rows, lanes = sizes
    x_first, x_last = at_ends("gx")
    marks = plane_marks(sizes)
    lane = lax.broadcasted_iota(jnp.int32, (TILE, lanes), 1)
    inner = (lane >= HALO) & (lane < lanes - HALO)
    factors = {}

    def start(p):
        if 0 <= p < planes:
            return jnp.concatenate([b_ref[p], mix_ref[p]], axis=0)
        i = p + HALO if p < 0 else p - planes + HALO
        return jnp.concatenate([halo_ref[i], halo_mix_ref[i]], axis=0)

    def factor(p):
        if 0 <= p < planes:
            return s_ref[p], k_ref[p]
        if p not in factors:
            factors[p] = sign_factors(start(p))
        return factors[p]

    def get(it, p):
        if it == 0:
            return start(p)
        if it <= p < planes - it:
            return (e1_ref, e2_ref)[it - 1][p]
        return (f1, f2)[it - 1][p + HALO if p < planes // 2 else p - planes + 3 * HALO]

    for it in range(ITERS):
        acc = jnp.zeros((TILE, lanes), jnp.float32)
        lows = range(it + 1 - HALO, it + 1)
        for p in (*lows, *(planes - 1 - p for p in lows)):
            c = get(it, p)
            before, after = get(it, p - 1), get(it, p + 1)
            if p == 0:
                before = jnp.where(x_first, c, before)
            if p == planes - 1:
                after = jnp.where(x_last, c, after)
            s, k = factor(p)
            new, part = plane_step(c, s, k, before, after, marks)
            if it == ITERS - 1:
                out_ref[p if p < HALO else p - planes + 2 * HALO] = new[0:rows]
            else:
                (f1, f2)[it][p + HALO if p < planes // 2 else p - planes + 3 * HALO] = new
            if 0 <= p < planes:
                acc = acc + part
        acc_ref[it] = pre_acc_ref[it] + jnp.where(inner, acc, 0.0)


def edge_kernel(sizes, strip_ref, za_ref, zb_ref, acc_ref, out_ref, sum_ref):
    planes, rows, lanes = sizes
    pitch = strip_ref.shape[0] // (3 * HALO)
    x_first, x_last = at_ends("gx")
    y_first, y_last = at_ends("gy")
    z_first, z_last = at_ends("gz")
    shape = (pitch, 2 * HALF)
    line = lax.broadcasted_iota(jnp.int32, shape, 0)
    lane = lax.broadcasted_iota(jnp.int32, shape, 1)
    near = lane < HALF
    y = jnp.where(near, lane, lane - HALF) - TILE
    x = line - HALO
    low_x = (x == 0) & x_first
    high_x = (x == planes - 1) & x_last
    low_y = (y == 0) & y_first
    high_y = (y == rows - 1) & y_last
    low_z = near & z_first
    high_z = (lane >= HALF) & z_last
    mine = (x >= 0) & (x < planes) & (y >= 0) & (y < rows)

    state = []
    for j in range(3 * HALO):
        own = strip_ref[j * pitch : (j + 1) * pitch]
        if j < HALO:
            got = low_high(
                za_ref[j * pitch : (j + 1) * pitch], zb_ref[j * pitch : (j + 1) * pitch], "gz"
            )[0]
            own = jnp.where(near, pltpu.roll(got, HALF, 1), own)
        elif j >= 2 * HALO:
            i = j - 2 * HALO
            got = low_high(
                za_ref[i * pitch : (i + 1) * pitch], zb_ref[i * pitch : (i + 1) * pitch], "gz"
            )[1]
            own = jnp.where(near, own, pltpu.roll(got, HALF, 1))
        state.append(own)
    factors = [sign_factors(v) for v in state]

    sums = []
    for it in range(ITERS):
        new = list(state)
        change = jnp.zeros(shape, jnp.float32)
        for j in range(it + 1, 3 * HALO - 1 - it):
            c = state[j]
            s, k = factors[j]
            sc = s * c
            total = upwind(
                sc,
                s,
                jnp.where(low_x, c, pltpu.roll(c, 1, 0)),
                jnp.where(high_x, c, pltpu.roll(c, pitch - 1, 0)),
            )
            total = total + upwind(
                sc,
                s,
                jnp.where(low_y, c, pltpu.roll(c, 1, 1)),
                jnp.where(high_y, c, pltpu.roll(c, 2 * HALF - 1, 1)),
            )
            before, after = state[j - 1], state[j + 1]
            if j == HALO:
                before = jnp.where(low_z, c, before)
            if j == 2 * HALO - 1:
                after = jnp.where(high_z, c, after)
            total = total + upwind(sc, s, before, after)
            new[j] = stepped(c, k, total)
            if HALO <= j < 2 * HALO:
                change = change + (new[j] - c) * (new[j] - c)
        state = new
        change = jnp.where(mine, change, 0.0)
        part = acc_ref[it]
        for t in range(0, pitch, TILE):
            part = part + change[t : t + TILE]
        sums.append(jnp.sum(part, axis=0, keepdims=True))
    for i in range(HALO):
        out_ref[i * pitch : (i + 1) * pitch] = state[HALO + i]
    sums.append(jnp.zeros((TILE - ITERS, 2 * HALF), jnp.float32))
    sum_ref[...] = jnp.concatenate(sums, axis=0)


def merge_kernel(sizes, main_ref, ends_ref, edge_ref, out_ref):
    planes, rows, lanes = sizes
    pitch = edge_ref.shape[0] // HALO
    lane = lax.broadcasted_iota(jnp.int32, (rows, lanes), 1)
    for x in range(planes):
        lines = edge_ref[pl.ds(x + HALO, HALO, stride=pitch)]
        lines = jnp.concatenate(
            [lines, jnp.zeros((lanes - HALO, 2 * HALF), jnp.float32)], axis=0
        )
        turned = lines.T
        near = turned[TILE : TILE + rows]
        far = pltpu.roll(turned[HALF + TILE : HALF + TILE + rows], lanes - HALO, 1)
        if x < HALO:
            main = ends_ref[x]
        elif x >= planes - HALO:
            main = ends_ref[x - planes + 2 * HALO]
        else:
            main = main_ref[x]
        value = jnp.where(lane < HALO, near, main)
        out_ref[x] = jnp.where(lane >= lanes - HALO, far, value)


def vmem(n):
    return [pl.BlockSpec(memory_space=pltpu.VMEM)] * n


def grant(mib):
    return pltpu.CompilerParams(vmem_limit_bytes=mib * 2**20)


def cost(us, nbytes):
    return pl.CostEstimate(flops=int(us * 3.5e6), bytes_accessed=nbytes, transcendentals=0)


def call(kernel, sizes, inputs, outputs, scratch, mib, us, name):
    return pl.pallas_call(
        functools.partial(kernel, sizes),
        out_shape=tuple(jax.ShapeDtypeStruct(o, jnp.float32) for o in outputs),
        in_specs=vmem(len(inputs)),
        out_specs=tuple(vmem(len(outputs))),
        scratch_shapes=[pltpu.VMEM(t, jnp.float32) for t in scratch],
        compiler_params=grant(mib),
        cost_estimate=cost(us, 10**6),
        name=name,
    )(*inputs)


def local(phi_start):
    sizes = phi_start.shape
    planes, rows, lanes = sizes
    wide = planes + 2 * HALO
    tall = rows + TILE
    pitch = -(-wide // TILE) * TILE
    cross = lax.axis_size("gy") == 2
    y_odd = odd("gy")

    def mixed(first, second):
        if first is second:
            return first
        low, high = low_high(first, second, "gy")
        sub = lax.broadcasted_iota(jnp.int32, first.shape, 1)
        return jnp.where(sub < TILE // 2, high, low)

    face, tile = (HALO, rows, lanes), (planes, TILE, lanes)
    xs_even, xs_odd, *ys = call(
        faces_kernel,
        sizes,
        (phi_start,),
        (face, face, tile) if cross else (face, face, tile, tile),
        (),
        2,
        0.5,
        "faces",
    )

    xa, xb = exchange(xs_even, xs_odd, 0, cross)
    mix = mixed(*exchange(ys[0], ys[-1], 1))

    block = (planes, tall, lanes)
    e1, e2, inner, s, k, acc, lines, mid = call(
        pre_kernel,
        sizes,
        (phi_start, mix),
        (block, block, sizes, block, block, (ITERS, TILE, lanes))
        + ((TILE * pitch, 2 * HALF), (HALO * pitch, 2 * HALF)),
        (block,),
        8,
        2,
        "pre",
    )

    halo = jnp.concatenate(low_high(xa, xb, "gx"), axis=0)
    first_rows, last_rows = slice(0, TILE), slice(rows - TILE, rows)
    if cross:
        held = halo
        flat = held.reshape(2 * HALO * rows, lanes)
        swapped = pair_swap(jnp.concatenate([flat, mid], axis=0), other_row)
        halo = swapped[: 2 * HALO * rows].reshape(held.shape)
        mid = swapped[2 * HALO * rows :]
        halo_mix = jnp.where(y_odd, held[:, last_rows], held[:, first_rows])
        held_mix = jnp.where(y_odd, halo[:, first_rows], halo[:, last_rows])
        given = (mid, held, held_mix)
    else:
        top, tail = halo[:, first_rows], halo[:, last_rows]
        halo_mix = mixed(
            *exchange(jnp.where(y_odd, top, tail), jnp.where(y_odd, tail, top), 1)
        )
        given = ()

    strip, send = call(
        lambda sizes, *refs: ends_kernel(sizes, cross, *refs),
        sizes,
        (lines, halo, halo_mix, *given),
        ((3 * HALO * pitch, 2 * HALF), (HALO * pitch, 2 * HALF)),
        ((TILE * pitch, 2 * HALF),) * 2,
        4,
        0.5,
        "ends",
    )
    za, zb = exchange(send, send, 2, cross)

    tips, acc = call(
        post_kernel,
        sizes,
        (phi_start, mix, halo, halo_mix, e1, e2, s, k, acc),
        ((2 * HALO, rows, lanes), (ITERS, TILE, lanes)),
        ((4 * HALO, tall, lanes),) * 2,
        8,
        2,
        "post",
    )

    edge, sums = call(
        edge_kernel,
        sizes,
        (strip, za, zb, acc),
        ((HALO * pitch, 2 * HALF), (TILE, 2 * HALF)),
        (),
        4,
        0.5,
        "edges",
    )

    (phi_final,) = call(
        merge_kernel, sizes, (inner, tips, edge), (sizes,), (), 4, 1.5, "merge"
    )

    totals = jnp.sum(sum_over_devices(sums)[:ITERS], axis=1)
    cells = planes * rows * lanes
    for axis in AXES:
        cells = cells * lax.axis_size(axis)
    residuals = jnp.sqrt(totals / jnp.float32(cells)) / pseudo_step
    return (phi_final, residuals)


def solution(mesh):
    return jax.shard_map(
        local,
        mesh=mesh,
        in_specs=(P("gx", "gy", "gz"),),
        out_specs=(P("gx", "gy", "gz"), P()),
        check_vma=False,
    )
```

time: 40.4 us -> 31.8 us (0.79)
  Pallas kernels: 10.5 us -> 4.19 us
  starting transfers between devices: 9.77 us -> 14.2 us
  waiting for transfers between devices: 14 us -> 10.8 us
  local copies, waits for them, and re-layouts: 2.73 us -> 1.01 us
  other arithmetic: 2.31 us -> 0.72 us
    pallas_call x4 -> x6, Pallas kernels: 10.5 us -> 4.19 us  [call(): pl.pallas_call(functools.partial(kernel, sizes), out_shape=tuple((jax.Sha...]
    ppermute x10 -> x11, starting transfers between devices: 9.77 us -> 14.2 us  [pair_swap(): return lax.ppermute(value, AXES, pairs)]
    ppermute x10 -> x11, waiting for transfers between devices: 14 us -> 10.8 us  [pair_swap(): return lax.ppermute(value, AXES, pairs)]
    select_n x2, other arithmetic: 0.95 us -> 0.01 us  [the longest x1 0.01 us: local(): held_mix = jnp.where(y_odd, halo[:, first_rows], halo[:, last_rows])]
    slice x2, local copies, waits for them, and re-layouts: 0.89 us -> 0.02 us  [the longest x1 0.01 us: local(): halo = swapped[:2 * HALO * rows].reshape(held.shape)]
    unnamed x10 -> x4, local copies, waits for them, and re-layouts: 1.84 us -> 0.99 us
    add x5, other arithmetic: 0.7 us -> 0.02 us  [sum_over_devices(): value = value + pair_swap(value, partner)]
  transfers between devices with their start and end apart: 10 -> 11, of which waited for: 7 -> 8; matrix products, arithmetic and copies ran while one was open for 2% -> 0% of each run, Pallas kernels for 16% -> 11%
where the time goes in v3:
time: 31.8 us; the launch traced here: 31.6 us
  starting transfers between devices  14.2 us (45%)
  waiting for transfers between devices  10.8 us (34%)
  Pallas kernels  4.19 us (13%)
  local copies, waits for them, and re-layouts  1.01 us (3%)
  between operations  0.73 us (2%)
  other arithmetic  0.72 us (2%)
    ppermute x11, starting transfers between devices, pair_swap(): return lax.ppermute(value, AXES, pairs)  14.2 us
    ppermute x11, waiting for transfers between devices, pair_swap(): return lax.ppermute(value, AXES, pairs)  10.8 us
    pallas_call x6, Pallas kernels, call(): pl.pallas_call(functools.partial(kernel, sizes), out_shape=tuple((jax.Sha...  4.19 us
    unnamed x4, local copies, waits for them, and re-layouts  0.99 us
  transfers between devices with their start and end apart: 11, of which 8 were waited for; matrix products, arithmetic and copies ran while one was open for 0% of the time, Pallas kernels for 11%

profile of v3, /device:TPU:0, one launch (start us, length us, event | category | flops | bytes accessed | tf_op | source)
XLA Modules:
  0.0 31.6 jit_solution(1592079651359670190)
XLA Ops:
  0.6 0.0 copy-start
  0.6 1.0 %copy-done = f32[16,48,128]{2,1,0:T(8,128)S(1)} copy-done((f32[16,48,128]{2,1,0:T(8,128)S(1)}, f32[16,48,128]{2,1,0:T(8,128)}, u32[]{:S(2)}) %copy-start) | copy-done | bytes 393240
  1.6 2.5 %collective-permute-start.1 = (f32[3,48,128]{2,1,0:T(8,128)S(1)}, f32[3,48,128]{2,1,0:T(8,128)S(1)}, u32[]{:S(2)}, u32[]{:S(2)}) collective-permute-start(f32[3,48,128]{2,1,0:T(8,128)S(1)} %get-tuple-element.21), channel_id=1, source_target_pairs={{0,12},{1,13},{2,14},{3,15},{4,8},{5,9},{6,10},{7,11},{8,4},{9,5},... | collective-permute-start | bytes 221192 | tf_op jit(solution)/shard_map/ppermute | solution.py:30
  4.1 0.7 %collective-permute-start.2 = (f32[3,48,128]{2,1,0:T(8,128)S(1)}, f32[3,48,128]{2,1,0:T(8,128)S(1)}, u32[]{:S(2)}, u32[]{:S(2)}) collective-permute-start(f32[3,48,128]{2,1,0:T(8,128)S(1)} %get-tuple-element.22), channel_id=1, source_target_pairs={{0,4},{1,5},{2,6},{3,7},{4,0},{5,1},{6,2},{7,3},{8,20},{9,21},{10,... | collective-permute-start | bytes 221192 | tf_op jit(solution)/shard_map/ppermute | solution.py:30
  4.8 0.0 collective-permute-start
  4.8 1.3 %collective-permute-done.mix_ref = f32[16,8,128]{2,1,0:T(8,128)S(1)} collective-permute-done((f32[16,8,128]{2,1,0:T(8,128)S(1)}, f32[16,8,128]{2,1,0:T(8,128)S(1)}, u32[]{:S(2)}, u32[]{:S(2)}) %collective-permute-start) | collective-permute-done | bytes 65568 | tf_op jit(solution)/shard_map/ppermute | solution.py:30
  6.0 0.0 copy-done.1
  6.1 1.6 %pre.1 = (f32[16,56,128]{2,1,0:T(8,128)S(1)}, f32[16,56,128]{2,1,0:T(8,128)S(1)}, f32[16,48,128]{2,1,0:T(8,128)S(1)}, f32[16,56,128]{2,1,0:T(8,128)S(1)}, f32[16...) custom-call(f32[16,48,128]{2,1,0:T(8,128)S(1)} %copy-done.1, ...), custom_call_target="tpu_custom_call" | custom-call | flops 7000000 | bytes 1000000 | tf_op jit(solution)/shard_map/pre/pallas_call | solution.py:416
  7.7 0.0 collective-permute-done.1
  7.7 0.0 collective-permute-done.2
  7.8 0.2 collective-permute-start.3
  8.0 1.3 %collective-permute-done.3 = f32[360,128]{1,0:T(8,128)S(1)} collective-permute-done((f32[360,128]{1,0:T(8,128)S(1)}, f32[360,128]{1,0:T(8,128)S(1)}, u32[]{:S(2)}, u32[]{:S(2)}) %collective-permute-start.3) | collective-permute-done | bytes 184352 | tf_op jit(solution)/shard_map/ppermute | solution.py:30
  9.3 0.3 %ends.1 = (f32[216,128]{1,0:T(8,128)S(1)}, f32[72,128]{1,0:T(8,128)S(1)}) custom-call(f32[192,128]{1,0:T(8,128)S(1)} %get-tuple-element.30.refs_0_, f32[6,48,128]{2,1,0:T(8,128)S(1)} %bitcast.3, f32[6,8,128]{2,1,0:T(8,128)S(1)} %fusion.1.halo_mix_ref.refs_2_, f32[72,128]{1,0:T(8,128)S(1)} %slice.33.refs_3_, f32[6,48,128]{2,1,0:T(8,128)S(1)} %pad_maximum_fusion.refs_4_, ...), custom_call_target="tpu_custom_call" | custom-call | flops 1750000 | bytes 1000000 | tf_op jit(solution)/shard_map/ends/pallas_call | solution.py:416
  9.7 0.2 collective-permute-start.5
  9.9 2.7 %collective-permute-start.4 = (f32[72,128]{1,0:T(8,128)S(1)}, f32[72,128]{1,0:T(8,128)S(1)}, u32[]{:S(2)}, u32[]{:S(2)}) collective-permute-start(f32[72,128]{1,0:T(8,128)S(1)} %get-tuple-element.32), channel_id=1, source_target_pairs={{0,5},{1,4},{2,7},{3,6},{4,1},{5,0},{6,3},{7,2},{8,13},{9,12},{10,... | collective-permute-start | bytes 110600 | tf_op jit(solution)/shard_map/ppermute | solution.py:30
  12.6 0.6 %post.1 = (f32[6,48,128]{2,1,0:T(8,128)S(1)}, f32[3,8,128]{2,1,0:T(8,128)S(1)}) custom-call(f32[16,48,128]{2,1,0:T(8,128)S(1)} %copy-done.1, f32[16,8,128]{2,1,0:T(8,128)S(1)} %collective-permute-done.mix_ref, f32[6,48,128]{2,1,0:T(8,128)S(1)} %bitcast.4, f32[6,8,128]{2,1,0:T(8,128)S(1)} %fusion.1.halo_mix_ref.refs_2_, ...), custom_call_target="tpu_custom_call" | custom-call | flops 7000000 | bytes 1000000 | tf_op jit(solution)/shard_map/post/pallas_call | solution.py:416
  13.2 0.0 collective-permute-done.5.zb_ref
  13.2 1.1 %collective-permute-done.4.za_ref = f32[72,128]{1,0:T(8,128)S(1)} collective-permute-done((f32[72,128]{1,0:T(8,128)S(1)}, f32[72,128]{1,0:T(8,128)S(1)}, u32[]{:S(2)}, u32[]{:S(2)}) %collective-permute-start.4) | collective-permute-done | bytes 36896 | tf_op jit(solution)/shard_map/ppermute | solution.py:30
  14.3 0.3 %edges.1 = (f32[72,128]{1,0:T(8,128)S(1)}, f32[8,128]{1,0:T(8,128)S(1)}) custom-call(f32[216,128]{1,0:T(8,128)S(1)} %get-tuple-element.31.strip_ref, f32[72,128]{1,0:T(8,128)S(1)} %collective-permute-done.4.za_ref, f32[72,128]{1,0:T(8,128)S(1)} %collective-permute-done.5.zb_ref, f32[3,8,128]{2,1,0:T(8,128)S(1)} %get-tuple-element.33.acc_ref), custom_call_target="tpu_custom_call" | custom-call | flops 1750000 | bytes 1000000 | tf_op jit(solution)/shard_map/edges/pallas_call | solution.py:416
  14.6 0.2 collective-permute-start.6
  14.8 1.0 %collective-permute-done.6 = f32[8,128]{1,0:T(8,128)S(1)} collective-permute-done((f32[8,128]{1,0:T(8,128)S(1)}, f32[8,128]{1,0:T(8,128)S(1)}, u32[]{:S(2)}, u32[]{:S(2)}) %collective-permute-start.6) | collective-permute-done | bytes 4128 | tf_op jit(solution)/shard_map/ppermute | solution.py:30
  15.8 3.8 %collective-permute-start.7 = (f32[8,128]{1,0:T(8,128)S(1)}, f32[8,128]{1,0:T(8,128)S(1)}, u32[]{:S(2)}, u32[]{:S(2)}) collective-permute-start(f32[8,128]{1,0:T(8,128)S(1)} %add.15), channel_id=1, source_target_pairs={{0,12},{1,13},{2,14},{3,15},{4,8},{5,9},{6,10},{7,11},{8,4},{9,5},... | collective-permute-start | bytes 12296 | tf_op jit(solution)/shard_map/ppermute | solution.py:30
  19.7 1.3 %collective-permute-done.7 = f32[8,128]{1,0:T(8,128)S(1)} collective-permute-done((f32[8,128]{1,0:T(8,128)S(1)}, f32[8,128]{1,0:T(8,128)S(1)}, u32[]{:S(2)}, u32[]{:S(2)}) %collective-permute-start.7) | collective-permute-done | bytes 4128 | tf_op jit(solution)/shard_map/ppermute | solution.py:30
  21.0 0.7 %collective-permute-start.8 = (f32[8,128]{1,0:T(8,128)S(1)}, f32[8,128]{1,0:T(8,128)S(1)}, u32[]{:S(2)}, u32[]{:S(2)}) collective-permute-start(f32[8,128]{1,0:T(8,128)S(1)} %add.16), channel_id=1, source_target_pairs={{0,20},{1,21},{2,22},{3,23},{4,16},{5,17},{6,18},{7,19},{8,28},{9,... | collective-permute-start | bytes 12296 | tf_op jit(solution)/shard_map/ppermute | solution.py:30
  21.7 2.3 %collective-permute-done.8 = f32[8,128]{1,0:T(8,128)S(1)} collective-permute-done((f32[8,128]{1,0:T(8,128)S(1)}, f32[8,128]{1,0:T(8,128)S(1)}, u32[]{:S(2)}, u32[]{:S(2)}) %collective-permute-start.8) | collective-permute-done | bytes 4128 | tf_op jit(solution)/shard_map/ppermute | solution.py:30
  24.0 1.6 %collective-permute-start.9 = (f32[8,128]{1,0:T(8,128)S(1)}, f32[8,128]{1,0:T(8,128)S(1)}, u32[]{:S(2)}, u32[]{:S(2)}) collective-permute-start(f32[8,128]{1,0:T(8,128)S(1)} %add.17), channel_id=1, source_target_pairs={{0,5},{1,4},{2,7},{3,6},{4,1},{5,0},{6,3},{7,2},{8,13},{9,12},{10,... | collective-permute-start | bytes 12296 | tf_op jit(solution)/shard_map/ppermute | solution.py:30
  25.7 1.4 %collective-permute-done.9 = f32[8,128]{1,0:T(8,128)S(1)} collective-permute-done((f32[8,128]{1,0:T(8,128)S(1)}, f32[8,128]{1,0:T(8,128)S(1)}, u32[]{:S(2)}, u32[]{:S(2)}) %collective-permute-start.9) | collective-permute-done | bytes 4128 | tf_op jit(solution)/shard_map/ppermute | solution.py:30
  27.1 1.5 %collective-permute-start.10 = (f32[8,128]{1,0:T(8,128)S(1)}, f32[8,128]{1,0:T(8,128)S(1)}, u32[]{:S(2)}, u32[]{:S(2)}) collective-permute-start(f32[8,128]{1,0:T(8,128)S(1)} %add.18), channel_id=1, source_target_pairs={{0,6},{1,7},{2,4},{3,5},{4,2},{5,3},{6,0},{7,1},{8,14},{9,15},{10,... | collective-permute-start | bytes 12296 | tf_op jit(solution)/shard_map/ppermute | solution.py:30
  28.6 1.3 %merge.1 = f32[16,48,128]{2,1,0:T(8,128)} custom-call(f32[16,48,128]{2,1,0:T(8,128)S(1)} %get-tuple-element.20.main_ref, f32[6,48,128]{2,1,0:T(8,128)S(1)} %get-tuple-element.29.ends_ref, f32[72,128]{1,0:T(8,128)S(1)} %get-tuple-element.34.edge_ref), custom_call_target="tpu_custom_call" | custom-call | flops 5250000 | bytes 1000000 | tf_op jit(solution)/shard_map/merge/pallas_call | solution.py:416
  29.9 1.1 %collective-permute-done.10 = f32[8,128]{1,0:T(8,128)S(1)} collective-permute-done((f32[8,128]{1,0:T(8,128)S(1)}, f32[8,128]{1,0:T(8,128)S(1)}, u32[]{:S(2)}, u32[]{:S(2)}) %collective-permute-start.10) | collective-permute-done | bytes 4128 | tf_op jit(solution)/shard_map/ppermute | solution.py:30
  31.0 0.1 slice_reduce_fusion
  31.1 0.5 %sqrt_multiply_fusion = f32[3]{0:T(128)} fusion(f32[3]{0:T(128)S(1)} %slice_reduce_fusion), kind=kLoop, calls=%fused_computation.13 | loop fusion | flops 6 | bytes 24 | tf_op jit(solution)/shard_map/div | solution.py:532
  (14 shorter events, 0.1 us)
Async XLA Ops:
  0.6 1.0 %copy-start = (f32[16,48,128]{2,1,0:T(8,128)S(1)}, f32[16,48,128]{2,1,0:T(8,128)}, u32[]{:S(2)}) copy-start(f32[16,48,128]{2,1,0:T(8,128)} %b_ref.5) | copy-start | bytes 1179652
  1.6 4.4 %copy-start.1 = (f32[16,48,128]{2,1,0:T(8,128)S(1)}, f32[16,48,128]{2,1,0:T(8,128)}, u32[]{:S(2)}) copy-start(f32[16,48,128]{2,1,0:T(8,128)} %b_ref.5) | copy-start | bytes 1179652
  1.6 6.1 %collective-permute-start.1 = (f32[3,48,128]{2,1,0:T(8,128)S(1)}, f32[3,48,128]{2,1,0:T(8,128)S(1)}, u32[]{:S(2)}, u32[]{:S(2)}) collective-permute-start(f32[3,48,128]{2,1,0:T(8,128)S(1)} %get-tuple-element.21), channel_id=1, source_target_pairs={{0,12},{1,13},{2,14},{3,15},{4,8},{5,9},{6,10},{7,11},{8,4},{9,5},... | collective-permute-start | bytes 221192 | tf_op jit(solution)/shard_map/ppermute | solution.py:30
  4.1 3.6 %collective-permute-start.2 = (f32[3,48,128]{2,1,0:T(8,128)S(1)}, f32[3,48,128]{2,1,0:T(8,128)S(1)}, u32[]{:S(2)}, u32[]{:S(2)}) collective-permute-start(f32[3,48,128]{2,1,0:T(8,128)S(1)} %get-tuple-element.22), channel_id=1, source_target_pairs={{0,4},{1,5},{2,6},{3,7},{4,0},{5,1},{6,2},{7,3},{8,20},{9,21},{10,... | collective-permute-start | bytes 221192 | tf_op jit(solution)/shard_map/ppermute | solution.py:30
  4.8 1.3 %collective-permute-start = (f32[16,8,128]{2,1,0:T(8,128)S(1)}, f32[16,8,128]{2,1,0:T(8,128)S(1)}, u32[]{:S(2)}, u32[]{:S(2)}) collective-permute-start(f32[16,8,128]{2,1,0:T(8,128)S(1)} %get-tuple-element.19), channel_id=1, source_target_pairs={{0,4},{1,5},{2,6},{3,7},{4,0},{5,1},{6,2},{7,3},{8,12},{9,13},{10,... | collective-permute-start | bytes 196616 | tf_op jit(solution)/shard_map/ppermute | solution.py:30
  7.8 1.5 %collective-permute-start.3 = (f32[360,128]{1,0:T(8,128)S(1)}, f32[360,128]{1,0:T(8,128)S(1)}, u32[]{:S(2)}, u32[]{:S(2)}) collective-permute-start(f32[360,128]{1,0:T(8,128)S(1)} %pad_maximum_fusion.1), channel_id=1, source_target_pairs={{0,4},{1,5},{2,6},{3,7},{4,0},{5,1},{6,2},{7,3},{8,12},{9,13},{10,... | collective-permute-start | bytes 552968 | tf_op jit(solution)/shard_map/ppermute | solution.py:30
  9.7 3.5 %collective-permute-start.5 = (f32[72,128]{1,0:T(8,128)S(1)}, f32[72,128]{1,0:T(8,128)S(1)}, u32[]{:S(2)}, u32[]{:S(2)}) collective-permute-start(f32[72,128]{1,0:T(8,128)S(1)} %get-tuple-element.32), channel_id=1, source_target_pairs={{0,4},{1,6},{2,5},{3,7},{4,0},{5,2},{6,1},{7,3},{8,12},{9,14},{10,... | collective-permute-start | bytes 110600 | tf_op jit(solution)/shard_map/ppermute | solution.py:30
  9.9 4.4 %collective-permute-start.4 = (f32[72,128]{1,0:T(8,128)S(1)}, f32[72,128]{1,0:T(8,128)S(1)}, u32[]{:S(2)}, u32[]{:S(2)}) collective-permute-start(f32[72,128]{1,0:T(8,128)S(1)} %get-tuple-element.32), channel_id=1, source_target_pairs={{0,5},{1,4},{2,7},{3,6},{4,1},{5,0},{6,3},{7,2},{8,13},{9,12},{10,... | collective-permute-start | bytes 110600 | tf_op jit(solution)/shard_map/ppermute | solution.py:30
  14.6 1.2 %collective-permute-start.6 = (f32[8,128]{1,0:T(8,128)S(1)}, f32[8,128]{1,0:T(8,128)S(1)}, u32[]{:S(2)}, u32[]{:S(2)}) collective-permute-start(f32[8,128]{1,0:T(8,128)S(1)} %get-tuple-element.35), channel_id=1, source_target_pairs={{0,4},{1,5},{2,6},{3,7},{4,0},{5,1},{6,2},{7,3},{8,12},{9,13},{10,... | collective-permute-start | bytes 12296 | tf_op jit(solution)/shard_map/ppermute | solution.py:30
  15.8 5.1 %collective-permute-start.7 = (f32[8,128]{1,0:T(8,128)S(1)}, f32[8,128]{1,0:T(8,128)S(1)}, u32[]{:S(2)}, u32[]{:S(2)}) collective-permute-start(f32[8,128]{1,0:T(8,128)S(1)} %add.15), channel_id=1, source_target_pairs={{0,12},{1,13},{2,14},{3,15},{4,8},{5,9},{6,10},{7,11},{8,4},{9,5},... | collective-permute-start | bytes 12296 | tf_op jit(solution)/shard_map/ppermute | solution.py:30
  21.0 3.0 %collective-permute-start.8 = (f32[8,128]{1,0:T(8,128)S(1)}, f32[8,128]{1,0:T(8,128)S(1)}, u32[]{:S(2)}, u32[]{:S(2)}) collective-permute-start(f32[8,128]{1,0:T(8,128)S(1)} %add.16), channel_id=1, source_target_pairs={{0,20},{1,21},{2,22},{3,23},{4,16},{5,17},{6,18},{7,19},{8,28},{9,... | collective-permute-start | bytes 12296 | tf_op jit(solution)/shard_map/ppermute | solution.py:30
  24.0 3.0 %collective-permute-start.9 = (f32[8,128]{1,0:T(8,128)S(1)}, f32[8,128]{1,0:T(8,128)S(1)}, u32[]{:S(2)}, u32[]{:S(2)}) collective-permute-start(f32[8,128]{1,0:T(8,128)S(1)} %add.17), channel_id=1, source_target_pairs={{0,5},{1,4},{2,7},{3,6},{4,1},{5,0},{6,3},{7,2},{8,13},{9,12},{10,... | collective-permute-start | bytes 12296 | tf_op jit(solution)/shard_map/ppermute | solution.py:30
  27.1 3.9 %collective-permute-start.10 = (f32[8,128]{1,0:T(8,128)S(1)}, f32[8,128]{1,0:T(8,128)S(1)}, u32[]{:S(2)}, u32[]{:S(2)}) collective-permute-start(f32[8,128]{1,0:T(8,128)S(1)} %add.18), channel_id=1, source_target_pairs={{0,6},{1,7},{2,4},{3,5},{4,2},{5,3},{6,0},{7,1},{8,14},{9,15},{10,... | collective-permute-start | bytes 12296 | tf_op jit(solution)/shard_map/ppermute | solution.py:30

commit v4 on v3

--- a/solution.py
+++ b/solution.py
@@ -7,6 +7,7 @@
 from jax.experimental.pallas import tpu as pltpu
 from jax.sharding import PartitionSpec as P
 
+
 ITERS = 3
 HALO = ITERS
 AXES = ("gx", "gy", "gz")
@@ -30,7 +31,7 @@
     return lax.ppermute(value, AXES, pairs)
 
 
-def neighbour(dim, colour, cross):
+def neighbour(dim, colour):
     sizes = [lax.axis_size(a) for a in AXES]
 
     def partner(place):
@@ -39,8 +40,6 @@
         there = here ^ 1 if colour == 0 else ((here - 1) ^ 1) + 1
         if 0 <= there < sizes[dim]:
             place[dim] = there
-            if cross:
-                place[1] ^= 1
         elif dim != 1 and sizes[1] % 2 == 0:
             place[1] ^= 1
         elif colour == 1 and sizes[dim] % 2 == 0:
@@ -50,15 +49,11 @@
     return partner
 
 
-def exchange(value_even, value_odd, dim, cross=False):
-    first = pair_swap(value_even, neighbour(dim, 0, cross))
+def exchange(value_even, value_odd, dim):
+    first = pair_swap(value_even, neighbour(dim, 0))
     if lax.axis_size(AXES[dim]) == 2:
         return first, first
-    return first, pair_swap(value_odd, neighbour(dim, 1, cross))
-
-
-def other_row(place):
-    return (place[0], place[1] ^ 1, place[2])
+    return first, pair_swap(value_odd, neighbour(dim, 1))
 
 
 def sum_over_devices(value):
@@ -115,13 +110,10 @@
     return c - k * (root - 1.0)
 
 
-def faces_kernel(sizes, b_ref, *outs):
-    planes, rows, _ = sizes
-    x_odd, y_odd = odd("gx"), odd("gy")
-    for n, ref in enumerate(outs[:2]):
-        low = x_odd if n == 0 else ~x_odd
-        ref[...] = b_ref[pl.ds(jnp.where(low, 0, planes - HALO), HALO)]
-    for n, ref in enumerate(outs[2:]):
+def tiles_kernel(sizes, b_ref, *outs):
+    rows = sizes[1]
+    y_odd = odd("gy")
+    for n, ref in enumerate(outs):
         low = y_odd if n == 0 else ~y_odd
         start = pl.multiple_of(jnp.where(low, 0, rows - TILE), TILE)
         ref[...] = b_ref[:, pl.ds(start, TILE)]
@@ -164,23 +156,39 @@
     return jnp.where(near, low, lines_ref[(i + shift) * pitch : (i + shift + 1) * pitch])
 
 
-def pre_kernel(
-    sizes, b_ref, mix_ref, e1_ref, e2_ref, out_ref, s_ref, k_ref, acc_ref, lines_ref, mid_ref, e0
-):
+def fronts_kernel(sizes, b_ref, mix_ref, la_ref, lb_ref, xa_ref, xb_ref):
     planes, rows, lanes = sizes
+    x_odd = odd("gx")
+    low = [turned_lines(b_ref[p], mix_ref[p], lanes) for p in range(HALO)]
+    high = [turned_lines(b_ref[p], mix_ref[p], lanes) for p in range(planes - HALO, planes)]
+    for i in range(HALO):
+        here = pl.ds(i * TILE, TILE)
+        la_ref[here] = jnp.where(x_odd, low[i], high[i])
+        lb_ref[here] = jnp.where(x_odd, high[i], low[i])
+    for ref, is_low in ((xa_ref, x_odd), (xb_ref, ~x_odd)):
+        start = jnp.where(is_low, 0, planes - HALO)
+        ref[:, 0:rows] = b_ref[pl.ds(start, HALO)]
+        ref[:, rows : rows + TILE] = mix_ref[pl.ds(start, HALO)]
+
+
+def lines_kernel(sizes, b_ref, mix_ref, lines_ref):
+    planes, _, lanes = sizes
     pitch = lines_ref.shape[0] // TILE
+    for p in range(planes):
+        lines_ref[pl.ds(p + HALO, TILE, stride=pitch)] = turned_lines(
+            b_ref[p], mix_ref[p], lanes
+        )
+
+
+def pre_kernel(sizes, b_ref, mix_ref, e1_ref, e2_ref, out_ref, s_ref, k_ref, acc_ref, e0):
+    planes, rows, lanes = sizes
     marks = plane_marks(sizes)
     lane = lax.broadcasted_iota(jnp.int32, (TILE, lanes), 1)
-    near = lax.broadcasted_iota(jnp.int32, (pitch, 2 * HALF), 1) < HALF
 
     for p in range(planes):
-        own, mix = b_ref[p], mix_ref[p]
-        lines_ref[pl.ds(p + HALO, TILE, stride=pitch)] = turned_lines(own, mix, lanes)
-        full = jnp.concatenate([own, mix], axis=0)
+        full = jnp.concatenate([b_ref[p], mix_ref[p]], axis=0)
         e0[p] = full
         s_ref[p], k_ref[p] = sign_factors(full)
-    for i in range(HALO):
-        mid_ref[i * pitch : (i + 1) * pitch] = middle(lines_ref, i, pitch, near)
 
     inner = (lane >= HALO) & (lane < lanes - HALO)
     bufs = (e0, e1_ref, e2_ref)
@@ -200,22 +208,16 @@
         acc_ref[it] = jnp.where(inner, acc, 0.0)
 
 
-def ends_kernel(sizes, cross, *refs):
-    planes, rows, lanes = sizes
-    lines_ref, halo_ref, mix_ref = refs[:3]
-    if cross:
-        mid_ref, held_ref, held_mix_ref = refs[3:6]
-    strip_ref, send_ref, lines, given = refs[-4:]
+def ends_kernel(sizes, lines_ref, la_ref, lb_ref, strip_ref, send_ref, lines):
+    planes = sizes[0]
     pitch = lines_ref.shape[0] // TILE
     near = lax.broadcasted_iota(jnp.int32, (pitch, 2 * HALF), 1) < HALF
     lines[...] = lines_ref[...]
-    for i in range(2 * HALO):
-        x = i if i < HALO else i + planes
-        lines[pl.ds(x, TILE, stride=pitch)] = turned_lines(halo_ref[i], mix_ref[i], lanes)
-        if cross:
-            given[pl.ds(x, TILE, stride=pitch)] = turned_lines(
-                held_ref[i], held_mix_ref[i], lanes
-            )
+    low, high = low_high(la_ref[...], lb_ref[...], "gx")
+    for i in range(HALO):
+        here = slice(i * TILE, (i + 1) * TILE)
+        lines[pl.ds(i, TILE, stride=pitch)] = low[here]
+        lines[pl.ds(i + HALO + planes, TILE, stride=pitch)] = high[here]
     shift = TILE - 2 * HALO
     for j in range(3 * HALO):
         if j < HALO:
@@ -224,24 +226,16 @@
             value = lines[(j - HALO) * pitch : (j - HALO + 1) * pitch]
         else:
             value = middle(lines, j - HALO, pitch, near)
+            send_ref[(j - HALO) * pitch : (j - HALO + 1) * pitch] = value
         strip_ref[j * pitch : (j + 1) * pitch] = value
-        i = j - HALO
-        if 0 <= i < HALO:
-            if cross:
-                line = lax.broadcasted_iota(jnp.int32, (pitch, 2 * HALF), 0)
-                theirs = (line >= HALO) & (line < HALO + planes)
-                value = jnp.where(
-                    theirs, mid_ref[i * pitch : (i + 1) * pitch], middle(given, i, pitch, near)
-                )
-            send_ref[i * pitch : (i + 1) * pitch] = value
 
 
 def post_kernel(
     sizes,
     b_ref,
     mix_ref,
-    halo_ref,
-    halo_mix_ref,
+    xa_ref,
+    xb_ref,
     e1_ref,
     e2_ref,
     s_ref,
@@ -262,8 +256,8 @@
     def start(p):
         if 0 <= p < planes:
             return jnp.concatenate([b_ref[p], mix_ref[p]], axis=0)
-        i = p + HALO if p < 0 else p - planes + HALO
-        return jnp.concatenate([halo_ref[i], halo_mix_ref[i]], axis=0)
+        i = p + HALO if p < 0 else p - planes
+        return low_high(xa_ref[i], xb_ref[i], "gx")[0 if p < 0 else 1]
 
     def factor(p):
         if 0 <= p < planes:
@@ -301,7 +295,7 @@
 
 
 def edge_kernel(sizes, strip_ref, za_ref, zb_ref, acc_ref, out_ref, sum_ref):
-    planes, rows, lanes = sizes
+    planes, rows, _ = sizes
     pitch = strip_ref.shape[0] // (3 * HALO)
     x_first, x_last = at_ends("gx")
     y_first, y_last = at_ends("gy")
@@ -412,7 +406,7 @@
     return pl.CostEstimate(flops=int(us * 3.5e6), bytes_accessed=nbytes, transcendentals=0)
 
 
-def call(kernel, sizes, inputs, outputs, scratch, mib, us, name):
+def call(kernel, sizes, inputs, outputs, scratch, mib, us):
     return pl.pallas_call(
         functools.partial(kernel, sizes),
         out_shape=tuple(jax.ShapeDtypeStruct(o, jnp.float32) for o in outputs),
@@ -421,7 +415,6 @@
         scratch_shapes=[pltpu.VMEM(t, jnp.float32) for t in scratch],
         compiler_params=grant(mib),
         cost_estimate=cost(us, 10**6),
-        name=name,
     )(*inputs)
 
 
@@ -431,8 +424,6 @@
     wide = planes + 2 * HALO
     tall = rows + TILE
     pitch = -(-wide // TILE) * TILE
-    cross = lax.axis_size("gy") == 2
-    y_odd = odd("gy")
 
     def mixed(first, second):
         if first is second:
@@ -441,73 +432,47 @@
         sub = lax.broadcasted_iota(jnp.int32, first.shape, 1)
         return jnp.where(sub < TILE // 2, high, low)
 
-    face, tile = (HALO, rows, lanes), (planes, TILE, lanes)
-    xs_even, xs_odd, *ys = call(
-        faces_kernel,
+    colours = 1 if lax.axis_size("gy") == 2 else 2
+    ys = call(tiles_kernel, sizes, (phi_start,), ((planes, TILE, lanes),) * colours, (), 2, 0.2)
+    mix = mixed(*exchange(ys[0], ys[-1], 1))
+
+    line, front = (HALO * TILE, 2 * HALF), (HALO, tall, lanes)
+    la, lb, xa, xb = call(
+        fronts_kernel, sizes, (phi_start, mix), (line, line, front, front), (), 2, 0.2
+    )
+    la, lb = exchange(la, lb, 0)
+    xa, xb = exchange(xa, xb, 0)
+
+    (lines,) = call(lines_kernel, sizes, (phi_start, mix), ((TILE * pitch, 2 * HALF),), (), 2, 0.5)
+    strip, send = call(
+        ends_kernel,
         sizes,
-        (phi_start,),
-        (face, face, tile) if cross else (face, face, tile, tile),
-        (),
-        2,
-        0.5,
-        "faces",
+        (lines, la, lb),
+        ((3 * HALO * pitch, 2 * HALF), (HALO * pitch, 2 * HALF)),
+        ((TILE * pitch, 2 * HALF),),
+        4,
+        0.2,
     )
-
-    xa, xb = exchange(xs_even, xs_odd, 0, cross)
-    mix = mixed(*exchange(ys[0], ys[-1], 1))
+    za, zb = exchange(send, send, 2)
 
     block = (planes, tall, lanes)
-    e1, e2, inner, s, k, acc, lines, mid = call(
+    e1, e2, inner, s, k, acc = call(
         pre_kernel,
         sizes,
         (phi_start, mix),
-        (block, block, sizes, block, block, (ITERS, TILE, lanes))
-        + ((TILE * pitch, 2 * HALF), (HALO * pitch, 2 * HALF)),
+        (block, block, sizes, block, block, (ITERS, TILE, lanes)),
         (block,),
         8,
-        2,
-        "pre",
+        1.5,
     )
-
-    halo = jnp.concatenate(low_high(xa, xb, "gx"), axis=0)
-    first_rows, last_rows = slice(0, TILE), slice(rows - TILE, rows)
-    if cross:
-        held = halo
-        flat = held.reshape(2 * HALO * rows, lanes)
-        swapped = pair_swap(jnp.concatenate([flat, mid], axis=0), other_row)
-        halo = swapped[: 2 * HALO * rows].reshape(held.shape)
-        mid = swapped[2 * HALO * rows :]
-        halo_mix = jnp.where(y_odd, held[:, last_rows], held[:, first_rows])
-        held_mix = jnp.where(y_odd, halo[:, first_rows], halo[:, last_rows])
-        given = (mid, held, held_mix)
-    else:
-        top, tail = halo[:, first_rows], halo[:, last_rows]
-        halo_mix = mixed(
-            *exchange(jnp.where(y_odd, top, tail), jnp.where(y_odd, tail, top), 1)
-        )
-        given = ()
-
-    strip, send = call(
-        lambda sizes, *refs: ends_kernel(sizes, cross, *refs),
-        sizes,
-        (lines, halo, halo_mix, *given),
-        ((3 * HALO * pitch, 2 * HALF), (HALO * pitch, 2 * HALF)),
-        ((TILE * pitch, 2 * HALF),) * 2,
-        4,
-        0.5,
-        "ends",
-    )
-    za, zb = exchange(send, send, 2, cross)
-
     tips, acc = call(
         post_kernel,
         sizes,
-        (phi_start, mix, halo, halo_mix, e1, e2, s, k, acc),
+        (phi_start, mix, xa, xb, e1, e2, s, k, acc),
         ((2 * HALO, rows, lanes), (ITERS, TILE, lanes)),
         ((4 * HALO, tall, lanes),) * 2,
         8,
-        2,
-        "post",
+        0.6,
     )
 
     edge, sums = call(
@@ -518,12 +483,9 @@
         (),
         4,
         0.5,
-        "edges",
     )
 
-    (phi_final,) = call(
-        merge_kernel, sizes, (inner, tips, edge), (sizes,), (), 4, 1.5, "merge"
-    )
+    (phi_final,) = call(merge_kernel, sizes, (inner, tips, edge), (sizes,), (), 4, 1.5)
 
     totals = jnp.sum(sum_over_devices(sums)[:ITERS], axis=1)
     cells = planes * rows * lanes

time: 31.8 us -> 33 us (1.038)
  starting transfers between devices: 14.2 us -> 17.1 us
  waiting for transfers between devices: 10.8 us -> 9.21 us
    ppermute x11 -> x12, starting transfers between devices: 14.2 us -> 17.1 us  [pair_swap(): return lax.ppermute(value, AXES, pairs)]
    ppermute x11 -> x12, waiting for transfers between devices: 10.8 us -> 9.21 us  [pair_swap(): return lax.ppermute(value, AXES, pairs)]
    pallas_call x6 -> x8, Pallas kernels: 4.19 us -> 4.26 us  [call(): pl.pallas_call(functools.partial(kernel, sizes), out_shape=tuple((jax.Sha...]
  transfers between devices with their start and end apart: 11 -> 12, of which waited for: 8 -> 7; matrix products, arithmetic and copies ran while one was open for 0% -> 0% of each run, Pallas kernels for 11% -> 11%
where the time goes in v4:
time: 33 us; the launch traced here: 32.9 us
  starting transfers between devices  17.1 us (52%)
  waiting for transfers between devices  9.21 us (28%)
  Pallas kernels  4.26 us (13%)
  local copies, waits for them, and re-layouts  0.99 us (3%)
  between operations  0.68 us (2%)
  other arithmetic  0.66 us (2%)
    ppermute x12, starting transfers between devices, pair_swap(): return lax.ppermute(value, AXES, pairs)  17.1 us
    ppermute x12, waiting for transfers between devices, pair_swap(): return lax.ppermute(value, AXES, pairs)  9.21 us
    pallas_call x8, Pallas kernels, call(): pl.pallas_call(functools.partial(kernel, sizes), out_shape=tuple((jax.Sha...  4.26 us
    unnamed x4, local copies, waits for them, and re-layouts  0.99 us
  transfers between devices with their start and end apart: 12, of which 7 were waited for; matrix products, arithmetic and copies ran while one was open for 0% of the time, Pallas kernels for 11%

profile of v4, /device:TPU:0, one launch (start us, length us, event | category | flops | bytes accessed | tf_op | source)
XLA Modules:
  0.0 32.9 jit_solution(2286674673931596851)
XLA Ops:
  0.6 0.0 copy-start
  0.6 1.0 %copy-done = f32[16,48,128]{2,1,0:T(8,128)S(1)} copy-done((f32[16,48,128]{2,1,0:T(8,128)S(1)}, f32[16,48,128]{2,1,0:T(8,128)}, u32[]{:S(2)}) %copy-start) | copy-done | bytes 393240
  1.6 0.5 %collective-permute-start = (f32[16,8,128]{2,1,0:T(8,128)S(1)}, f32[16,8,128]{2,1,0:T(8,128)S(1)}, u32[]{:S(2)}, u32[]{:S(2)}) collective-permute-start(f32[16,8,128]{2,1,0:T(8,128)S(1)} %shard_map.30), channel_id=1, source_target_pairs={{0,4},{1,5},{2,6},{3,7},{4,0},{5,1},{6,2},{7,3},{8,12},{9,13},{10,... | collective-permute-start | bytes 196616 | tf_op jit(solution)/shard_map/ppermute | solution.py:31
  2.1 0.9 %collective-permute-done.mix_ref = f32[16,8,128]{2,1,0:T(8,128)S(1)} collective-permute-done((f32[16,8,128]{2,1,0:T(8,128)S(1)}, f32[16,8,128]{2,1,0:T(8,128)S(1)}, u32[]{:S(2)}, u32[]{:S(2)}) %collective-permute-start) | collective-permute-done | bytes 65568 | tf_op jit(solution)/shard_map/ppermute | solution.py:31
  3.0 0.2 shard_map.32
  3.2 2.9 %collective-permute-start.1 = (f32[3,56,128]{2,1,0:T(8,128)S(1)}, f32[3,56,128]{2,1,0:T(8,128)S(1)}, u32[]{:S(2)}, u32[]{:S(2)}) collective-permute-start(f32[3,56,128]{2,1,0:T(8,128)S(1)} %get-tuple-element.19), channel_id=1, source_target_pairs={{0,8},{1,9},{2,10},{3,11},{4,12},{5,13},{6,14},{7,15},{8,0},{9,1},... | collective-permute-start | bytes 258056 | tf_op jit(solution)/shard_map/ppermute | solution.py:31
  6.1 0.0 collective-permute-start.2
  6.1 3.0 %collective-permute-start.3 = (f32[24,128]{1,0:T(8,128)S(1)}, f32[24,128]{1,0:T(8,128)S(1)}, u32[]{:S(2)}, u32[]{:S(2)}) collective-permute-start(f32[24,128]{1,0:T(8,128)S(1)} %get-tuple-element.27), channel_id=1, source_target_pairs={{0,8},{1,9},{2,10},{3,11},{4,12},{5,13},{6,14},{7,15},{8,0},{9,1},... | collective-permute-start | bytes 36872 | tf_op jit(solution)/shard_map/ppermute | solution.py:31
  9.1 0.0 collective-permute-start.4
  9.1 0.4 %shard_map.34.lines_ref = f32[192,128]{1,0:T(8,128)S(1)} custom-call(f32[16,48,128]{2,1,0:T(8,128)S(1)} %copy-done, f32[16,8,128]{2,1,0:T(8,128)S(1)} %collective-permute-done.mix_ref), custom_call_target="tpu_custom_call" | custom-call | flops 1750000 | bytes 1000000 | tf_op jit(solution)/shard_map/pallas_call | solution.py:410
  9.5 2.3 %collective-permute-done.3.la_ref = f32[24,128]{1,0:T(8,128)S(1)} collective-permute-done((f32[24,128]{1,0:T(8,128)S(1)}, f32[24,128]{1,0:T(8,128)S(1)}, u32[]{:S(2)}, u32[]{:S(2)}) %collective-permute-start.3) | collective-permute-done | bytes 12320 | tf_op jit(solution)/shard_map/ppermute | solution.py:31
  11.8 0.0 collective-permute-done.4.lb_ref
  11.8 1.6 %collective-permute-start.5 = (f32[72,128]{1,0:T(8,128)S(1)}, f32[72,128]{1,0:T(8,128)S(1)}, u32[]{:S(2)}, u32[]{:S(2)}) collective-permute-start(f32[72,128]{1,0:T(8,128)S(1)} %get-tuple-element.30), channel_id=1, source_target_pairs={{0,1},{1,0},{2,3},{3,2},{4,5},{5,4},{6,7},{7,6},{8,9},{9,8},{10,11... | collective-permute-start | bytes 110600 | tf_op jit(solution)/shard_map/ppermute | solution.py:31
  13.5 0.0 collective-permute-start.6
  13.5 1.4 %shard_map.31 = (f32[16,56,128]{2,1,0:T(8,128)S(1)}, f32[16,56,128]{2,1,0:T(8,128)S(1)}, f32[16,48,128]{2,1,0:T(8,128)S(1)}, f32[16,56,128]{2,1,0:T(8,128)S(1)},...) custom-call(f32[16,48,128]{2,1,0:T(8,128)S(1)} %copy-done.1, f32[16,8,128]{2,1,0:T(8,128)S(1)} %collective-permute-done.mix_ref), custom_call_target="tpu_custom_call" | custom-call | flops 5250000 | bytes 1000000 | tf_op jit(solution)/shard_map/pallas_call | solution.py:410
  14.9 0.0 collective-permute-done.2.xb_ref
  14.9 0.6 %shard_map.33 = (f32[6,48,128]{2,1,0:T(8,128)S(1)}, f32[3,8,128]{2,1,0:T(8,128)S(1)}) custom-call(f32[16,48,128]{2,1,0:T(8,128)S(1)} %copy-done.1, f32[16,8,128]{2,1,0:T(8,128)S(1)} %collective-permute-done.mix_ref, f32[3,56,128]{2,1,0:T(8,128)S(1)} %collective-permute-done.1.xa_ref, f32[3,56,128]{2,1,0:T(8,128)S(1)} %collective-permute-done.2.xb_ref, ...), custom_call_target="tpu_custom_call" | custom-call | flops 2100000 | bytes 1000000 | tf_op jit(solution)/shard_map/pallas_call | solution.py:410
  15.5 0.3 %collective-permute-done.5.za_ref = f32[72,128]{1,0:T(8,128)S(1)} collective-permute-done((f32[72,128]{1,0:T(8,128)S(1)}, f32[72,128]{1,0:T(8,128)S(1)}, u32[]{:S(2)}, u32[]{:S(2)}) %collective-permute-start.5) | collective-permute-done | bytes 36896 | tf_op jit(solution)/shard_map/ppermute | solution.py:31
  15.8 0.3 shard_map.36
  16.2 0.2 collective-permute-start.7
  16.4 1.0 %collective-permute-done.7 = f32[8,128]{1,0:T(8,128)S(1)} collective-permute-done((f32[8,128]{1,0:T(8,128)S(1)}, f32[8,128]{1,0:T(8,128)S(1)}, u32[]{:S(2)}, u32[]{:S(2)}) %collective-permute-start.7) | collective-permute-done | bytes 4128 | tf_op jit(solution)/shard_map/ppermute | solution.py:31
  17.4 2.0 %collective-permute-start.8 = (f32[8,128]{1,0:T(8,128)S(1)}, f32[8,128]{1,0:T(8,128)S(1)}, u32[]{:S(2)}, u32[]{:S(2)}) collective-permute-start(f32[8,128]{1,0:T(8,128)S(1)} %add.15), channel_id=1, source_target_pairs={{0,12},{1,13},{2,14},{3,15},{4,8},{5,9},{6,10},{7,11},{8,4},{9,5},... | collective-permute-start | bytes 12296 | tf_op jit(solution)/shard_map/ppermute | solution.py:31
  19.4 1.3 %collective-permute-done.8 = f32[8,128]{1,0:T(8,128)S(1)} collective-permute-done((f32[8,128]{1,0:T(8,128)S(1)}, f32[8,128]{1,0:T(8,128)S(1)}, u32[]{:S(2)}, u32[]{:S(2)}) %collective-permute-start.8) | collective-permute-done | bytes 4128 | tf_op jit(solution)/shard_map/ppermute | solution.py:31
  20.8 1.0 %collective-permute-start.9 = (f32[8,128]{1,0:T(8,128)S(1)}, f32[8,128]{1,0:T(8,128)S(1)}, u32[]{:S(2)}, u32[]{:S(2)}) collective-permute-start(f32[8,128]{1,0:T(8,128)S(1)} %add.16), channel_id=1, source_target_pairs={{0,20},{1,21},{2,22},{3,23},{4,16},{5,17},{6,18},{7,19},{8,28},{9,... | collective-permute-start | bytes 12296 | tf_op jit(solution)/shard_map/ppermute | solution.py:31
  21.8 2.0 %collective-permute-done.9 = f32[8,128]{1,0:T(8,128)S(1)} collective-permute-done((f32[8,128]{1,0:T(8,128)S(1)}, f32[8,128]{1,0:T(8,128)S(1)}, u32[]{:S(2)}, u32[]{:S(2)}) %collective-permute-start.9) | collective-permute-done | bytes 4128 | tf_op jit(solution)/shard_map/ppermute | solution.py:31
  23.8 2.7 %collective-permute-start.10 = (f32[8,128]{1,0:T(8,128)S(1)}, f32[8,128]{1,0:T(8,128)S(1)}, u32[]{:S(2)}, u32[]{:S(2)}) collective-permute-start(f32[8,128]{1,0:T(8,128)S(1)} %add.17), channel_id=1, source_target_pairs={{0,5},{1,4},{2,7},{3,6},{4,1},{5,0},{6,3},{7,2},{8,13},{9,12},{10,... | collective-permute-start | bytes 12296 | tf_op jit(solution)/shard_map/ppermute | solution.py:31
  26.5 1.3 %collective-permute-done.10 = f32[8,128]{1,0:T(8,128)S(1)} collective-permute-done((f32[8,128]{1,0:T(8,128)S(1)}, f32[8,128]{1,0:T(8,128)S(1)}, u32[]{:S(2)}, u32[]{:S(2)}) %collective-permute-start.10) | collective-permute-done | bytes 4128 | tf_op jit(solution)/shard_map/ppermute | solution.py:31
  27.8 3.0 %collective-permute-start.11 = (f32[8,128]{1,0:T(8,128)S(1)}, f32[8,128]{1,0:T(8,128)S(1)}, u32[]{:S(2)}, u32[]{:S(2)}) collective-permute-start(f32[8,128]{1,0:T(8,128)S(1)} %add.18), channel_id=1, source_target_pairs={{0,6},{1,7},{2,4},{3,5},{4,2},{5,3},{6,0},{7,1},{8,14},{9,15},{10,... | collective-permute-start | bytes 12296 | tf_op jit(solution)/shard_map/ppermute | solution.py:31
  30.9 1.3 %shard_map.37 = f32[16,48,128]{2,1,0:T(8,128)} custom-call(f32[16,48,128]{2,1,0:T(8,128)S(1)} %get-tuple-element.18.main_ref, f32[6,48,128]{2,1,0:T(8,128)S(1)} %get-tuple-element.26.ends_ref, f32[72,128]{1,0:T(8,128)S(1)} %get-tuple-element.32.edge_ref), custom_call_target="tpu_custom_call" | custom-call | flops 5250000 | bytes 1000000 | tf_op jit(solution)/shard_map/pallas_call | solution.py:410
  32.2 0.0 collective-permute-done.11
  32.2 0.1 slice_reduce_fusion
  32.3 0.5 %sqrt_multiply_fusion = f32[3]{0:T(128)} fusion(f32[3]{0:T(128)S(1)} %slice_reduce_fusion), kind=kLoop, calls=%fused_computation.1 | loop fusion | flops 6 | bytes 24 | tf_op jit(solution)/shard_map/div | solution.py:494
  (11 shorter events, 0.1 us)
Async XLA Ops:
  0.6 1.0 %copy-start = (f32[16,48,128]{2,1,0:T(8,128)S(1)}, f32[16,48,128]{2,1,0:T(8,128)}, u32[]{:S(2)}) copy-start(f32[16,48,128]{2,1,0:T(8,128)} %b_ref.9) | copy-start | bytes 1179652
  1.6 1.4 %collective-permute-start = (f32[16,8,128]{2,1,0:T(8,128)S(1)}, f32[16,8,128]{2,1,0:T(8,128)S(1)}, u32[]{:S(2)}, u32[]{:S(2)}) collective-permute-start(f32[16,8,128]{2,1,0:T(8,128)S(1)} %shard_map.30), channel_id=1, source_target_pairs={{0,4},{1,5},{2,6},{3,7},{4,0},{5,1},{6,2},{7,3},{8,12},{9,13},{10,... | collective-permute-start | bytes 196616 | tf_op jit(solution)/shard_map/ppermute | solution.py:31
  3.2 10.2 %copy-start.1 = (f32[16,48,128]{2,1,0:T(8,128)S(1)}, f32[16,48,128]{2,1,0:T(8,128)}, u32[]{:S(2)}) copy-start(f32[16,48,128]{2,1,0:T(8,128)} %b_ref.9) | copy-start | bytes 1179652
  3.2 11.6 %collective-permute-start.1 = (f32[3,56,128]{2,1,0:T(8,128)S(1)}, f32[3,56,128]{2,1,0:T(8,128)S(1)}, u32[]{:S(2)}, u32[]{:S(2)}) collective-permute-start(f32[3,56,128]{2,1,0:T(8,128)S(1)} %get-tuple-element.19), channel_id=1, source_target_pairs={{0,8},{1,9},{2,10},{3,11},{4,12},{5,13},{6,14},{7,15},{8,0},{9,1},... | collective-permute-start | bytes 258056 | tf_op jit(solution)/shard_map/ppermute | solution.py:31
  6.1 8.8 %collective-permute-start.2 = (f32[3,56,128]{2,1,0:T(8,128)S(1)}, f32[3,56,128]{2,1,0:T(8,128)S(1)}, u32[]{:S(2)}, u32[]{:S(2)}) collective-permute-start(f32[3,56,128]{2,1,0:T(8,128)S(1)} %get-tuple-element.20), channel_id=1, source_target_pairs={{0,4},{1,5},{2,6},{3,7},{4,0},{5,1},{6,2},{7,3},{8,16},{9,17},{10,... | collective-permute-start | bytes 258056 | tf_op jit(solution)/shard_map/ppermute | solution.py:31
  6.1 5.7 %collective-permute-start.3 = (f32[24,128]{1,0:T(8,128)S(1)}, f32[24,128]{1,0:T(8,128)S(1)}, u32[]{:S(2)}, u32[]{:S(2)}) collective-permute-start(f32[24,128]{1,0:T(8,128)S(1)} %get-tuple-element.27), channel_id=1, source_target_pairs={{0,8},{1,9},{2,10},{3,11},{4,12},{5,13},{6,14},{7,15},{8,0},{9,1},... | collective-permute-start | bytes 36872 | tf_op jit(solution)/shard_map/ppermute | solution.py:31
  9.1 2.7 %collective-permute-start.4 = (f32[24,128]{1,0:T(8,128)S(1)}, f32[24,128]{1,0:T(8,128)S(1)}, u32[]{:S(2)}, u32[]{:S(2)}) collective-permute-start(f32[24,128]{1,0:T(8,128)S(1)} %get-tuple-element.28), channel_id=1, source_target_pairs={{0,4},{1,5},{2,6},{3,7},{4,0},{5,1},{6,2},{7,3},{8,16},{9,17},{10,... | collective-permute-start | bytes 36872 | tf_op jit(solution)/shard_map/ppermute | solution.py:31
  11.8 4.0 %collective-permute-start.5 = (f32[72,128]{1,0:T(8,128)S(1)}, f32[72,128]{1,0:T(8,128)S(1)}, u32[]{:S(2)}, u32[]{:S(2)}) collective-permute-start(f32[72,128]{1,0:T(8,128)S(1)} %get-tuple-element.30), channel_id=1, source_target_pairs={{0,1},{1,0},{2,3},{3,2},{4,5},{5,4},{6,7},{7,6},{8,9},{9,8},{10,11... | collective-permute-start | bytes 110600 | tf_op jit(solution)/shard_map/ppermute | solution.py:31
  13.5 2.4 %collective-permute-start.6 = (f32[72,128]{1,0:T(8,128)S(1)}, f32[72,128]{1,0:T(8,128)S(1)}, u32[]{:S(2)}, u32[]{:S(2)}) collective-permute-start(f32[72,128]{1,0:T(8,128)S(1)} %get-tuple-element.30), channel_id=1, source_target_pairs={{0,4},{1,2},{2,1},{3,7},{4,0},{5,6},{6,5},{7,3},{8,12},{9,10},{10,... | collective-permute-start | bytes 110600 | tf_op jit(solution)/shard_map/ppermute | solution.py:31
  16.2 1.2 %collective-permute-start.7 = (f32[8,128]{1,0:T(8,128)S(1)}, f32[8,128]{1,0:T(8,128)S(1)}, u32[]{:S(2)}, u32[]{:S(2)}) collective-permute-start(f32[8,128]{1,0:T(8,128)S(1)} %get-tuple-element.33), channel_id=1, source_target_pairs={{0,4},{1,5},{2,6},{3,7},{4,0},{5,1},{6,2},{7,3},{8,12},{9,13},{10,... | collective-permute-start | bytes 12296 | tf_op jit(solution)/shard_map/ppermute | solution.py:31
  17.4 3.4 %collective-permute-start.8 = (f32[8,128]{1,0:T(8,128)S(1)}, f32[8,128]{1,0:T(8,128)S(1)}, u32[]{:S(2)}, u32[]{:S(2)}) collective-permute-start(f32[8,128]{1,0:T(8,128)S(1)} %add.15), channel_id=1, source_target_pairs={{0,12},{1,13},{2,14},{3,15},{4,8},{5,9},{6,10},{7,11},{8,4},{9,5},... | collective-permute-start | bytes 12296 | tf_op jit(solution)/shard_map/ppermute | solution.py:31
  20.8 3.0 %collective-permute-start.9 = (f32[8,128]{1,0:T(8,128)S(1)}, f32[8,128]{1,0:T(8,128)S(1)}, u32[]{:S(2)}, u32[]{:S(2)}) collective-permute-start(f32[8,128]{1,0:T(8,128)S(1)} %add.16), channel_id=1, source_target_pairs={{0,20},{1,21},{2,22},{3,23},{4,16},{5,17},{6,18},{7,19},{8,28},{9,... | collective-permute-start | bytes 12296 | tf_op jit(solution)/shard_map/ppermute | solution.py:31
  23.8 4.0 %collective-permute-start.10 = (f32[8,128]{1,0:T(8,128)S(1)}, f32[8,128]{1,0:T(8,128)S(1)}, u32[]{:S(2)}, u32[]{:S(2)}) collective-permute-start(f32[8,128]{1,0:T(8,128)S(1)} %add.17), channel_id=1, source_target_pairs={{0,5},{1,4},{2,7},{3,6},{4,1},{5,0},{6,3},{7,2},{8,13},{9,12},{10,... | collective-permute-start | bytes 12296 | tf_op jit(solution)/shard_map/ppermute | solution.py:31
  27.8 4.4 %collective-permute-start.11 = (f32[8,128]{1,0:T(8,128)S(1)}, f32[8,128]{1,0:T(8,128)S(1)}, u32[]{:S(2)}, u32[]{:S(2)}) collective-permute-start(f32[8,128]{1,0:T(8,128)S(1)} %add.18), channel_id=1, source_target_pairs={{0,6},{1,7},{2,4},{3,5},{4,2},{5,3},{6,0},{7,1},{8,14},{9,15},{10,... | collective-permute-start | bytes 12296 | tf_op jit(solution)/shard_map/ppermute | solution.py:31

commit v5 on v4

--- a/solution.py
+++ b/solution.py
@@ -31,7 +31,7 @@
     return lax.ppermute(value, AXES, pairs)
 
 
-def neighbour(dim, colour):
+def neighbour(dim, colour, cross):
     sizes = [lax.axis_size(a) for a in AXES]
 
     def partner(place):
@@ -40,6 +40,8 @@
         there = here ^ 1 if colour == 0 else ((here - 1) ^ 1) + 1
         if 0 <= there < sizes[dim]:
             place[dim] = there
+            if cross:
+                place[1] ^= 1
         elif dim != 1 and sizes[1] % 2 == 0:
             place[1] ^= 1
         elif colour == 1 and sizes[dim] % 2 == 0:
@@ -49,11 +51,11 @@
     return partner
 
 
-def exchange(value_even, value_odd, dim):
-    first = pair_swap(value_even, neighbour(dim, 0))
+def exchange(value_even, value_odd, dim, cross=False):
+    first = pair_swap(value_even, neighbour(dim, 0, cross))
     if lax.axis_size(AXES[dim]) == 2:
         return first, first
-    return first, pair_swap(value_odd, neighbour(dim, 1))
+    return first, pair_swap(value_odd, neighbour(dim, 1, cross))
 
 
 def sum_over_devices(value):
@@ -156,28 +158,61 @@
     return jnp.where(near, low, lines_ref[(i + shift) * pitch : (i + shift + 1) * pitch])
 
 
-def fronts_kernel(sizes, b_ref, mix_ref, la_ref, lb_ref, xa_ref, xb_ref):
+def pair_tiles_kernel(sizes, b_ref, out_ref):
     planes, rows, lanes = sizes
+    start = pl.multiple_of(jnp.where(odd("gy"), 0, rows - TILE), TILE)
+    for p in range(planes):
+        plane = b_ref[p]
+        out_ref[p * TILE : (p + 1) * TILE] = b_ref[p, pl.ds(start, TILE)]
+        out_ref[(planes + p) * TILE : (planes + p + 1) * TILE] = turned_lines(
+            plane, plane[0:TILE], lanes
+        )
+
+
+def pair_lines(sizes, mine_ref, theirs_ref):
+    planes, rows, _ = sizes
+    lane = lax.rem(lax.broadcasted_iota(jnp.int32, (TILE, 2 * HALF), 1), HALF)
+    inside = (lane >= TILE) & (lane < TILE + rows)
+    y_odd = odd("gy")
+    up, down = rows, 2 * HALF - rows
+
+    def lines(p):
+        here = slice((planes + p) * TILE, (planes + p + 1) * TILE)
+        mine, theirs = mine_ref[here], theirs_ref[here]
+        beside_mine = pltpu.roll(theirs, jnp.where(y_odd, down, up), 1)
+        beside_theirs = pltpu.roll(mine, jnp.where(y_odd, up, down), 1)
+        return jnp.where(inside, mine, beside_mine), jnp.where(inside, theirs, beside_theirs)
+
+    return lines
+
+
+def own_lines(sizes, b_ref, mix_ref):
+    return lambda p: (turned_lines(b_ref[p], mix_ref[p], sizes[2]),)
+
+
+def fronts_kernel(sizes, paired, b_ref, mix_ref, *refs):
+    planes, rows, _ = sizes
+    la_ref, lb_ref, xa_ref, xb_ref = refs[-4:]
+    lines = pair_lines(sizes, *refs[:2]) if paired else own_lines(sizes, b_ref, mix_ref)
     x_odd = odd("gx")
-    low = [turned_lines(b_ref[p], mix_ref[p], lanes) for p in range(HALO)]
-    high = [turned_lines(b_ref[p], mix_ref[p], lanes) for p in range(planes - HALO, planes)]
     for i in range(HALO):
-        here = pl.ds(i * TILE, TILE)
-        la_ref[here] = jnp.where(x_odd, low[i], high[i])
-        lb_ref[here] = jnp.where(x_odd, high[i], low[i])
+        for n, (low, high) in enumerate(zip(lines(i), lines(planes - HALO + i))):
+            here = pl.ds((n * HALO + i) * TILE, TILE)
+            la_ref[here] = jnp.where(x_odd, low, high)
+            lb_ref[here] = jnp.where(x_odd, high, low)
     for ref, is_low in ((xa_ref, x_odd), (xb_ref, ~x_odd)):
         start = jnp.where(is_low, 0, planes - HALO)
         ref[:, 0:rows] = b_ref[pl.ds(start, HALO)]
         ref[:, rows : rows + TILE] = mix_ref[pl.ds(start, HALO)]
 
 
-def lines_kernel(sizes, b_ref, mix_ref, lines_ref):
-    planes, _, lanes = sizes
-    pitch = lines_ref.shape[0] // TILE
+def lines_kernel(sizes, paired, first_ref, second_ref, *outs):
+    planes = sizes[0]
+    pitch = outs[0].shape[0] // TILE
+    lines = (pair_lines if paired else own_lines)(sizes, first_ref, second_ref)
     for p in range(planes):
-        lines_ref[pl.ds(p + HALO, TILE, stride=pitch)] = turned_lines(
-            b_ref[p], mix_ref[p], lanes
-        )
+        for ref, value in zip(outs, lines(p)):
+            ref[pl.ds(p + HALO, TILE, stride=pitch)] = value
 
 
 def pre_kernel(sizes, b_ref, mix_ref, e1_ref, e2_ref, out_ref, s_ref, k_ref, acc_ref, e0):
@@ -208,16 +243,23 @@
         acc_ref[it] = jnp.where(inner, acc, 0.0)
 
 
-def ends_kernel(sizes, lines_ref, la_ref, lb_ref, strip_ref, send_ref, lines):
+def ends_kernel(sizes, paired, *refs):
     planes = sizes[0]
-    pitch = lines_ref.shape[0] // TILE
+    kinds = 2 if paired else 1
+    la_ref, lb_ref, strip_ref, sa_ref, sb_ref = refs[kinds : kinds + 5]
+    sets = refs[kinds + 5 :]
+    pitch = refs[0].shape[0] // TILE
     near = lax.broadcasted_iota(jnp.int32, (pitch, 2 * HALF), 1) < HALF
-    lines[...] = lines_ref[...]
     low, high = low_high(la_ref[...], lb_ref[...], "gx")
-    for i in range(HALO):
-        here = slice(i * TILE, (i + 1) * TILE)
-        lines[pl.ds(i, TILE, stride=pitch)] = low[here]
-        lines[pl.ds(i + HALO + planes, TILE, stride=pitch)] = high[here]
+    for n in range(kinds):
+        lines = sets[n]
+        lines[...] = refs[n][...]
+        for i in range(HALO):
+            k = (kinds - 1 - n) * HALO + i
+            here = slice(k * TILE, (k + 1) * TILE)
+            lines[pl.ds(i, TILE, stride=pitch)] = low[here]
+            lines[pl.ds(i + HALO + planes, TILE, stride=pitch)] = high[here]
+    lines, given = sets[0], sets[kinds - 1]
     shift = TILE - 2 * HALO
     for j in range(3 * HALO):
         if j < HALO:
@@ -226,8 +268,19 @@
             value = lines[(j - HALO) * pitch : (j - HALO + 1) * pitch]
         else:
             value = middle(lines, j - HALO, pitch, near)
-            send_ref[(j - HALO) * pitch : (j - HALO + 1) * pitch] = value
         strip_ref[j * pitch : (j + 1) * pitch] = value
+    layers = [middle(given, i, pitch, near) for i in range(HALO)]
+    swung = [pltpu.roll(v, HALF, 1) for v in layers]
+    z_odd = odd("gz")
+    for i in range(0, HALO, 2):
+        if i + 1 < HALO:
+            to_low = jnp.where(near, layers[i], swung[i + 1])
+            to_high = jnp.where(near, swung[i], layers[i + 1])
+        else:
+            to_low, to_high = layers[i], swung[i]
+        here = slice(i // 2 * pitch, (i // 2 + 1) * pitch)
+        sa_ref[here] = jnp.where(z_odd, to_low, to_high)
+        sb_ref[here] = jnp.where(z_odd, to_high, to_low)
 
 
 def post_kernel(
@@ -315,19 +368,21 @@
     mine = (x >= 0) & (x < planes) & (y >= 0) & (y < rows)
 
     state = []
+    packs = [
+        low_high(za_ref[n : n + pitch], zb_ref[n : n + pitch], "gz")
+        for n in range(0, za_ref.shape[0], pitch)
+    ]
     for j in range(3 * HALO):
         own = strip_ref[j * pitch : (j + 1) * pitch]
         if j < HALO:
-            got = low_high(
-                za_ref[j * pitch : (j + 1) * pitch], zb_ref[j * pitch : (j + 1) * pitch], "gz"
-            )[0]
-            own = jnp.where(near, pltpu.roll(got, HALF, 1), own)
+            got = packs[j // 2][0]
+            got = got if j % 2 == 0 else pltpu.roll(got, HALF, 1)
+            own = jnp.where(near, got, own)
         elif j >= 2 * HALO:
             i = j - 2 * HALO
-            got = low_high(
-                za_ref[i * pitch : (i + 1) * pitch], zb_ref[i * pitch : (i + 1) * pitch], "gz"
-            )[1]
-            own = jnp.where(near, own, pltpu.roll(got, HALF, 1))
+            got = packs[i // 2][1]
+            got = pltpu.roll(got, HALF, 1) if i % 2 == 0 else got
+            own = jnp.where(near, own, got)
         state.append(own)
     factors = [sign_factors(v) for v in state]
 
@@ -426,34 +481,63 @@
     pitch = -(-wide // TILE) * TILE
 
     def mixed(first, second):
-        if first is second:
-            return first
         low, high = low_high(first, second, "gy")
         sub = lax.broadcasted_iota(jnp.int32, first.shape, 1)
         return jnp.where(sub < TILE // 2, high, low)
 
-    colours = 1 if lax.axis_size("gy") == 2 else 2
-    ys = call(tiles_kernel, sizes, (phi_start,), ((planes, TILE, lanes),) * colours, (), 2, 0.2)
-    mix = mixed(*exchange(ys[0], ys[-1], 1))
-
-    line, front = (HALO * TILE, 2 * HALF), (HALO, tall, lanes)
+    paired = lax.axis_size("gy") == 2
+    kinds = 2 if paired else 1
+    if paired:
+        (mine,) = call(
+            pair_tiles_kernel,
+            sizes,
+            (phi_start,),
+            ((2 * planes * TILE, lanes),),
+            (),
+            2,
+            0.5,
+        )
+        theirs, _ = exchange(mine, mine, 1)
+        mix = theirs[: planes * TILE].reshape(planes, TILE, lanes)
+        front_inputs, line_inputs = (phi_start, mix, mine, theirs), (mine, theirs)
+    else:
+        ys = call(
+            tiles_kernel, sizes, (phi_start,), ((planes, TILE, lanes),) * 2, (), 2, 0.2
+        )
+        mix = mixed(*exchange(ys[0], ys[1], 1))
+        front_inputs = line_inputs = (phi_start, mix)
+
+    def with_kinds(kernel):
+        return lambda sizes, *refs: kernel(sizes, paired, *refs)
+
+    line, front = (kinds * HALO * TILE, 2 * HALF), (HALO, tall, lanes)
     la, lb, xa, xb = call(
-        fronts_kernel, sizes, (phi_start, mix), (line, line, front, front), (), 2, 0.2
-    )
-    la, lb = exchange(la, lb, 0)
+        with_kinds(fronts_kernel),
+        sizes,
+        front_inputs,
+        (line, line, front, front),
+        (),
+        2,
+        0.2,
+    )
+    la, lb = exchange(la, lb, 0, paired)
     xa, xb = exchange(xa, xb, 0)
 
-    (lines,) = call(lines_kernel, sizes, (phi_start, mix), ((TILE * pitch, 2 * HALF),), (), 2, 0.5)
-    strip, send = call(
-        ends_kernel,
+    edge_lines = (TILE * pitch, 2 * HALF)
+    lines = call(
+        with_kinds(lines_kernel), sizes, line_inputs, (edge_lines,) * kinds, (), 2, 0.5
+    )
+    packed = ((HALO + 1) // 2 * pitch, 2 * HALF)
+    strip, sa, sb = call(
+        with_kinds(ends_kernel),
         sizes,
-        (lines, la, lb),
-        ((3 * HALO * pitch, 2 * HALF), (HALO * pitch, 2 * HALF)),
-        ((TILE * pitch, 2 * HALF),),
+        (*lines, la, lb),
+        ((3 * HALO * pitch, 2 * HALF), packed, packed),
+        (edge_lines,) * kinds,
         4,
         0.2,
     )
-    za, zb = exchange(send, send, 2)
+    za, zb = exchange(sa, sb, 2, paired)
 
     block = (planes, tall, lanes)
     e1, e2, inner, s, k, acc = call(

time: 33 us -> 33 us (level)
  waiting for transfers between devices: 9.21 us -> 7.96 us
  starting transfers between devices: 17.1 us -> 18.2 us
    ppermute x12, waiting for transfers between devices: 9.21 us -> 7.96 us  [pair_swap(): return lax.ppermute(value, AXES, pairs)]
    ppermute x12, starting transfers between devices: 17.1 us -> 18.2 us  [pair_swap(): return lax.ppermute(value, AXES, pairs)]
  transfers between devices with their start and end apart: 12 -> 12, of which waited for: 7 -> 6; matrix products, arithmetic and copies ran while one was open for 0% -> 0% of each run, Pallas kernels for 11% -> 11%
where the time goes in v5:
time: 33 us; the launch traced here: 32.8 us
  starting transfers between devices  18.2 us (55%)
  waiting for transfers between devices  7.96 us (24%)
  Pallas kernels  4.27 us (13%)
  local copies, waits for them, and re-layouts  1 us (3%)
  between operations  0.7 us (2%)
  other arithmetic  0.66 us (2%)
    ppermute x12, starting transfers between devices, pair_swap(): return lax.ppermute(value, AXES, pairs)  18.2 us
    ppermute x12, waiting for transfers between devices, pair_swap(): return lax.ppermute(value, AXES, pairs)  7.96 us
    pallas_call x8, Pallas kernels, call(): pl.pallas_call(functools.partial(kernel, sizes), out_shape=tuple((jax.Sha...  4.27 us
    unnamed x4, local copies, waits for them, and re-layouts  0.99 us
  transfers between devices with their start and end apart: 12, of which 6 were waited for; matrix products, arithmetic and copies ran while one was open for 0% of the time, Pallas kernels for 11%

profile of v5, /device:TPU:0, one launch (start us, length us, event | category | flops | bytes accessed | tf_op | source)
XLA Modules:
  0.0 32.8 jit_solution(3868578751441569894)
XLA Ops:
  0.6 1.0 %copy-done = f32[16,48,128]{2,1,0:T(8,128)S(1)} copy-done((f32[16,48,128]{2,1,0:T(8,128)S(1)}, f32[16,48,128]{2,1,0:T(8,128)}, u32[]{:S(2)}) %copy-start) | copy-done | bytes 393240
  1.6 0.4 %shard_map.30.refs_2_.refs_0_ = f32[256,128]{1,0:T(8,128)S(1)} custom-call(f32[16,48,128]{2,1,0:T(8,128)S(1)} %copy-done), custom_call_target="tpu_custom_call" | custom-call | flops 1750000 | bytes 1000000 | tf_op jit(solution)/shard_map/pallas_call | solution.py:465
  2.0 0.5 %collective-permute-start = (f32[256,128]{1,0:T(8,128)S(1)}, f32[256,128]{1,0:T(8,128)S(1)}, u32[]{:S(2)}, u32[]{:S(2)}) collective-permute-start(f32[256,128]{1,0:T(8,128)S(1)} %shard_map.30.refs_2_.refs_0_), channel_id=1, source_target_pairs={{0,4},{1,5},{2,6},{3,7},{4,0},{5,1},{6,2},{7,3},{8,12},{9,13},{10,... | collective-permute-start | bytes 393224 | tf_op jit(solution)/shard_map/ppermute | solution.py:31
  2.6 1.0 %collective-permute-done.refs_3_.refs_1_ = f32[256,128]{1,0:T(8,128)S(1)} collective-permute-done((f32[256,128]{1,0:T(8,128)S(1)}, f32[256,128]{1,0:T(8,128)S(1)}, u32[]{:S(2)}, u32[]{:S(2)}) %collective-permute-start) | collective-permute-done | bytes 131104 | tf_op jit(solution)/shard_map/ppermute | solution.py:31
  3.6 0.1 shard_map.32
  3.7 2.9 %collective-permute-start.1 = (f32[3,56,128]{2,1,0:T(8,128)S(1)}, f32[3,56,128]{2,1,0:T(8,128)S(1)}, u32[]{:S(2)}, u32[]{:S(2)}) collective-permute-start(f32[3,56,128]{2,1,0:T(8,128)S(1)} %get-tuple-element.22), channel_id=1, source_target_pairs={{0,8},{1,9},{2,10},{3,11},{4,12},{5,13},{6,14},{7,15},{8,0},{9,1},... | collective-permute-start | bytes 258056 | tf_op jit(solution)/shard_map/ppermute | solution.py:31
  6.6 2.2 %collective-permute-start.3 = (f32[48,128]{1,0:T(8,128)S(1)}, f32[48,128]{1,0:T(8,128)S(1)}, u32[]{:S(2)}, u32[]{:S(2)}) collective-permute-start(f32[48,128]{1,0:T(8,128)S(1)} %get-tuple-element.32), channel_id=1, source_target_pairs={{0,12},{1,13},{2,14},{3,15},{4,8},{5,9},{6,10},{7,11},{8,4},{9,5},... | collective-permute-start | bytes 73736 | tf_op jit(solution)/shard_map/ppermute | solution.py:31
  8.7 0.9 %collective-permute-start.4 = (f32[48,128]{1,0:T(8,128)S(1)}, f32[48,128]{1,0:T(8,128)S(1)}, u32[]{:S(2)}, u32[]{:S(2)}) collective-permute-start(f32[48,128]{1,0:T(8,128)S(1)} %get-tuple-element.33), channel_id=1, source_target_pairs={{0,4},{1,5},{2,6},{3,7},{4,0},{5,1},{6,2},{7,3},{8,20},{9,21},{10,... | collective-permute-start | bytes 73736 | tf_op jit(solution)/shard_map/ppermute | solution.py:31
  9.7 0.1 shard_map.34
  9.8 1.5 %collective-permute-done.3.refs_2_ = f32[48,128]{1,0:T(8,128)S(1)} collective-permute-done((f32[48,128]{1,0:T(8,128)S(1)}, f32[48,128]{1,0:T(8,128)S(1)}, u32[]{:S(2)}, u32[]{:S(2)}) %collective-permute-start.3) | collective-permute-done | bytes 24608 | tf_op jit(solution)/shard_map/ppermute | solution.py:31
  11.2 0.0 collective-permute-done.4.refs_3_
  11.2 0.1 shard_map.35
  11.3 2.4 %collective-permute-start.5 = (f32[48,128]{1,0:T(8,128)S(1)}, f32[48,128]{1,0:T(8,128)S(1)}, u32[]{:S(2)}, u32[]{:S(2)}) collective-permute-start(f32[48,128]{1,0:T(8,128)S(1)} %get-tuple-element.35), channel_id=1, source_target_pairs={{0,5},{1,4},{2,7},{3,6},{4,1},{5,0},{6,3},{7,2},{8,13},{9,12},{10,... | collective-permute-start | bytes 73736 | tf_op jit(solution)/shard_map/ppermute | solution.py:31
  13.8 0.0 collective-permute-start.6
  13.8 1.4 %shard_map.31 = (f32[16,56,128]{2,1,0:T(8,128)S(1)}, f32[16,56,128]{2,1,0:T(8,128)S(1)}, f32[16,48,128]{2,1,0:T(8,128)S(1)}, f32[16,56,128]{2,1,0:T(8,128)S(1)},...) custom-call(f32[16,48,128]{2,1,0:T(8,128)S(1)} %copy-done.1, f32[16,8,128]{2,1,0:T(8,128)S(1)} %slice_bitcast_fusion.mix_ref.refs_1_), custom_call_target="tpu_custom_call" | custom-call | flops 5250000 | bytes 1000000 | tf_op jit(solution)/shard_map/pallas_call | solution.py:465
  15.1 0.6 %shard_map.33 = (f32[6,48,128]{2,1,0:T(8,128)S(1)}, f32[3,8,128]{2,1,0:T(8,128)S(1)}) custom-call(f32[16,48,128]{2,1,0:T(8,128)S(1)} %copy-done.1, f32[16,8,128]{2,1,0:T(8,128)S(1)} %slice_bitcast_fusion.mix_ref.refs_1_, f32[3,56,128]{2,1,0:T(8,128)S(1)} %collective-permute-done.1.xa_ref, f32[3,56,128]{2,1,0:T(8,128)S(1)} %collective-permute-done.2.xb_ref, ...), custom_call_target="tpu_custom_call" | custom-call | flops 2100000 | bytes 1000000 | tf_op jit(solution)/shard_map/pallas_call | solution.py:465
  15.8 0.0 collective-permute-done.5.za_ref
  15.8 0.0 collective-permute-done.6.zb_ref
  15.8 0.3 shard_map.36
  16.1 0.6 %collective-permute-start.7 = (f32[8,128]{1,0:T(8,128)S(1)}, f32[8,128]{1,0:T(8,128)S(1)}, u32[]{:S(2)}, u32[]{:S(2)}) collective-permute-start(f32[8,128]{1,0:T(8,128)S(1)} %get-tuple-element.39), channel_id=1, source_target_pairs={{0,4},{1,5},{2,6},{3,7},{4,0},{5,1},{6,2},{7,3},{8,12},{9,13},{10,... | collective-permute-start | bytes 12296 | tf_op jit(solution)/shard_map/ppermute | solution.py:31
  16.7 0.8 %collective-permute-done.7 = f32[8,128]{1,0:T(8,128)S(1)} collective-permute-done((f32[8,128]{1,0:T(8,128)S(1)}, f32[8,128]{1,0:T(8,128)S(1)}, u32[]{:S(2)}, u32[]{:S(2)}) %collective-permute-start.7) | collective-permute-done | bytes 4128 | tf_op jit(solution)/shard_map/ppermute | solution.py:31
  17.5 2.3 %collective-permute-start.8 = (f32[8,128]{1,0:T(8,128)S(1)}, f32[8,128]{1,0:T(8,128)S(1)}, u32[]{:S(2)}, u32[]{:S(2)}) collective-permute-start(f32[8,128]{1,0:T(8,128)S(1)} %add.15), channel_id=1, source_target_pairs={{0,12},{1,13},{2,14},{3,15},{4,8},{5,9},{6,10},{7,11},{8,4},{9,5},... | collective-permute-start | bytes 12296 | tf_op jit(solution)/shard_map/ppermute | solution.py:31
  19.8 1.3 %collective-permute-done.8 = f32[8,128]{1,0:T(8,128)S(1)} collective-permute-done((f32[8,128]{1,0:T(8,128)S(1)}, f32[8,128]{1,0:T(8,128)S(1)}, u32[]{:S(2)}, u32[]{:S(2)}) %collective-permute-start.8) | collective-permute-done | bytes 4128 | tf_op jit(solution)/shard_map/ppermute | solution.py:31
  21.1 1.0 %collective-permute-start.9 = (f32[8,128]{1,0:T(8,128)S(1)}, f32[8,128]{1,0:T(8,128)S(1)}, u32[]{:S(2)}, u32[]{:S(2)}) collective-permute-start(f32[8,128]{1,0:T(8,128)S(1)} %add.16), channel_id=1, source_target_pairs={{0,20},{1,21},{2,22},{3,23},{4,16},{5,17},{6,18},{7,19},{8,28},{9,... | collective-permute-start | bytes 12296 | tf_op jit(solution)/shard_map/ppermute | solution.py:31
  22.2 2.0 %collective-permute-done.9 = f32[8,128]{1,0:T(8,128)S(1)} collective-permute-done((f32[8,128]{1,0:T(8,128)S(1)}, f32[8,128]{1,0:T(8,128)S(1)}, u32[]{:S(2)}, u32[]{:S(2)}) %collective-permute-start.9) | collective-permute-done | bytes 4128 | tf_op jit(solution)/shard_map/ppermute | solution.py:31
  24.2 2.5 %collective-permute-start.10 = (f32[8,128]{1,0:T(8,128)S(1)}, f32[8,128]{1,0:T(8,128)S(1)}, u32[]{:S(2)}, u32[]{:S(2)}) collective-permute-start(f32[8,128]{1,0:T(8,128)S(1)} %add.17), channel_id=1, source_target_pairs={{0,5},{1,4},{2,7},{3,6},{4,1},{5,0},{6,3},{7,2},{8,13},{9,12},{10,... | collective-permute-start | bytes 12296 | tf_op jit(solution)/shard_map/ppermute | solution.py:31
  26.7 1.3 %collective-permute-done.10 = f32[8,128]{1,0:T(8,128)S(1)} collective-permute-done((f32[8,128]{1,0:T(8,128)S(1)}, f32[8,128]{1,0:T(8,128)S(1)}, u32[]{:S(2)}, u32[]{:S(2)}) %collective-permute-start.10) | collective-permute-done | bytes 4128 | tf_op jit(solution)/shard_map/ppermute | solution.py:31
  28.0 2.8 %collective-permute-start.11 = (f32[8,128]{1,0:T(8,128)S(1)}, f32[8,128]{1,0:T(8,128)S(1)}, u32[]{:S(2)}, u32[]{:S(2)}) collective-permute-start(f32[8,128]{1,0:T(8,128)S(1)} %add.18), channel_id=1, source_target_pairs={{0,6},{1,7},{2,4},{3,5},{4,2},{5,3},{6,0},{7,1},{8,14},{9,15},{10,... | collective-permute-start | bytes 12296 | tf_op jit(solution)/shard_map/ppermute | solution.py:31
  30.8 1.3 %shard_map.37 = f32[16,48,128]{2,1,0:T(8,128)} custom-call(f32[16,48,128]{2,1,0:T(8,128)S(1)} %get-tuple-element.21.main_ref, f32[6,48,128]{2,1,0:T(8,128)S(1)} %get-tuple-element.29.ends_ref, f32[72,128]{1,0:T(8,128)S(1)} %get-tuple-element.38.edge_ref), custom_call_target="tpu_custom_call" | custom-call | flops 5250000 | bytes 1000000 | tf_op jit(solution)/shard_map/pallas_call | solution.py:465
  32.1 0.0 collective-permute-done.11
  32.2 0.1 slice_reduce_fusion
  32.3 0.5 %sqrt_multiply_fusion = f32[3]{0:T(128)} fusion(f32[3]{0:T(128)S(1)} %slice_reduce_fusion), kind=kLoop, calls=%fused_computation.2 | loop fusion | flops 6 | bytes 24 | tf_op jit(solution)/shard_map/div | solution.py:578
  (12 shorter events, 0.0 us)
Async XLA Ops:
  0.6 1.0 %copy-start = (f32[16,48,128]{2,1,0:T(8,128)S(1)}, f32[16,48,128]{2,1,0:T(8,128)}, u32[]{:S(2)}) copy-start(f32[16,48,128]{2,1,0:T(8,128)} %b_ref.5) | copy-start | bytes 1179652
  1.6 1.9 %copy-start.1 = (f32[16,48,128]{2,1,0:T(8,128)S(1)}, f32[16,48,128]{2,1,0:T(8,128)}, u32[]{:S(2)}) copy-start(f32[16,48,128]{2,1,0:T(8,128)} %b_ref.5) | copy-start | bytes 1179652
  2.0 1.5 %collective-permute-start = (f32[256,128]{1,0:T(8,128)S(1)}, f32[256,128]{1,0:T(8,128)S(1)}, u32[]{:S(2)}, u32[]{:S(2)}) collective-permute-start(f32[256,128]{1,0:T(8,128)S(1)} %shard_map.30.refs_2_.refs_0_), channel_id=1, source_target_pairs={{0,4},{1,5},{2,6},{3,7},{4,0},{5,1},{6,2},{7,3},{8,12},{9,13},{10,... | collective-permute-start | bytes 393224 | tf_op jit(solution)/shard_map/ppermute | solution.py:31
  3.7 11.5 %collective-permute-start.1 = (f32[3,56,128]{2,1,0:T(8,128)S(1)}, f32[3,56,128]{2,1,0:T(8,128)S(1)}, u32[]{:S(2)}, u32[]{:S(2)}) collective-permute-start(f32[3,56,128]{2,1,0:T(8,128)S(1)} %get-tuple-element.22), channel_id=1, source_target_pairs={{0,8},{1,9},{2,10},{3,11},{4,12},{5,13},{6,14},{7,15},{8,0},{9,1},... | collective-permute-start | bytes 258056 | tf_op jit(solution)/shard_map/ppermute | solution.py:31
  6.6 8.6 %collective-permute-start.2 = (f32[3,56,128]{2,1,0:T(8,128)S(1)}, f32[3,56,128]{2,1,0:T(8,128)S(1)}, u32[]{:S(2)}, u32[]{:S(2)}) collective-permute-start(f32[3,56,128]{2,1,0:T(8,128)S(1)} %get-tuple-element.23), channel_id=1, source_target_pairs={{0,4},{1,5},{2,6},{3,7},{4,0},{5,1},{6,2},{7,3},{8,16},{9,17},{10,... | collective-permute-start | bytes 258056 | tf_op jit(solution)/shard_map/ppermute | solution.py:31
  6.6 4.7 %collective-permute-start.3 = (f32[48,128]{1,0:T(8,128)S(1)}, f32[48,128]{1,0:T(8,128)S(1)}, u32[]{:S(2)}, u32[]{:S(2)}) collective-permute-start(f32[48,128]{1,0:T(8,128)S(1)} %get-tuple-element.32), channel_id=1, source_target_pairs={{0,12},{1,13},{2,14},{3,15},{4,8},{5,9},{6,10},{7,11},{8,4},{9,5},... | collective-permute-start | bytes 73736 | tf_op jit(solution)/shard_map/ppermute | solution.py:31
  8.7 2.5 %collective-permute-start.4 = (f32[48,128]{1,0:T(8,128)S(1)}, f32[48,128]{1,0:T(8,128)S(1)}, u32[]{:S(2)}, u32[]{:S(2)}) collective-permute-start(f32[48,128]{1,0:T(8,128)S(1)} %get-tuple-element.33), channel_id=1, source_target_pairs={{0,4},{1,5},{2,6},{3,7},{4,0},{5,1},{6,2},{7,3},{8,20},{9,21},{10,... | collective-permute-start | bytes 73736 | tf_op jit(solution)/shard_map/ppermute | solution.py:31
  11.3 4.4 %collective-permute-start.5 = (f32[48,128]{1,0:T(8,128)S(1)}, f32[48,128]{1,0:T(8,128)S(1)}, u32[]{:S(2)}, u32[]{:S(2)}) collective-permute-start(f32[48,128]{1,0:T(8,128)S(1)} %get-tuple-element.35), channel_id=1, source_target_pairs={{0,5},{1,4},{2,7},{3,6},{4,1},{5,0},{6,3},{7,2},{8,13},{9,12},{10,... | collective-permute-start | bytes 73736 | tf_op jit(solution)/shard_map/ppermute | solution.py:31
  13.8 2.0 %collective-permute-start.6 = (f32[48,128]{1,0:T(8,128)S(1)}, f32[48,128]{1,0:T(8,128)S(1)}, u32[]{:S(2)}, u32[]{:S(2)}) collective-permute-start(f32[48,128]{1,0:T(8,128)S(1)} %get-tuple-element.36), channel_id=1, source_target_pairs={{0,4},{1,6},{2,5},{3,7},{4,0},{5,2},{6,1},{7,3},{8,12},{9,14},{10,... | collective-permute-start | bytes 73736 | tf_op jit(solution)/shard_map/ppermute | solution.py:31
  16.1 1.4 %collective-permute-start.7 = (f32[8,128]{1,0:T(8,128)S(1)}, f32[8,128]{1,0:T(8,128)S(1)}, u32[]{:S(2)}, u32[]{:S(2)}) collective-permute-start(f32[8,128]{1,0:T(8,128)S(1)} %get-tuple-element.39), channel_id=1, source_target_pairs={{0,4},{1,5},{2,6},{3,7},{4,0},{5,1},{6,2},{7,3},{8,12},{9,13},{10,... | collective-permute-start | bytes 12296 | tf_op jit(solution)/shard_map/ppermute | solution.py:31
  17.5 3.7 %collective-permute-start.8 = (f32[8,128]{1,0:T(8,128)S(1)}, f32[8,128]{1,0:T(8,128)S(1)}, u32[]{:S(2)}, u32[]{:S(2)}) collective-permute-start(f32[8,128]{1,0:T(8,128)S(1)} %add.15), channel_id=1, source_target_pairs={{0,12},{1,13},{2,14},{3,15},{4,8},{5,9},{6,10},{7,11},{8,4},{9,5},... | collective-permute-start | bytes 12296 | tf_op jit(solution)/shard_map/ppermute | solution.py:31
  21.1 3.0 %collective-permute-start.9 = (f32[8,128]{1,0:T(8,128)S(1)}, f32[8,128]{1,0:T(8,128)S(1)}, u32[]{:S(2)}, u32[]{:S(2)}) collective-permute-start(f32[8,128]{1,0:T(8,128)S(1)} %add.16), channel_id=1, source_target_pairs={{0,20},{1,21},{2,22},{3,23},{4,16},{5,17},{6,18},{7,19},{8,28},{9,... | collective-permute-start | bytes 12296 | tf_op jit(solution)/shard_map/ppermute | solution.py:31
  24.2 3.8 %collective-permute-start.10 = (f32[8,128]{1,0:T(8,128)S(1)}, f32[8,128]{1,0:T(8,128)S(1)}, u32[]{:S(2)}, u32[]{:S(2)}) collective-permute-start(f32[8,128]{1,0:T(8,128)S(1)} %add.17), channel_id=1, source_target_pairs={{0,5},{1,4},{2,7},{3,6},{4,1},{5,0},{6,3},{7,2},{8,13},{9,12},{10,... | collective-permute-start | bytes 12296 | tf_op jit(solution)/shard_map/ppermute | solution.py:31
  28.0 4.2 %collective-permute-start.11 = (f32[8,128]{1,0:T(8,128)S(1)}, f32[8,128]{1,0:T(8,128)S(1)}, u32[]{:S(2)}, u32[]{:S(2)}) collective-permute-start(f32[8,128]{1,0:T(8,128)S(1)} %add.18), channel_id=1, source_target_pairs={{0,6},{1,7},{2,4},{3,5},{4,2},{5,3},{6,0},{7,1},{8,14},{9,15},{10,... | collective-permute-start | bytes 12296 | tf_op jit(solution)/shard_map/ppermute | solution.py:31

commit v6 on v5

--- a/solution.py
+++ b/solution.py
@@ -200,10 +200,15 @@
             here = pl.ds((n * HALO + i) * TILE, TILE)
             la_ref[here] = jnp.where(x_odd, low, high)
             lb_ref[here] = jnp.where(x_odd, high, low)
+    sub = lax.broadcasted_iota(jnp.int32, mix_ref.shape[1:], 0)
     for ref, is_low in ((xa_ref, x_odd), (xb_ref, ~x_odd)):
         start = jnp.where(is_low, 0, planes - HALO)
-        ref[:, 0:rows] = b_ref[pl.ds(start, HALO)]
-        ref[:, rows : rows + TILE] = mix_ref[pl.ds(start, HALO)]
+        for i in range(HALO):
+            ref[i * rows : (i + 1) * rows] = b_ref[start + i]
+        nearest = mix_ref[jnp.where(is_low, 0, planes - 1)]
+        second = mix_ref[jnp.where(is_low, 1, planes - 2)]
+        nearest = jnp.where(sub == 3, second[0:1], nearest)
+        ref[HALO * rows :] = jnp.where(sub == 4, second[TILE - 1 : TILE], nearest)
 
 
 def lines_kernel(sizes, paired, first_ref, second_ref, *outs):
@@ -304,13 +309,21 @@
     marks = plane_marks(sizes)
     lane = lax.broadcasted_iota(jnp.int32, (TILE, lanes), 1)
     inner = (lane >= HALO) & (lane < lanes - HALO)
+    sub = lax.broadcasted_iota(jnp.int32, mix_ref.shape[1:], 0)
     factors = {}
 
     def start(p):
         if 0 <= p < planes:
             return jnp.concatenate([b_ref[p], mix_ref[p]], axis=0)
         i = p + HALO if p < 0 else p - planes
-        return low_high(xa_ref[i], xb_ref[i], "gx")[0 if p < 0 else 1]
+        side = 0 if p < 0 else 1
+        low_rows = HALO * rows
+        own = low_high(xa_ref[i * rows : (i + 1) * rows], xb_ref[i * rows : (i + 1) * rows], "gx")
+        tile = low_high(xa_ref[low_rows : low_rows + TILE], xb_ref[low_rows : low_rows + TILE], "gx")
+        tile = tile[side]
+        if i == 1:
+            tile = jnp.where(sub < TILE // 2, tile[3:4], tile[4:5])
+        return jnp.concatenate([own[side], tile], axis=0)
 
     def factor(p):
         if 0 <= p < planes:
@@ -510,7 +523,7 @@
     def with_kinds(kernel):
         return lambda sizes, *refs: kernel(sizes, paired, *refs)
 
-    line, front = (kinds * HALO * TILE, 2 * HALF), (HALO, tall, lanes)
+    line, front = (kinds * HALO * TILE, 2 * HALF), (HALO * rows + TILE, lanes)
     la, lb, xa, xb = call(
         with_kinds(fronts_kernel),
         sizes,

time: 33 us -> 32.5 us (0.985)
  waiting for transfers between devices: 7.96 us -> 7.62 us
    ppermute x12, waiting for transfers between devices: 7.96 us -> 7.62 us  [pair_swap(): return lax.ppermute(value, AXES, pairs)]
where the time goes in v6:
time: 32.5 us; the launch traced here: 32.3 us
  starting transfers between devices  18.1 us (56%)
  waiting for transfers between devices  7.62 us (23%)
  Pallas kernels  4.28 us (13%)
  local copies, waits for them, and re-layouts  1 us (3%)
  between operations  0.7 us (2%)
  other arithmetic  0.66 us (2%)
    ppermute x12, starting transfers between devices, pair_swap(): return lax.ppermute(value, AXES, pairs)  18.1 us
    ppermute x12, waiting for transfers between devices, pair_swap(): return lax.ppermute(value, AXES, pairs)  7.62 us
    pallas_call x8, Pallas kernels, call(): pl.pallas_call(functools.partial(kernel, sizes), out_shape=tuple((jax.Sha...  4.28 us
    unnamed x4, local copies, waits for them, and re-layouts  0.99 us
  transfers between devices with their start and end apart: 12, of which 6 were waited for; matrix products, arithmetic and copies ran while one was open for 0% of the time, Pallas kernels for 11%

profile of v6, /device:TPU:0, one launch (start us, length us, event | category | flops | bytes accessed | tf_op | source)
XLA Modules:
  0.0 32.3 jit_solution(2046933724485037768)
XLA Ops:
  0.6 1.0 %copy-done = f32[16,48,128]{2,1,0:T(8,128)S(1)} copy-done((f32[16,48,128]{2,1,0:T(8,128)S(1)}, f32[16,48,128]{2,1,0:T(8,128)}, u32[]{:S(2)}) %copy-start) | copy-done | bytes 393240
  1.6 0.4 %shard_map.30.refs_2_.refs_0_ = f32[256,128]{1,0:T(8,128)S(1)} custom-call(f32[16,48,128]{2,1,0:T(8,128)S(1)} %copy-done), custom_call_target="tpu_custom_call" | custom-call | flops 1750000 | bytes 1000000 | tf_op jit(solution)/shard_map/pallas_call | solution.py:478
  2.0 0.5 %collective-permute-start = (f32[256,128]{1,0:T(8,128)S(1)}, f32[256,128]{1,0:T(8,128)S(1)}, u32[]{:S(2)}, u32[]{:S(2)}) collective-permute-start(f32[256,128]{1,0:T(8,128)S(1)} %shard_map.30.refs_2_.refs_0_), channel_id=1, source_target_pairs={{0,4},{1,5},{2,6},{3,7},{4,0},{5,1},{6,2},{7,3},{8,12},{9,13},{10,... | collective-permute-start | bytes 393224 | tf_op jit(solution)/shard_map/ppermute | solution.py:31
  2.6 1.0 %collective-permute-done.refs_3_.refs_1_ = f32[256,128]{1,0:T(8,128)S(1)} collective-permute-done((f32[256,128]{1,0:T(8,128)S(1)}, f32[256,128]{1,0:T(8,128)S(1)}, u32[]{:S(2)}, u32[]{:S(2)}) %collective-permute-start) | collective-permute-done | bytes 131104 | tf_op jit(solution)/shard_map/ppermute | solution.py:31
  3.6 0.1 shard_map.32
  3.7 2.9 %collective-permute-start.1 = (f32[152,128]{1,0:T(8,128)S(1)}, f32[152,128]{1,0:T(8,128)S(1)}, u32[]{:S(2)}, u32[]{:S(2)}) collective-permute-start(f32[152,128]{1,0:T(8,128)S(1)} %get-tuple-element.22), channel_id=1, source_target_pairs={{0,8},{1,9},{2,10},{3,11},{4,12},{5,13},{6,14},{7,15},{8,0},{9,1},... | collective-permute-start | bytes 233480 | tf_op jit(solution)/shard_map/ppermute | solution.py:31
  6.6 0.0 collective-permute-start.2
  6.6 2.2 %collective-permute-start.3 = (f32[48,128]{1,0:T(8,128)S(1)}, f32[48,128]{1,0:T(8,128)S(1)}, u32[]{:S(2)}, u32[]{:S(2)}) collective-permute-start(f32[48,128]{1,0:T(8,128)S(1)} %get-tuple-element.32), channel_id=1, source_target_pairs={{0,12},{1,13},{2,14},{3,15},{4,8},{5,9},{6,10},{7,11},{8,4},{9,5},... | collective-permute-start | bytes 73736 | tf_op jit(solution)/shard_map/ppermute | solution.py:31
  8.7 0.9 %collective-permute-start.4 = (f32[48,128]{1,0:T(8,128)S(1)}, f32[48,128]{1,0:T(8,128)S(1)}, u32[]{:S(2)}, u32[]{:S(2)}) collective-permute-start(f32[48,128]{1,0:T(8,128)S(1)} %get-tuple-element.33), channel_id=1, source_target_pairs={{0,4},{1,5},{2,6},{3,7},{4,0},{5,1},{6,2},{7,3},{8,20},{9,21},{10,... | collective-permute-start | bytes 73736 | tf_op jit(solution)/shard_map/ppermute | solution.py:31
  9.7 0.1 shard_map.34
  9.8 1.3 %collective-permute-done.3.refs_2_ = f32[48,128]{1,0:T(8,128)S(1)} collective-permute-done((f32[48,128]{1,0:T(8,128)S(1)}, f32[48,128]{1,0:T(8,128)S(1)}, u32[]{:S(2)}, u32[]{:S(2)}) %collective-permute-start.3) | collective-permute-done | bytes 24608 | tf_op jit(solution)/shard_map/ppermute | solution.py:31
  11.1 0.0 collective-permute-done.4.refs_3_
  11.1 0.1 shard_map.35
  11.2 2.4 %collective-permute-start.5 = (f32[48,128]{1,0:T(8,128)S(1)}, f32[48,128]{1,0:T(8,128)S(1)}, u32[]{:S(2)}, u32[]{:S(2)}) collective-permute-start(f32[48,128]{1,0:T(8,128)S(1)} %get-tuple-element.35), channel_id=1, source_target_pairs={{0,5},{1,4},{2,7},{3,6},{4,1},{5,0},{6,3},{7,2},{8,13},{9,12},{10,... | collective-permute-start | bytes 73736 | tf_op jit(solution)/shard_map/ppermute | solution.py:31
  13.6 1.4 %shard_map.31 = (f32[16,56,128]{2,1,0:T(8,128)S(1)}, f32[16,56,128]{2,1,0:T(8,128)S(1)}, f32[16,48,128]{2,1,0:T(8,128)S(1)}, f32[16,56,128]{2,1,0:T(8,128)S(1)},...) custom-call(f32[16,48,128]{2,1,0:T(8,128)S(1)} %copy-done.1, f32[16,8,128]{2,1,0:T(8,128)S(1)} %slice_bitcast_fusion.mix_ref.refs_1_), custom_call_target="tpu_custom_call" | custom-call | flops 5250000 | bytes 1000000 | tf_op jit(solution)/shard_map/pallas_call | solution.py:478
  15.0 0.0 collective-permute-done.2.xb_ref
  15.0 0.6 %shard_map.33 = (f32[6,48,128]{2,1,0:T(8,128)S(1)}, f32[3,8,128]{2,1,0:T(8,128)S(1)}) custom-call(f32[16,48,128]{2,1,0:T(8,128)S(1)} %copy-done.1, f32[16,8,128]{2,1,0:T(8,128)S(1)} %slice_bitcast_fusion.mix_ref.refs_1_, f32[152,128]{1,0:T(8,128)S(1)} %collective-permute-done.1.xa_ref, f32[152,128]{1,0:T(8,128)S(1)} %collective-permute-done.2.xb_ref, ...), custom_call_target="tpu_custom_call" | custom-call | flops 2100000 | bytes 1000000 | tf_op jit(solution)/shard_map/pallas_call | solution.py:478
  15.6 0.0 collective-permute-done.5.za_ref
  15.6 0.3 shard_map.36
  15.9 0.6 %collective-permute-start.7 = (f32[8,128]{1,0:T(8,128)S(1)}, f32[8,128]{1,0:T(8,128)S(1)}, u32[]{:S(2)}, u32[]{:S(2)}) collective-permute-start(f32[8,128]{1,0:T(8,128)S(1)} %get-tuple-element.39), channel_id=1, source_target_pairs={{0,4},{1,5},{2,6},{3,7},{4,0},{5,1},{6,2},{7,3},{8,12},{9,13},{10,... | collective-permute-start | bytes 12296 | tf_op jit(solution)/shard_map/ppermute | solution.py:31
  16.5 0.8 %collective-permute-done.7 = f32[8,128]{1,0:T(8,128)S(1)} collective-permute-done((f32[8,128]{1,0:T(8,128)S(1)}, f32[8,128]{1,0:T(8,128)S(1)}, u32[]{:S(2)}, u32[]{:S(2)}) %collective-permute-start.7) | collective-permute-done | bytes 4128 | tf_op jit(solution)/shard_map/ppermute | solution.py:31
  17.3 2.1 %collective-permute-start.8 = (f32[8,128]{1,0:T(8,128)S(1)}, f32[8,128]{1,0:T(8,128)S(1)}, u32[]{:S(2)}, u32[]{:S(2)}) collective-permute-start(f32[8,128]{1,0:T(8,128)S(1)} %add.15), channel_id=1, source_target_pairs={{0,12},{1,13},{2,14},{3,15},{4,8},{5,9},{6,10},{7,11},{8,4},{9,5},... | collective-permute-start | bytes 12296 | tf_op jit(solution)/shard_map/ppermute | solution.py:31
  19.5 1.3 %collective-permute-done.8 = f32[8,128]{1,0:T(8,128)S(1)} collective-permute-done((f32[8,128]{1,0:T(8,128)S(1)}, f32[8,128]{1,0:T(8,128)S(1)}, u32[]{:S(2)}, u32[]{:S(2)}) %collective-permute-start.8) | collective-permute-done | bytes 4128 | tf_op jit(solution)/shard_map/ppermute | solution.py:31
  20.8 1.2 %collective-permute-start.9 = (f32[8,128]{1,0:T(8,128)S(1)}, f32[8,128]{1,0:T(8,128)S(1)}, u32[]{:S(2)}, u32[]{:S(2)}) collective-permute-start(f32[8,128]{1,0:T(8,128)S(1)} %add.16), channel_id=1, source_target_pairs={{0,20},{1,21},{2,22},{3,23},{4,16},{5,17},{6,18},{7,19},{8,28},{9,... | collective-permute-start | bytes 12296 | tf_op jit(solution)/shard_map/ppermute | solution.py:31
  22.0 1.8 %collective-permute-done.9 = f32[8,128]{1,0:T(8,128)S(1)} collective-permute-done((f32[8,128]{1,0:T(8,128)S(1)}, f32[8,128]{1,0:T(8,128)S(1)}, u32[]{:S(2)}, u32[]{:S(2)}) %collective-permute-start.9) | collective-permute-done | bytes 4128 | tf_op jit(solution)/shard_map/ppermute | solution.py:31
  23.8 2.5 %collective-permute-start.10 = (f32[8,128]{1,0:T(8,128)S(1)}, f32[8,128]{1,0:T(8,128)S(1)}, u32[]{:S(2)}, u32[]{:S(2)}) collective-permute-start(f32[8,128]{1,0:T(8,128)S(1)} %add.17), channel_id=1, source_target_pairs={{0,5},{1,4},{2,7},{3,6},{4,1},{5,0},{6,3},{7,2},{8,13},{9,12},{10,... | collective-permute-start | bytes 12296 | tf_op jit(solution)/shard_map/ppermute | solution.py:31
  26.3 1.3 %collective-permute-done.10 = f32[8,128]{1,0:T(8,128)S(1)} collective-permute-done((f32[8,128]{1,0:T(8,128)S(1)}, f32[8,128]{1,0:T(8,128)S(1)}, u32[]{:S(2)}, u32[]{:S(2)}) %collective-permute-start.10) | collective-permute-done | bytes 4128 | tf_op jit(solution)/shard_map/ppermute | solution.py:31
  27.7 2.7 %collective-permute-start.11 = (f32[8,128]{1,0:T(8,128)S(1)}, f32[8,128]{1,0:T(8,128)S(1)}, u32[]{:S(2)}, u32[]{:S(2)}) collective-permute-start(f32[8,128]{1,0:T(8,128)S(1)} %add.18), channel_id=1, source_target_pairs={{0,6},{1,7},{2,4},{3,5},{4,2},{5,3},{6,0},{7,1},{8,14},{9,15},{10,... | collective-permute-start | bytes 12296 | tf_op jit(solution)/shard_map/ppermute | solution.py:31
  30.4 1.3 %shard_map.37 = f32[16,48,128]{2,1,0:T(8,128)} custom-call(f32[16,48,128]{2,1,0:T(8,128)S(1)} %get-tuple-element.21.main_ref, f32[6,48,128]{2,1,0:T(8,128)S(1)} %get-tuple-element.29.ends_ref, f32[72,128]{1,0:T(8,128)S(1)} %get-tuple-element.38.edge_ref), custom_call_target="tpu_custom_call" | custom-call | flops 5250000 | bytes 1000000 | tf_op jit(solution)/shard_map/pallas_call | solution.py:478
  31.6 0.0 collective-permute-done.11
  31.7 0.1 slice_reduce_fusion
  31.8 0.5 %sqrt_multiply_fusion = f32[3]{0:T(128)} fusion(f32[3]{0:T(128)S(1)} %slice_reduce_fusion), kind=kLoop, calls=%fused_computation.2 | loop fusion | flops 6 | bytes 24 | tf_op jit(solution)/shard_map/div | solution.py:591
  (12 shorter events, 0.0 us)
Async XLA Ops:
  0.6 1.0 %copy-start = (f32[16,48,128]{2,1,0:T(8,128)S(1)}, f32[16,48,128]{2,1,0:T(8,128)}, u32[]{:S(2)}) copy-start(f32[16,48,128]{2,1,0:T(8,128)} %b_ref.5) | copy-start | bytes 1179652
  1.6 1.9 %copy-start.1 = (f32[16,48,128]{2,1,0:T(8,128)S(1)}, f32[16,48,128]{2,1,0:T(8,128)}, u32[]{:S(2)}) copy-start(f32[16,48,128]{2,1,0:T(8,128)} %b_ref.5) | copy-start | bytes 1179652
  2.0 1.5 %collective-permute-start = (f32[256,128]{1,0:T(8,128)S(1)}, f32[256,128]{1,0:T(8,128)S(1)}, u32[]{:S(2)}, u32[]{:S(2)}) collective-permute-start(f32[256,128]{1,0:T(8,128)S(1)} %shard_map.30.refs_2_.refs_0_), channel_id=1, source_target_pairs={{0,4},{1,5},{2,6},{3,7},{4,0},{5,1},{6,2},{7,3},{8,12},{9,13},{10,... | collective-permute-start | bytes 393224 | tf_op jit(solution)/shard_map/ppermute | solution.py:31
  3.7 11.3 %collective-permute-start.1 = (f32[152,128]{1,0:T(8,128)S(1)}, f32[152,128]{1,0:T(8,128)S(1)}, u32[]{:S(2)}, u32[]{:S(2)}) collective-permute-start(f32[152,128]{1,0:T(8,128)S(1)} %get-tuple-element.22), channel_id=1, source_target_pairs={{0,8},{1,9},{2,10},{3,11},{4,12},{5,13},{6,14},{7,15},{8,0},{9,1},... | collective-permute-start | bytes 233480 | tf_op jit(solution)/shard_map/ppermute | solution.py:31
  6.6 8.4 %collective-permute-start.2 = (f32[152,128]{1,0:T(8,128)S(1)}, f32[152,128]{1,0:T(8,128)S(1)}, u32[]{:S(2)}, u32[]{:S(2)}) collective-permute-start(f32[152,128]{1,0:T(8,128)S(1)} %get-tuple-element.23), channel_id=1, source_target_pairs={{0,4},{1,5},{2,6},{3,7},{4,0},{5,1},{6,2},{7,3},{8,16},{9,17},{10,... | collective-permute-start | bytes 233480 | tf_op jit(solution)/shard_map/ppermute | solution.py:31
  6.6 4.5 %collective-permute-start.3 = (f32[48,128]{1,0:T(8,128)S(1)}, f32[48,128]{1,0:T(8,128)S(1)}, u32[]{:S(2)}, u32[]{:S(2)}) collective-permute-start(f32[48,128]{1,0:T(8,128)S(1)} %get-tuple-element.32), channel_id=1, source_target_pairs={{0,12},{1,13},{2,14},{3,15},{4,8},{5,9},{6,10},{7,11},{8,4},{9,5},... | collective-permute-start | bytes 73736 | tf_op jit(solution)/shard_map/ppermute | solution.py:31
  8.7 2.3 %collective-permute-start.4 = (f32[48,128]{1,0:T(8,128)S(1)}, f32[48,128]{1,0:T(8,128)S(1)}, u32[]{:S(2)}, u32[]{:S(2)}) collective-permute-start(f32[48,128]{1,0:T(8,128)S(1)} %get-tuple-element.33), channel_id=1, source_target_pairs={{0,4},{1,5},{2,6},{3,7},{4,0},{5,1},{6,2},{7,3},{8,20},{9,21},{10,... | collective-permute-start | bytes 73736 | tf_op jit(solution)/shard_map/ppermute | solution.py:31
  11.2 4.4 %collective-permute-start.5 = (f32[48,128]{1,0:T(8,128)S(1)}, f32[48,128]{1,0:T(8,128)S(1)}, u32[]{:S(2)}, u32[]{:S(2)}) collective-permute-start(f32[48,128]{1,0:T(8,128)S(1)} %get-tuple-element.35), channel_id=1, source_target_pairs={{0,5},{1,4},{2,7},{3,6},{4,1},{5,0},{6,3},{7,2},{8,13},{9,12},{10,... | collective-permute-start | bytes 73736 | tf_op jit(solution)/shard_map/ppermute | solution.py:31
  13.6 2.0 %collective-permute-start.6 = (f32[48,128]{1,0:T(8,128)S(1)}, f32[48,128]{1,0:T(8,128)S(1)}, u32[]{:S(2)}, u32[]{:S(2)}) collective-permute-start(f32[48,128]{1,0:T(8,128)S(1)} %get-tuple-element.36), channel_id=1, source_target_pairs={{0,4},{1,6},{2,5},{3,7},{4,0},{5,2},{6,1},{7,3},{8,12},{9,14},{10,... | collective-permute-start | bytes 73736 | tf_op jit(solution)/shard_map/ppermute | solution.py:31
  15.9 1.4 %collective-permute-start.7 = (f32[8,128]{1,0:T(8,128)S(1)}, f32[8,128]{1,0:T(8,128)S(1)}, u32[]{:S(2)}, u32[]{:S(2)}) collective-permute-start(f32[8,128]{1,0:T(8,128)S(1)} %get-tuple-element.39), channel_id=1, source_target_pairs={{0,4},{1,5},{2,6},{3,7},{4,0},{5,1},{6,2},{7,3},{8,12},{9,13},{10,... | collective-permute-start | bytes 12296 | tf_op jit(solution)/shard_map/ppermute | solution.py:31
  17.3 3.5 %collective-permute-start.8 = (f32[8,128]{1,0:T(8,128)S(1)}, f32[8,128]{1,0:T(8,128)S(1)}, u32[]{:S(2)}, u32[]{:S(2)}) collective-permute-start(f32[8,128]{1,0:T(8,128)S(1)} %add.15), channel_id=1, source_target_pairs={{0,12},{1,13},{2,14},{3,15},{4,8},{5,9},{6,10},{7,11},{8,4},{9,5},... | collective-permute-start | bytes 12296 | tf_op jit(solution)/shard_map/ppermute | solution.py:31
  20.8 3.0 %collective-permute-start.9 = (f32[8,128]{1,0:T(8,128)S(1)}, f32[8,128]{1,0:T(8,128)S(1)}, u32[]{:S(2)}, u32[]{:S(2)}) collective-permute-start(f32[8,128]{1,0:T(8,128)S(1)} %add.16), channel_id=1, source_target_pairs={{0,20},{1,21},{2,22},{3,23},{4,16},{5,17},{6,18},{7,19},{8,28},{9,... | collective-permute-start | bytes 12296 | tf_op jit(solution)/shard_map/ppermute | solution.py:31
  23.8 3.8 %collective-permute-start.10 = (f32[8,128]{1,0:T(8,128)S(1)}, f32[8,128]{1,0:T(8,128)S(1)}, u32[]{:S(2)}, u32[]{:S(2)}) collective-permute-start(f32[8,128]{1,0:T(8,128)S(1)} %add.17), channel_id=1, source_target_pairs={{0,5},{1,4},{2,7},{3,6},{4,1},{5,0},{6,3},{7,2},{8,13},{9,12},{10,... | collective-permute-start | bytes 12296 | tf_op jit(solution)/shard_map/ppermute | solution.py:31
  27.7 4.0 %collective-permute-start.11 = (f32[8,128]{1,0:T(8,128)S(1)}, f32[8,128]{1,0:T(8,128)S(1)}, u32[]{:S(2)}, u32[]{:S(2)}) collective-permute-start(f32[8,128]{1,0:T(8,128)S(1)} %add.18), channel_id=1, source_target_pairs={{0,6},{1,7},{2,4},{3,5},{4,2},{5,3},{6,0},{7,1},{8,14},{9,15},{10,... | collective-permute-start | bytes 12296 | tf_op jit(solution)/shard_map/ppermute | solution.py:31

commit v7 on v6

--- a/solution.py
+++ b/solution.py
@@ -13,6 +13,8 @@
 AXES = ("gx", "gy", "gz")
 TILE = 8
 HALF = 64
+GROUP = 32
+DIRECT = 64
 
 pseudo_step = 0.45
 
@@ -60,6 +62,8 @@
 
 def sum_over_devices(value):
     sizes = [lax.axis_size(a) for a in AXES]
+    if value.shape[0] > 1:
+        return jnp.sum(lax.all_to_all(value, AXES, 0, 0), axis=0, keepdims=True)
     if any(n & (n - 1) for n in sizes):
         return lax.psum(value, AXES)
     rounds = []
@@ -436,8 +440,15 @@
         sums.append(jnp.sum(part, axis=0, keepdims=True))
     for i in range(HALO):
         out_ref[i * pitch : (i + 1) * pitch] = state[HALO + i]
-    sums.append(jnp.zeros((TILE - ITERS, 2 * HALF), jnp.float32))
-    sum_ref[...] = jnp.concatenate(sums, axis=0)
+    groups = lax.broadcasted_iota(jnp.int32, (1, 2 * HALF), 1) // GROUP
+    row = jnp.zeros((1, 2 * HALF), jnp.float32)
+    for it, part in enumerate(sums):
+        width = 2 * HALF
+        while width > GROUP:
+            width //= 2
+            part = part + pltpu.roll(part, width, 1)
+        row = jnp.where(groups == it, part, row)
+    sum_ref[...] = jnp.broadcast_to(row[None], sum_ref.shape)
 
 
 def merge_kernel(sizes, main_ref, ends_ref, edge_ref, out_ref):
@@ -572,11 +583,14 @@
         0.6,
     )
 
+    devices = 1
+    for axis in AXES:
+        devices = devices * lax.axis_size(axis)
     edge, sums = call(
         edge_kernel,
         sizes,
         (strip, za, zb, acc),
-        ((HALO * pitch, 2 * HALF), (TILE, 2 * HALF)),
+        ((HALO * pitch, 2 * HALF), (devices if devices <= DIRECT else 1, 1, 2 * HALF)),
         (),
         4,
         0.5,
@@ -584,10 +598,11 @@
 
     (phi_final,) = call(merge_kernel, sizes, (inner, tips, edge), (sizes,), (), 4, 1.5)
 
-    totals = jnp.sum(sum_over_devices(sums)[:ITERS], axis=1)
-    cells = planes * rows * lanes
-    for axis in AXES:
-        cells = cells * lax.axis_size(axis)
+    row = sum_over_devices(sums).reshape(1, 2 * HALF)
+    groups = lax.broadcasted_iota(jnp.int32, (ITERS, 2 * HALF), 1) // GROUP
+    wanted = lax.broadcasted_iota(jnp.int32, (ITERS, 2 * HALF), 0)
+    totals = jnp.sum(jnp.where(groups == wanted, row, 0.0), axis=1)
+    cells = planes * rows * lanes * devices
     residuals = jnp.sqrt(totals / jnp.float32(cells)) / pseudo_step
     return (phi_final, residuals)
 

time: 32.5 us -> 28.9 us (0.89)
  starting transfers between devices: 18.1 us -> 14 us
  Pallas kernels: 4.28 us -> 5.01 us
  waiting for transfers between devices: 7.62 us -> 7.28 us
    ppermute x12 -> x7, starting transfers between devices: 18.1 us -> 7.88 us  [pair_swap(): return lax.ppermute(value, AXES, pairs)]
    ppermute x12 -> x7, waiting for transfers between devices: 7.62 us -> 1.39 us  [pair_swap(): return lax.ppermute(value, AXES, pairs)]
    all_to_all x0 -> x1, starting transfers between devices: none -> 6.16 us  [sum_over_devices(): return jnp.sum(lax.all_to_all(value, AXES, 0, 0), axis=0, keepdims=True)]
    all_to_all x0 -> x1, waiting for transfers between devices: none -> 5.9 us  [sum_over_devices(): return jnp.sum(lax.all_to_all(value, AXES, 0, 0), axis=0, keepdims=True)]
    pallas_call x8, Pallas kernels: 4.28 us -> 5.01 us  [call(): pl.pallas_call(functools.partial(kernel, sizes), out_shape=tuple((jax.Sha...]
  transfers between devices with their start and end apart: 12 -> 8, of which waited for: 6 -> 3; matrix products, arithmetic and copies ran while one was open for 0% -> 0% of each run, Pallas kernels for 11% -> 12%
where the time goes in v7:
time: 28.9 us; the launch traced here: 28.7 us
  starting transfers between devices  14 us (48%)
  waiting for transfers between devices  7.28 us (25%)
  Pallas kernels  5.01 us (17%)
  local copies, waits for them, and re-layouts  1 us (3%)
  other arithmetic  0.71 us (2%)
  between operations  0.7 us (2%)
    ppermute x7, starting transfers between devices, pair_swap(): return lax.ppermute(value, AXES, pairs)  7.88 us
    all_to_all x1, starting transfers between devices, sum_over_devices(): return jnp.sum(lax.all_to_all(value, AXES, 0, 0), axis=0, keepdims=True)  6.16 us
    all_to_all x1, waiting for transfers between devices, sum_over_devices(): return jnp.sum(lax.all_to_all(value, AXES, 0, 0), axis=0, keepdims=True)  5.9 us
    pallas_call x8, Pallas kernels, call(): pl.pallas_call(functools.partial(kernel, sizes), out_shape=tuple((jax.Sha...  5.01 us
    ppermute x7, waiting for transfers between devices, pair_swap(): return lax.ppermute(value, AXES, pairs)  1.39 us
    unnamed x4, local copies, waits for them, and re-layouts  0.99 us
  transfers between devices with their start and end apart: 8, of which 3 were waited for; matrix products, arithmetic and copies ran while one was open for 0% of the time, Pallas kernels for 12%

profile of v7, /device:TPU:0, one launch (start us, length us, event | category | flops | bytes accessed | tf_op | source)
XLA Modules:
  0.0 28.7 jit_solution(8898338314811597202)
XLA Ops:
  0.6 0.0 copy-start
  0.6 1.0 %copy-done = f32[16,48,128]{2,1,0:T(8,128)S(1)} copy-done((f32[16,48,128]{2,1,0:T(8,128)S(1)}, f32[16,48,128]{2,1,0:T(8,128)}, u32[]{:S(2)}) %copy-start) | copy-done | bytes 393240
  1.6 0.0 copy-start.1
  1.6 0.4 %shard_map.30.refs_2_.refs_0_ = f32[256,128]{1,0:T(8,128)S(1)} custom-call(f32[16,48,128]{2,1,0:T(8,128)S(1)} %copy-done), custom_call_target="tpu_custom_call" | custom-call | flops 1750000 | bytes 1000000 | tf_op jit(solution)/shard_map/pallas_call | solution.py:489
  2.0 0.5 %collective-permute-start = (f32[256,128]{1,0:T(8,128)S(1)}, f32[256,128]{1,0:T(8,128)S(1)}, u32[]{:S(2)}, u32[]{:S(2)}) collective-permute-start(f32[256,128]{1,0:T(8,128)S(1)} %shard_map.30.refs_2_.refs_0_), channel_id=1, source_target_pairs={{0,4},{1,5},{2,6},{3,7},{4,0},{5,1},{6,2},{7,3},{8,12},{9,13},{10,... | collective-permute-start | bytes 393224 | tf_op jit(solution)/shard_map/ppermute | solution.py:33
  2.6 1.0 %collective-permute-done.refs_3_.refs_1_ = f32[256,128]{1,0:T(8,128)S(1)} collective-permute-done((f32[256,128]{1,0:T(8,128)S(1)}, f32[256,128]{1,0:T(8,128)S(1)}, u32[]{:S(2)}, u32[]{:S(2)}) %collective-permute-start) | collective-permute-done | bytes 131104 | tf_op jit(solution)/shard_map/ppermute | solution.py:33
  3.6 0.0 copy-done.1
  3.6 0.1 shard_map.32
  3.7 2.7 %collective-permute-start.3 = (f32[48,128]{1,0:T(8,128)S(1)}, f32[48,128]{1,0:T(8,128)S(1)}, u32[]{:S(2)}, u32[]{:S(2)}) collective-permute-start(f32[48,128]{1,0:T(8,128)S(1)} %get-tuple-element.32), channel_id=1, source_target_pairs={{0,12},{1,13},{2,14},{3,15},{4,8},{5,9},{6,10},{7,11},{8,4},{9,5},... | collective-permute-start | bytes 73736 | tf_op jit(solution)/shard_map/ppermute | solution.py:33
  6.3 0.4 %collective-permute-start.4 = (f32[48,128]{1,0:T(8,128)S(1)}, f32[48,128]{1,0:T(8,128)S(1)}, u32[]{:S(2)}, u32[]{:S(2)}) collective-permute-start(f32[48,128]{1,0:T(8,128)S(1)} %get-tuple-element.33), channel_id=1, source_target_pairs={{0,4},{1,5},{2,6},{3,7},{4,0},{5,1},{6,2},{7,3},{8,20},{9,21},{10,... | collective-permute-start | bytes 73736 | tf_op jit(solution)/shard_map/ppermute | solution.py:33
  6.7 2.6 %collective-permute-start.1 = (f32[152,128]{1,0:T(8,128)S(1)}, f32[152,128]{1,0:T(8,128)S(1)}, u32[]{:S(2)}, u32[]{:S(2)}) collective-permute-start(f32[152,128]{1,0:T(8,128)S(1)} %get-tuple-element.22), channel_id=1, source_target_pairs={{0,8},{1,9},{2,10},{3,11},{4,12},{5,13},{6,14},{7,15},{8,0},{9,1},... | collective-permute-start | bytes 233480 | tf_op jit(solution)/shard_map/ppermute | solution.py:33
  9.3 0.0 collective-permute-start.2
  9.3 0.1 shard_map.34
  9.4 0.0 collective-permute-done.3.refs_2_
  9.4 0.0 collective-permute-done.4.refs_3_
  9.4 0.1 shard_map.35
  9.5 1.7 %collective-permute-start.5 = (f32[48,128]{1,0:T(8,128)S(1)}, f32[48,128]{1,0:T(8,128)S(1)}, u32[]{:S(2)}, u32[]{:S(2)}) collective-permute-start(f32[48,128]{1,0:T(8,128)S(1)} %get-tuple-element.35), channel_id=1, source_target_pairs={{0,5},{1,4},{2,7},{3,6},{4,1},{5,0},{6,3},{7,2},{8,13},{9,12},{10,... | collective-permute-start | bytes 73736 | tf_op jit(solution)/shard_map/ppermute | solution.py:33
  11.2 0.0 collective-permute-start.6
  11.3 1.4 %shard_map.31 = (f32[16,56,128]{2,1,0:T(8,128)S(1)}, f32[16,56,128]{2,1,0:T(8,128)S(1)}, f32[16,48,128]{2,1,0:T(8,128)S(1)}, f32[16,56,128]{2,1,0:T(8,128)S(1)},...) custom-call(f32[16,48,128]{2,1,0:T(8,128)S(1)} %copy-done.1, f32[16,8,128]{2,1,0:T(8,128)S(1)} %slice_bitcast_fusion.mix_ref.refs_1_), custom_call_target="tpu_custom_call" | custom-call | flops 5250000 | bytes 1000000 | tf_op jit(solution)/shard_map/pallas_call | solution.py:489
  12.6 0.4 %collective-permute-done.1.xa_ref = f32[152,128]{1,0:T(8,128)S(1)} collective-permute-done((f32[152,128]{1,0:T(8,128)S(1)}, f32[152,128]{1,0:T(8,128)S(1)}, u32[]{:S(2)}, u32[]{:S(2)}) %collective-permute-start.1) | collective-permute-done | bytes 77856 | tf_op jit(solution)/shard_map/ppermute | solution.py:33
  13.0 0.0 collective-permute-done.2.xb_ref
  13.0 0.6 %shard_map.33 = (f32[6,48,128]{2,1,0:T(8,128)S(1)}, f32[3,8,128]{2,1,0:T(8,128)S(1)}) custom-call(f32[16,48,128]{2,1,0:T(8,128)S(1)} %copy-done.1, f32[16,8,128]{2,1,0:T(8,128)S(1)} %slice_bitcast_fusion.mix_ref.refs_1_, f32[152,128]{1,0:T(8,128)S(1)} %collective-permute-done.1.xa_ref, f32[152,128]{1,0:T(8,128)S(1)} %collective-permute-done.2.xb_ref, ...), custom_call_target="tpu_custom_call" | custom-call | flops 2100000 | bytes 1000000 | tf_op jit(solution)/shard_map/pallas_call | solution.py:489
  13.6 0.0 collective-permute-done.5.za_ref
  13.6 0.0 collective-permute-done.6.zb_ref
  13.6 1.1 %shard_map.36 = (f32[72,128]{1,0:T(8,128)S(1)}, f32[32,1,128]{2,1,0:T(1,128)}) custom-call(f32[216,128]{1,0:T(8,128)S(1)} %get-tuple-element.34.strip_ref, f32[48,128]{1,0:T(8,128)S(1)} %collective-permute-done.5.za_ref, f32[48,128]{1,0:T(8,128)S(1)} %collective-permute-done.6.zb_ref, f32[3,8,128]{2,1,0:T(8,128)S(1)} %get-tuple-element.37.acc_ref), custom_call_target="tpu_custom_call" | custom-call | flops 1750000 | bytes 1000000 | tf_op jit(solution)/shard_map/pallas_call | solution.py:489
  14.7 6.2 %all-to-all-start = ((f32[32,1,128]{2,1,0:T(1,128)}), f32[32,1,128]{2,1,0:T(1,128)S(1)}, u32[]{:S(2)}, u32[]{:S(2)}) async-start(f32[32,1,128]{2,1,0:T(1,128)} %get-tuple-element.39), calls=%async_computation | async-start | bytes 32768 | tf_op jit(solution)/shard_map/all_to_all | solution.py:66
  20.9 1.3 %shard_map.37 = f32[16,48,128]{2,1,0:T(8,128)} custom-call(f32[16,48,128]{2,1,0:T(8,128)S(1)} %get-tuple-element.21.main_ref, f32[6,48,128]{2,1,0:T(8,128)S(1)} %get-tuple-element.29.ends_ref, f32[72,128]{1,0:T(8,128)S(1)} %get-tuple-element.38.edge_ref), custom_call_target="tpu_custom_call" | custom-call | flops 5250000 | bytes 1000000 | tf_op jit(solution)/shard_map/pallas_call | solution.py:489
  22.2 5.9 %all-to-all-done = f32[32,1,128]{2,1,0:T(1,128)S(1)} async-done(((f32[32,1,128]{2,1,0:T(1,128)}), f32[32,1,128]{2,1,0:T(1,128)S(1)}, u32[]{:S(2)}, u32[]{:S(2)}) %all-to-all-start) | async-done | bytes 16416 | tf_op jit(solution)/shard_map/all_to_all | solution.py:66
  28.1 0.1 reduce_sum.18
  28.1 0.1 select_reduce_fusion
  28.2 0.5 %sqrt_multiply_fusion = f32[3]{0:T(128)} fusion(f32[3]{0:T(128)S(1)} %select_reduce_fusion), kind=kLoop, calls=%fused_computation.7 | loop fusion | flops 6 | bytes 24 | tf_op jit(solution)/shard_map/div | solution.py:606
  (3 shorter events, 0.0 us)
Async XLA Ops:
  0.6 1.0 %copy-start = (f32[16,48,128]{2,1,0:T(8,128)S(1)}, f32[16,48,128]{2,1,0:T(8,128)}, u32[]{:S(2)}) copy-start(f32[16,48,128]{2,1,0:T(8,128)} %b_ref.5) | copy-start | bytes 1179652
  1.6 1.9 %copy-start.1 = (f32[16,48,128]{2,1,0:T(8,128)S(1)}, f32[16,48,128]{2,1,0:T(8,128)}, u32[]{:S(2)}) copy-start(f32[16,48,128]{2,1,0:T(8,128)} %b_ref.5) | copy-start | bytes 1179652
  2.0 1.5 %collective-permute-start = (f32[256,128]{1,0:T(8,128)S(1)}, f32[256,128]{1,0:T(8,128)S(1)}, u32[]{:S(2)}, u32[]{:S(2)}) collective-permute-start(f32[256,128]{1,0:T(8,128)S(1)} %shard_map.30.refs_2_.refs_0_), channel_id=1, source_target_pairs={{0,4},{1,5},{2,6},{3,7},{4,0},{5,1},{6,2},{7,3},{8,12},{9,13},{10,... | collective-permute-start | bytes 393224 | tf_op jit(solution)/shard_map/ppermute | solution.py:33
  3.7 5.7 %collective-permute-start.3 = (f32[48,128]{1,0:T(8,128)S(1)}, f32[48,128]{1,0:T(8,128)S(1)}, u32[]{:S(2)}, u32[]{:S(2)}) collective-permute-start(f32[48,128]{1,0:T(8,128)S(1)} %get-tuple-element.32), channel_id=1, source_target_pairs={{0,12},{1,13},{2,14},{3,15},{4,8},{5,9},{6,10},{7,11},{8,4},{9,5},... | collective-permute-start | bytes 73736 | tf_op jit(solution)/shard_map/ppermute | solution.py:33
  6.3 3.1 %collective-permute-start.4 = (f32[48,128]{1,0:T(8,128)S(1)}, f32[48,128]{1,0:T(8,128)S(1)}, u32[]{:S(2)}, u32[]{:S(2)}) collective-permute-start(f32[48,128]{1,0:T(8,128)S(1)} %get-tuple-element.33), channel_id=1, source_target_pairs={{0,4},{1,5},{2,6},{3,7},{4,0},{5,1},{6,2},{7,3},{8,20},{9,21},{10,... | collective-permute-start | bytes 73736 | tf_op jit(solution)/shard_map/ppermute | solution.py:33
  6.7 6.3 %collective-permute-start.1 = (f32[152,128]{1,0:T(8,128)S(1)}, f32[152,128]{1,0:T(8,128)S(1)}, u32[]{:S(2)}, u32[]{:S(2)}) collective-permute-start(f32[152,128]{1,0:T(8,128)S(1)} %get-tuple-element.22), channel_id=1, source_target_pairs={{0,8},{1,9},{2,10},{3,11},{4,12},{5,13},{6,14},{7,15},{8,0},{9,1},... | collective-permute-start | bytes 233480 | tf_op jit(solution)/shard_map/ppermute | solution.py:33
  9.3 3.7 %collective-permute-start.2 = (f32[152,128]{1,0:T(8,128)S(1)}, f32[152,128]{1,0:T(8,128)S(1)}, u32[]{:S(2)}, u32[]{:S(2)}) collective-permute-start(f32[152,128]{1,0:T(8,128)S(1)} %get-tuple-element.23), channel_id=1, source_target_pairs={{0,4},{1,5},{2,6},{3,7},{4,0},{5,1},{6,2},{7,3},{8,16},{9,17},{10,... | collective-permute-start | bytes 233480 | tf_op jit(solution)/shard_map/ppermute | solution.py:33
  9.5 4.1 %collective-permute-start.5 = (f32[48,128]{1,0:T(8,128)S(1)}, f32[48,128]{1,0:T(8,128)S(1)}, u32[]{:S(2)}, u32[]{:S(2)}) collective-permute-start(f32[48,128]{1,0:T(8,128)S(1)} %get-tuple-element.35), channel_id=1, source_target_pairs={{0,5},{1,4},{2,7},{3,6},{4,1},{5,0},{6,3},{7,2},{8,13},{9,12},{10,... | collective-permute-start | bytes 73736 | tf_op jit(solution)/shard_map/ppermute | solution.py:33
  11.2 2.4 %collective-permute-start.6 = (f32[48,128]{1,0:T(8,128)S(1)}, f32[48,128]{1,0:T(8,128)S(1)}, u32[]{:S(2)}, u32[]{:S(2)}) collective-permute-start(f32[48,128]{1,0:T(8,128)S(1)} %get-tuple-element.36), channel_id=1, source_target_pairs={{0,4},{1,6},{2,5},{3,7},{4,0},{5,2},{6,1},{7,3},{8,12},{9,14},{10,... | collective-permute-start | bytes 73736 | tf_op jit(solution)/shard_map/ppermute | solution.py:33
  14.7 13.4 %all-to-all-start = ((f32[32,1,128]{2,1,0:T(1,128)}), f32[32,1,128]{2,1,0:T(1,128)S(1)}, u32[]{:S(2)}, u32[]{:S(2)}) async-start(f32[32,1,128]{2,1,0:T(1,128)} %get-tuple-element.39), calls=%async_computation | async-start | bytes 32768 | tf_op jit(solution)/shard_map/all_to_all | solution.py:66
